TPU v7x, 512 devices: a whole 4x4x16 slice. The times are simulated.
512 devices in a mesh: rep: 32 (over z, core), mdl: 16 (over y, x).
Axes of the slice: x: 4, y: 4, z: 16, core: 2. Of those that a mesh axis runs over, the one named last changes fastest.
Arguments:
- deltas: bfloat16 [32, 2560, 2560], P('rep', 'mdl'), may hold values from -72 to 72
- errors: bfloat16 [32, 2560, 2560], P('rep', 'mdl'), may hold values from -3 to 3
- starts: float32 [2560, 64], replicated, may hold values from -6 to 6
- momentum: float32 [2560, 2560], P('mdl', 'rep'), may hold values from -2 to 2
Outputs:
- new_errors: bfloat16 [32, 2560, 2560], P('rep', 'mdl')
- new_momentum: float32 [2560, 2560], P('mdl', 'rep')
- outer_step: float32 [2560, 2560], P('mdl', 'rep')
All inputs are finite; a program needn't handle non-finite values.
Results may differ from a plain program's by a relative error of at most 0.001.
Values sent between devices are 32-bit elements; how exact they have to be, the bound alone decides.
No kernel may reach another device: no remote copies, remote signals or barrier semaphores. Data moves between devices by JAX's collectives and lax.ppermute only.
A program may use at most 64 MiB of HBM per device.

v0:
```python
import jax
import jax.numpy as jnp
from jax import lax
from jax.sharding import Mesh
from jax.sharding import PartitionSpec as P

REP = ("rep_0", "rep_1")
MDL = ("mdl_0", "mdl_1")


highest = lax.Precision.HIGHEST


def from_everyone(shard, axis):
    count = lax.axis_size(axis)
    return lax.all_to_all(
        jnp.broadcast_to(shard[None], (count, *shard.shape)), axis, 0, 0, tiled=True
    )


def over_copies(shard, axis):
    return from_everyone(shard, axis).sum(axis=0)


def in_blocks(shard, dim, count):
    before, after = (shard.shape[:dim], shard.shape[dim + 1 :])
    return jnp.moveaxis(shard.reshape(*before, count, -1, *after), dim, 0)


def summed_on_arrival(shard, axis, dim):
    tiles = in_blocks(shard, dim, lax.axis_size(axis))
    arrived = lax.all_to_all(tiles, axis, split_axis=0, concat_axis=0, tiled=True)
    return arrived.sum(axis=0)


def sum_by_axis(shard, axes, dim):
    far, near = axes
    own = summed_on_arrival(in_blocks(shard, dim, lax.axis_size(far)), near, dim + 1)
    return jnp.sum(lax.all_to_all(own, far, 0, 0, tiled=True), axis=0)


def padded_to(lines, count):
    spare = -lines.shape[0] % count
    if not spare:
        return lines
    return jnp.concatenate([lines, jnp.zeros((spare, *lines.shape[1:]), lines.dtype)])


def in_order(tiles, dim):
    dims = list(tiles.shape[1:])
    dims[dim] *= tiles.shape[0]
    return jnp.moveaxis(tiles, 0, dim).reshape(dims)


def whole_of(shard, axes, dim):
    far, near = axes
    leading = from_everyone(shard, far)
    tiles = jnp.swapaxes(from_everyone(leading, near), 0, 1)
    return in_order(tiles.reshape(-1, *shard.shape), dim)


def total_of(shard, axes):
    lines = shard.reshape(-1)
    own = sum_by_axis(padded_to(lines, lax.axis_size(axes[0]) * lax.axis_size(axes[1])), axes, 0)
    whole = whole_of(own, axes, 0)
    return whole[: len(lines)].reshape(shard.shape)


def body(deltas, errors, starts, momentum):
    replicas = lax.axis_size(REP)
    merged = deltas[0].astype(jnp.float32) + errors[0].astype(jnp.float32)
    left_part = jnp.einsum("ac,ck->ka", merged, starts, precision=highest)
    left = over_copies(left_part, REP) / replicas
    gram = jnp.einsum("ka,la->kl", left, left, precision=highest)
    gram = over_copies(gram, MDL)
    lower = jnp.linalg.cholesky(gram)
    basis = jax.scipy.linalg.solve_triangular(lower, left, lower=True)
    right_part = jnp.einsum("ac,ka->kc", merged, basis, precision=highest)
    right = total_of(right_part, (("rep_0", "rep_1"), ("mdl_0", "mdl_1"))) / replicas
    approx = jnp.einsum("ka,kc->ac", basis, right, precision=highest)
    new_errors = (merged - approx).astype(jnp.bfloat16)[None]
    width = momentum.shape[1]
    owned = lax.dynamic_slice_in_dim(approx, lax.axis_index(REP) * width, width, 1)
    new_momentum = 0.9 * momentum + owned
    outer_step = 0.7 * (owned + 0.9 * new_momentum)
    return (new_errors, new_momentum, outer_step)


def solution(mesh):
    torus = Mesh(mesh.devices.reshape(16, 2, 4, 4), ("rep_0", "rep_1", "mdl_0", "mdl_1"))
    in_specs = (P(REP, MDL, None), P(REP, MDL, None), P(), P(MDL, REP))
    out_specs = (P(REP, MDL, None), P(MDL, REP), P(MDL, REP))
    return jax.shard_map(body, mesh=torus, in_specs=in_specs, out_specs=out_specs, check_vma=False)
```

profile of v0, /device:TPU:1, one launch (start us, length us, event | category | flops | bytes accessed | tf_op | source)
XLA Modules:
  0.0 229.3 jit_solution(9882970275612640456)
XLA Ops:
  0.6 0.0 copy-start
  0.6 1.1 copy-done
  1.7 3.2 %fusion.5 = f32[64,160]{1,0:T(8,128)S(1)} fusion(f32[2560,64]{0,1:T(8,128)S(1)} %copy-done, bf16[1,160,2560]{2,1,0:T(8,128)(2,1)} %param.5, bf16[1,160,2560]{2,1,0:T(8,128)(2,1)} %param.4), kind=kOutput, calls=%fused_computation.7 | convolution fusion | flops 315801600 | bytes 2334720 | tf_op jit(solution)/shard_map/ac,ck->ka/dot_general | solution.py:72
  4.9 0.2 broadcast_in_dim.14
  5.2 117.2 %all_to_all.35 = f32[32,64,160]{2,1,0:T(8,128)S(1)} all-to-all(f32[32,64,160]{2,1,0:T(8,128)S(1)} %broadcast_in_dim.14), channel_id=1, replica_groups=mesh['rep_0'=16,'rep_1'=2,'mdl_0'=4,'mdl_1'=4] {'rep_0','rep_1'}, dimensions={0} | all-to-all | bytes 2621440 | tf_op jit(solution)/shard_map/all_to_all | solution.py:16
  122.3 0.1 reduce_sum.36
  122.5 0.2 fusion.11
  122.7 0.0 copy-start.1
  122.8 0.0 copy-start.2
  122.8 0.3 reshape.33
  123.1 14.7 %all_to_all.36 = f32[16,1,4096]{2,1,0:T(1,128)S(1)} all-to-all(f32[16,1,4096]{2,1,0:T(1,128)S(1)} %reshape.33), channel_id=1, replica_groups=mesh['rep_0'=16,'rep_1'=2,'mdl_0'=4,'mdl_1'=4] {'mdl_0','mdl_1'}, dimensions={0} | all-to-all | bytes 524288 | tf_op jit(solution)/shard_map/all_to_all | solution.py:16
  137.8 0.5 broadcast.71
  138.3 1.3 reduce.7
  139.6 0.2 reshape.34
  139.8 0.1 copy.12
  139.9 5.8 %cholesky.16 = f32[64,64]{1,0:T(8,128)S(1)} custom-call(f32[64,64]{1,0:T(8,128)S(1)} %fusion.15), custom_call_target="Cholesky" | custom-call | tf_op jit(solution)/shard_map/jit(cholesky)/cholesky | solution.py:76
  145.8 0.6 compare_reduce_fusion
  146.4 0.7 fusion.13
  147.1 4.9 %custom-call.7 = f32[1,64,64]{1,2,0:T(8,128)S(1)} custom-call(f32[1,64,64]{2,1,0:T(8,128)S(1)} %fusion.13), custom_call_target="InvertDiagBlocksLowerTriangular" | custom-call | tf_op jit(solution)/shard_map/jit(_solve_triangular)/triangular_solve | solution.py:77
  152.0 0.3 fusion.9
  152.3 0.0 copy-done.1
  152.3 0.0 copy-done.2
  152.3 2.0 fusion
  154.3 1.3 reshape_reshape_reshape.4
  155.6 0.3 copy.18
  155.9 14.9 %all_to_all.37 = f32[16,32,320]{2,1,0:T(8,128)S(1)} all-to-all(f32[16,32,320]{2,1,0:T(8,128)S(1)} %bitcast.37), channel_id=1, replica_groups=mesh['rep_0'=16,'rep_1'=2,'mdl_0'=4,'mdl_1'=4] {'mdl_0','mdl_1'}, dimensions={0} | all-to-all | bytes 1310720 | tf_op jit(solution)/shard_map/all_to_all | solution.py:32
  170.9 18.2 %all_to_all.38 = f32[32,1,320]{2,1,0:T(1,128)S(1)} all-to-all(f32[32,1,320]{2,1,0:T(1,128)S(1)} %all_to_all.25), channel_id=1, replica_groups=mesh['rep_0'=16,'rep_1'=2,'mdl_0'=4,'mdl_1'=4] {'rep_0','rep_1'}, dimensions={0} | all-to-all | bytes 81920 | tf_op jit(solution)/shard_map/all_to_all | solution.py:39
  189.1 0.1 reduce_sum.39
  189.2 16.7 %all_to_all.39 = f32[32,1,320]{2,1,0:T(1,128)S(1)} all-to-all(f32[32,1,320]{2,1,0:T(1,128)S(1)} %broadcast_in_dim.16), channel_id=1, replica_groups=mesh['rep_0'=16,'rep_1'=2,'mdl_0'=4,'mdl_1'=4] {'rep_0','rep_1'}, dimensions={0} | all-to-all | bytes 81920 | tf_op jit(solution)/shard_map/all_to_all | solution.py:16
  205.8 1.0 broadcast_in_dim.18
  206.8 3.6 %all-to-all-start.5 = ((f32[16,32,320]{2,1,0:T(8,128)}), f32[16,32,320]{2,1,0:T(8,128)S(1)}, u32[]{:S(2)}, u32[]{:S(2)}) async-start(f32[16,32,320]{2,1,0:T(8,128)} %broadcast_in_dim.18), calls=%async_computation.5 | async-start | bytes 1572864 | tf_op jit(solution)/shard_map/all_to_all | solution.py:16
  210.4 12.7 %all-to-all-done.5 = f32[16,32,320]{2,1,0:T(8,128)S(1)} async-done(((f32[16,32,320]{2,1,0:T(8,128)}), f32[16,32,320]{2,1,0:T(8,128)S(1)}, u32[]{:S(2)}, u32[]{:S(2)}) %all-to-all-start.5) | async-done | bytes 655392 | tf_op jit(solution)/shard_map/all_to_all | solution.py:16
  223.1 0.1 multiply_bitcast_fusion
  223.2 0.5 copy.14
  223.7 1.0 div.31
  224.7 2.6 %fusion.20 = f32[160,2560]{1,0:T(8,128)S(1)} fusion(f32[64,160]{1,0:T(8,128)S(1)} %fusion.9, f32[64,2560]{1,0:T(8,128)} %div.31), kind=kOutput, calls=%fused_computation.31 | convolution fusion | flops 314572800 | bytes 2334720 | tf_op jit(solution)/shard_map/ka,kc->ac/dot_general | solution.py:80
  227.3 0.0 copy-start.3
  227.3 1.2 fusion.8
  228.5 0.0 copy-done.3
  228.5 0.8 add_multiply_fusion
  (8 shorter events, 0.3 us)
Async XLA Ops:
  0.6 1.1 copy-start
  122.7 29.5 %copy-start.1 = (bf16[1,160,2560]{2,1,0:T(8,128)(2,1)S(1)}, bf16[1,160,2560]{2,1,0:T(8,128)(2,1)}, u32[]{:S(2)}) copy-start(bf16[1,160,2560]{2,1,0:T(8,128)(2,1)} %param.5) | copy-start | bytes 2457604
  122.8 29.5 %copy-start.2 = (bf16[1,160,2560]{2,1,0:T(8,128)(2,1)S(1)}, bf16[1,160,2560]{2,1,0:T(8,128)(2,1)}, u32[]{:S(2)}) copy-start(bf16[1,160,2560]{2,1,0:T(8,128)(2,1)} %param.4) | copy-start | bytes 2457604
  206.8 16.3 %all-to-all-start.5 = ((f32[16,32,320]{2,1,0:T(8,128)}), f32[16,32,320]{2,1,0:T(8,128)S(1)}, u32[]{:S(2)}, u32[]{:S(2)}) async-start(f32[16,32,320]{2,1,0:T(8,128)} %broadcast_in_dim.18), calls=%async_computation.5 | async-start | bytes 1572864 | tf_op jit(solution)/shard_map/all_to_all | solution.py:16
  227.3 1.2 copy-start.3
where the time goes:
time: 230 us; the launch traced here: 229 us
  blocking collectives  182 us (79%)
  other arithmetic  15.7 us (7%)
  waiting for transfers between devices  12.7 us (6%)
  matrix products  8.22 us (4%)
  local copies, waits for them, and re-layouts  6.6 us (3%)
  starting transfers between devices  3.61 us (2%)
    all_to_all x3, blocking collectives, from_everyone(): lax.all_to_all(jnp.broadcast_to(shard[None], (count, *shard.shape)), axis...  149 us
    all_to_all x1, blocking collectives, sum_by_axis(): return jnp.sum(lax.all_to_all(own, far, 0, 0, tiled=True), axis=0)  18.2 us
    all_to_all x1, blocking collectives, summed_on_arrival(): lax.all_to_all(tiles, axis, split_axis=0, concat_axis=0, tiled=True)  14.9 us
    all_to_all x1, waiting for transfers between devices, from_everyone(): lax.all_to_all(jnp.broadcast_to(shard[None], (count, *shard.shape)), axis...  12.7 us
    another operation x3, other arithmetic, body(): lower = jnp.linalg.cholesky(gram)  6.52 us
    another operation x2, other arithmetic, body(): basis = jax.scipy.linalg.solve_triangular(lower, left, lower=True)  5.55 us
  transfers between devices with their start and end apart: 1, of which 1 were waited for; matrix products, arithmetic and copies ran while one was open for 0% of the time, Pallas kernels for 0%

commit v1 on v0

v1 whole, which is shorter than its diff:
```python
import jax
import jax.numpy as jnp
from jax import lax
from jax.sharding import Mesh
from jax.sharding import PartitionSpec as P

REP = ("far", "near", "core")
PAIR = ("near", "core")
WIDE = ("near", "core", "mdl")


highest = lax.Precision.HIGHEST


def to_each(shard, axes):
    count = lax.axis_size(axes)
    return lax.all_to_all(
        jnp.broadcast_to(shard[None], (count, *shard.shape)), axes, 0, 0, tiled=True
    )


def spread_sum(shard, near, far):
    count = lax.axis_size(near)
    tiles = shard.reshape(count, shard.shape[0] // count, shard.shape[1])
    own = lax.all_to_all(tiles, near, 0, 0, tiled=True).sum(axis=0)
    own = to_each(own, far).sum(axis=0)
    return to_each(own, near).reshape(shard.shape)


def body(deltas, errors, starts, momentum):
    replicas = lax.axis_size(REP)
    merged = deltas[0].astype(jnp.float32) + errors[0].astype(jnp.float32)
    left_part = jnp.einsum("ac,ck->ka", merged, starts, precision=highest)
    left = spread_sum(left_part, PAIR, "far") / replicas
    right_part = jnp.einsum("ac,ka->kc", merged, left, precision=highest)
    right = spread_sum(right_part, WIDE, "far") / replicas
    gram = jnp.einsum("ck,lc->kl", starts, right, precision=highest)
    lower = jnp.linalg.cholesky(gram)
    inverse = jax.scipy.linalg.solve_triangular(
        lower, jnp.eye(lower.shape[0], dtype=jnp.float32), lower=True
    )
    basis = jnp.einsum("kl,la->ka", inverse, left, precision=highest)
    turned = jnp.einsum("kl,ka->la", inverse, basis, precision=highest)
    approx = jnp.einsum("ka,kc->ac", turned, right, precision=highest)
    new_errors = (merged - approx).astype(jnp.bfloat16)[None]
    width = momentum.shape[1]
    owned = lax.dynamic_slice_in_dim(approx, lax.axis_index(REP) * width, width, 1)
    new_momentum = 0.9 * momentum + owned
    outer_step = 0.7 * (owned + 0.9 * new_momentum)
    return (new_errors, new_momentum, outer_step)


def solution(mesh):
    torus = Mesh(mesh.devices.reshape(8, 2, 2, 16), ("far", "near", "core", "mdl"))
    in_specs = (P(REP, "mdl", None), P(REP, "mdl", None), P(), P("mdl", REP))
    out_specs = (P(REP, "mdl", None), P("mdl", REP), P("mdl", REP))
    return jax.shard_map(body, mesh=torus, in_specs=in_specs, out_specs=out_specs, check_vma=False)
```

time: 230 us -> 128 us (0.56)
  blocking collectives: 182 us -> 79.8 us
  starting transfers between devices: 3.61 us -> 7.73 us
  local copies, waits for them, and re-layouts: 6.6 us -> 3.06 us
    all_to_all x5, blocking collectives: 182 us -> 79.8 us  [the longest x3 46.5 us: to_each(): lax.all_to_all(jnp.broadcast_to(shard[None], (count, *shard.shape)), axes...]
    all_to_all x1, starting transfers between devices: 3.61 us -> 7.73 us  [to_each(): lax.all_to_all(jnp.broadcast_to(shard[None], (count, *shard.shape)), axes...]
    dot_general x3 -> x5, matrix products: 4.76 us -> 3.75 us  [the longest x1 1.49 us: body(): approx = jnp.einsum('ka,kc->ac', turned, right, precision=highest)]
where the time goes in v1:
time: 128 us; the launch traced here: 127 us
  blocking collectives  79.8 us (62%)
  other arithmetic  16.2 us (13%)
  waiting for transfers between devices  12.6 us (10%)
  starting transfers between devices  7.73 us (6%)
  matrix products  7.17 us (6%)
  local copies, waits for them, and re-layouts  3.06 us (2%)
    all_to_all x3, blocking collectives, to_each(): lax.all_to_all(jnp.broadcast_to(shard[None], (count, *shard.shape)), axes...  46.5 us
    all_to_all x2, blocking collectives, spread_sum(): own = lax.all_to_all(tiles, near, 0, 0, tiled=True).sum(axis=0)  33.3 us
    all_to_all x1, waiting for transfers between devices, to_each(): lax.all_to_all(jnp.broadcast_to(shard[None], (count, *shard.shape)), axes...  12.6 us
    all_to_all x1, starting transfers between devices, to_each(): lax.all_to_all(jnp.broadcast_to(shard[None], (count, *shard.shape)), axes...  7.73 us
    another operation x3, other arithmetic, body(): lower = jnp.linalg.cholesky(gram)  6.52 us
    another operation x2, other arithmetic, body(): jax.scipy.linalg.solve_triangular(lower, jnp.eye(lower.shape[0], dtype=jn...  5.55 us
    dot_general x1, matrix products, body(): left_part = jnp.einsum('ac,ck->ka', merged, starts, precision=highest)  3.19 us
  transfers between devices with their start and end apart: 1, of which 1 were waited for; matrix products, arithmetic and copies ran while one was open for 0% of the time, Pallas kernels for 0%

profile of v1, /device:TPU:1, one launch (start us, length us, event | category | flops | bytes accessed | tf_op | source)
XLA Modules:
  0.0 127.3 jit_solution(422320694066174595)
XLA Ops:
  0.6 0.0 copy-start
  0.6 0.0 copy-start.2
  0.7 0.0 copy-start.1
  0.7 1.1 copy-done
  1.7 3.2 %fusion.1 = f32[160,64]{0,1:T(8,128)S(1)} fusion(f32[2560,64]{0,1:T(8,128)S(1)} %copy-done, bf16[1,160,2560]{2,1,0:T(8,128)(2,1)} %param.5, bf16[1,160,2560]{2,1,0:T(8,128)(2,1)} %param.4), kind=kOutput, calls=%fused_computation.3 | convolution fusion | flops 315801600 | bytes 2334720 | tf_op jit(solution)/shard_map/ac,ck->ka/dot_general | solution.py:33
  4.9 12.5 %all_to_all.30 = f32[4,16,160]{2,1,0:T(8,128)S(1)} all-to-all(f32[4,16,160]{2,1,0:T(8,128)S(1)} %bitcast.42), channel_id=1, replica_groups=mesh['far'=8,'near'=2,'core'=2,'mdl'=16] {'near','core'}, dimensions={0} | all-to-all | bytes 81920 | tf_op jit(solution)/shard_map/all_to_all | solution.py:25
  17.4 22.8 %all_to_all.31 = f32[8,16,160]{2,1,0:T(8,128)S(1)} all-to-all(f32[8,16,160]{2,1,0:T(8,128)S(1)} %broadcast_in_dim.11), channel_id=1, replica_groups=mesh['far'=8,'near'=2,'core'=2,'mdl'=16] {'far'}, dimensions={0} | all-to-all | bytes 163840 | tf_op jit(solution)/shard_map/all_to_all | solution.py:17
  40.3 8.3 %all_to_all.32 = f32[4,16,160]{2,1,0:T(8,128)S(1)} all-to-all(f32[4,16,160]{2,1,0:T(8,128)S(1)} %broadcast_in_dim.12), channel_id=1, replica_groups=mesh['far'=8,'near'=2,'core'=2,'mdl'=16] {'near','core'}, dimensions={0} | all-to-all | bytes 81920 | tf_op jit(solution)/shard_map/all_to_all | solution.py:17
  48.6 0.0 copy-done.2
  48.6 0.0 copy-done.1
  48.6 1.1 convolution_bitcast_fusion
  49.7 0.7 copy.12
  50.4 20.8 %all_to_all.33 = f32[64,1,2560]{2,1,0:T(1,128)S(1)} all-to-all(f32[64,1,2560]{2,1,0:T(1,128)S(1)} %copy.12), channel_id=1, replica_groups=mesh['far'=8,'near'=2,'core'=2,'mdl'=16] {'near','core','mdl'}, dimensions={0} | all-to-all | bytes 1310720 | tf_op jit(solution)/shard_map/all_to_all | solution.py:25
  71.3 0.4 reduce_sum.38
  71.7 15.3 %all_to_all.34 = f32[8,1,2560]{2,1,0:T(1,128)S(1)} all-to-all(f32[8,1,2560]{2,1,0:T(1,128)S(1)} %broadcast_in_dim.13), channel_id=1, replica_groups=mesh['far'=8,'near'=2,'core'=2,'mdl'=16] {'far'}, dimensions={0} | all-to-all | bytes 163840 | tf_op jit(solution)/shard_map/all_to_all | solution.py:17
  87.0 0.1 reduce_sum.39
  87.1 1.2 broadcast_in_dim.14
  88.3 7.7 %all-to-all-start.5 = ((f32[64,1,2560]{2,1,0:T(1,128)}), f32[64,1,2560]{2,1,0:T(1,128)}, u32[]{:S(2)}, u32[]{:S(2)}) async-start(f32[64,1,2560]{2,1,0:T(1,128)} %broadcast_in_dim.14), calls=%async_computation.5 | async-start | bytes 1310720 | tf_op jit(solution)/shard_map/all_to_all | solution.py:17
  96.0 12.6 %all-to-all-done.5 = f32[64,1,2560]{2,1,0:T(1,128)} async-done(((f32[64,1,2560]{2,1,0:T(1,128)}), f32[64,1,2560]{2,1,0:T(1,128)}, u32[]{:S(2)}, u32[]{:S(2)}) %all-to-all-start.5) | async-done | bytes 655392 | tf_op jit(solution)/shard_map/all_to_all | solution.py:17
  108.7 1.6 %broadcast_multiply_fusion = f32[64,1,2560]{2,1,0:T(1,128)S(1)} fusion(f32[64,1,2560]{2,1,0:T(1,128)} %all-to-all-done.5), kind=kLoop, calls=%fused_computation.14 | loop fusion | flops 163840 | bytes 1310720 | tf_op jit(solution)/shard_map/div | solution.py:36
  110.3 0.7 fusion.7
  111.0 0.1 copy.14
  111.1 5.8 %cholesky.17 = f32[64,64]{1,0:T(8,128)S(1)} custom-call(f32[64,64]{1,0:T(8,128)S(1)} %fusion.14), custom_call_target="Cholesky" | custom-call | tf_op jit(solution)/shard_map/jit(cholesky)/cholesky | solution.py:38
  117.0 0.6 compare_reduce_fusion
  117.6 0.7 fusion.11
  118.3 4.9 %custom-call.7 = f32[1,64,64]{1,2,0:T(8,128)S(1)} custom-call(f32[1,64,64]{2,1,0:T(8,128)S(1)} %fusion.11), custom_call_target="InvertDiagBlocksLowerTriangular" | custom-call | tf_op jit(solution)/shard_map/jit(_solve_triangular)/triangular_solve | solution.py:39
  123.2 0.2 fusion.12
  123.4 0.2 fusion.15
  123.6 0.3 fusion.16
  123.9 1.5 %fusion.5 = f32[160,2560]{1,0:T(8,128)S(1)} fusion(f32[64,160]{1,0:T(8,128)S(1)} %fusion.16, f32[64,1,2560]{2,1,0:T(1,128)S(1)} %broadcast_multiply_fusion), kind=kOutput, calls=%fused_computation.8 | convolution fusion | flops 314572800 | bytes 2334720 | tf_op jit(solution)/shard_map/ka,kc->ac/dot_general | solution.py:44
  125.4 0.0 copy-start.3
  125.4 1.2 fusion.4
  126.6 0.0 copy-done.3
  126.6 0.8 add_multiply_fusion
  (8 shorter events, 0.1 us)
Async XLA Ops:
  0.6 1.1 copy-start
  0.6 47.9 %copy-start.2 = (bf16[1,160,2560]{2,1,0:T(8,128)(2,1)S(1)}, bf16[1,160,2560]{2,1,0:T(8,128)(2,1)}, u32[]{:S(2)}) copy-start(bf16[1,160,2560]{2,1,0:T(8,128)(2,1)} %param.4) | copy-start | bytes 2457604
  0.7 47.9 %copy-start.1 = (bf16[1,160,2560]{2,1,0:T(8,128)(2,1)S(1)}, bf16[1,160,2560]{2,1,0:T(8,128)(2,1)}, u32[]{:S(2)}) copy-start(bf16[1,160,2560]{2,1,0:T(8,128)(2,1)} %param.5) | copy-start | bytes 2457604
  88.3 20.4 %all-to-all-start.5 = ((f32[64,1,2560]{2,1,0:T(1,128)}), f32[64,1,2560]{2,1,0:T(1,128)}, u32[]{:S(2)}, u32[]{:S(2)}) async-start(f32[64,1,2560]{2,1,0:T(1,128)} %broadcast_in_dim.14), calls=%async_computation.5 | async-start | bytes 1310720 | tf_op jit(solution)/shard_map/all_to_all | solution.py:17
  125.4 1.2 copy-start.3

commit v2 on v1

--- a/solution.py
+++ b/solution.py
@@ -19,25 +19,38 @@
     )
 
 
-def spread_sum(shard, near, far):
-    count = lax.axis_size(near)
-    tiles = shard.reshape(count, shard.shape[0] // count, shard.shape[1])
-    own = lax.all_to_all(tiles, near, 0, 0, tiled=True).sum(axis=0)
-    own = to_each(own, far).sum(axis=0)
-    return to_each(own, near).reshape(shard.shape)
+def left_sum(part):
+    rank, rows = part.shape
+    count = lax.axis_size(PAIR)
+    own = lax.all_to_all(part.reshape(count, rank // count, rows), PAIR, 0, 0, tiled=True)
+    own = to_each(own.sum(axis=0), "far").sum(axis=0) / lax.axis_size(REP)
+    return to_each(own, PAIR).reshape(rank, rows)
 
 
 def body(deltas, errors, starts, momentum):
-    replicas = lax.axis_size(REP)
     merged = deltas[0].astype(jnp.float32) + errors[0].astype(jnp.float32)
     left_part = jnp.einsum("ac,ck->ka", merged, starts, precision=highest)
-    left = spread_sum(left_part, PAIR, "far") / replicas
+    left = left_sum(left_part)
+    rank = left.shape[0]
+    columns = merged.shape[1]
     right_part = jnp.einsum("ac,ka->kc", merged, left, precision=highest)
-    right = spread_sum(right_part, WIDE, "far") / replicas
-    gram = jnp.einsum("ck,lc->kl", starts, right, precision=highest)
+    share = rank // lax.axis_size(REP)
+    mine = lax.dynamic_slice_in_dim(left, lax.axis_index(REP) * share, share, 0)
+    gram_part = jnp.einsum("ka,la->kl", mine, left, precision=highest).reshape(1, -1)
+    load = jnp.concatenate(
+        [right_part, jnp.broadcast_to(gram_part, (rank, gram_part.shape[1]))], axis=1
+    )
+    seen = lax.all_to_all(load, WIDE, 0, 0, tiled=True)
+    row = seen[:, :columns].sum(axis=0)
+    pairs = lax.axis_size(PAIR)
+    lines = seen[:, columns:].reshape(pairs, -1, gram_part.shape[1]).sum(axis=1)
+    far = to_each(jnp.concatenate([row, lines.reshape(-1)]), "far")
+    row = far[:, :columns].sum(axis=0) / lax.axis_size(REP)
+    right = to_each(row, WIDE)
+    gram = far[:, columns:].reshape(rank, rank)
     lower = jnp.linalg.cholesky(gram)
     inverse = jax.scipy.linalg.solve_triangular(
-        lower, jnp.eye(lower.shape[0], dtype=jnp.float32), lower=True
+        lower, jnp.eye(rank, dtype=jnp.float32), lower=True
     )
     basis = jnp.einsum("kl,la->ka", inverse, left, precision=highest)
     turned = jnp.einsum("kl,ka->la", inverse, basis, precision=highest)

time: 128 us -> 115 us (0.90)
  waiting for transfers between devices: 12.6 us -> 3.26 us
  blocking collectives: 79.8 us -> 71.9 us
  starting transfers between devices: 7.73 us -> 13.4 us
  other arithmetic: 16.2 us -> 14.3 us
    all_to_all x1 -> x2, waiting for transfers between devices: 12.6 us -> 3.26 us  [to_each(): lax.all_to_all(jnp.broadcast_to(shard[None], (count, *shard.shape)), axes...]
    all_to_all x3 -> x2, blocking collectives: 46.5 us -> 38.3 us  [to_each(): lax.all_to_all(jnp.broadcast_to(shard[None], (count, *shard.shape)), axes...]
    all_to_all x1 -> x2, starting transfers between devices: 7.73 us -> 13.4 us  [to_each(): lax.all_to_all(jnp.broadcast_to(shard[None], (count, *shard.shape)), axes...]
    div x2, other arithmetic: 1.66 us -> 0.01 us  [the longest x1 0.01 us: left_sum(): own = to_each(own.sum(axis=0), 'far').sum(axis=0) / lax.axis_size(REP)]
  transfers between devices with their start and end apart: 1 -> 2, of which waited for: 1 -> 1; matrix products, arithmetic and copies ran while one was open for 0% -> 11% of each run, Pallas kernels for 0% -> 0%
where the time goes in v2:
time: 115 us; the launch traced here: 114 us
  blocking collectives  71.9 us (63%)
  other arithmetic  14.3 us (12%)
  starting transfers between devices  13.4 us (12%)
  matrix products  6.64 us (6%)
  local copies, waits for them, and re-layouts  3.97 us (3%)
  waiting for transfers between devices  3.26 us (3%)
    all_to_all x2, blocking collectives, to_each(): lax.all_to_all(jnp.broadcast_to(shard[None], (count, *shard.shape)), axes...  38.3 us
    all_to_all x1, blocking collectives, body(): seen = lax.all_to_all(load, WIDE, 0, 0, tiled=True)  21.1 us
    all_to_all x2, starting transfers between devices, to_each(): lax.all_to_all(jnp.broadcast_to(shard[None], (count, *shard.shape)), axes...  13.4 us
    all_to_all x1, blocking collectives, left_sum(): lax.all_to_all(part.reshape(count, rank // count, rows), PAIR, 0, 0, tile...  12.5 us
    another operation x3, other arithmetic, body(): lower = jnp.linalg.cholesky(gram)  6.52 us
    another operation x2, other arithmetic, body(): jax.scipy.linalg.solve_triangular(lower, jnp.eye(rank, dtype=jnp.float32)...  5.55 us
    all_to_all x2, waiting for transfers between devices, to_each(): lax.all_to_all(jnp.broadcast_to(shard[None], (count, *shard.shape)), axes...  3.26 us
    dot_general x1, matrix products, body(): left_part = jnp.einsum('ac,ck->ka', merged, starts, precision=highest)  3.19 us
  transfers between devices with their start and end apart: 2, of which 1 were waited for; matrix products, arithmetic and copies ran while one was open for 11% of the time, Pallas kernels for 0%

profile of v2, /device:TPU:1, one launch (start us, length us, event | category | flops | bytes accessed | tf_op | source)
XLA Modules:
  0.0 114.3 jit_solution(8456867604696479378)
XLA Ops:
  0.6 0.0 copy-start
  0.6 0.0 copy-start.1
  0.7 0.0 copy-start.2
  0.7 1.1 copy-done
  1.7 3.2 %fusion.2 = f32[160,64]{0,1:T(8,128)S(1)} fusion(f32[2560,64]{0,1:T(8,128)S(1)} %copy-done, bf16[1,160,2560]{2,1,0:T(8,128)(2,1)} %param.5, bf16[1,160,2560]{2,1,0:T(8,128)(2,1)} %param.4), kind=kOutput, calls=%fused_computation.3 | convolution fusion | flops 315801600 | bytes 2334720 | tf_op jit(solution)/shard_map/ac,ck->ka/dot_general | solution.py:32
  4.9 12.5 %all_to_all.45 = f32[4,16,160]{2,1,0:T(8,128)S(1)} all-to-all(f32[4,16,160]{2,1,0:T(8,128)S(1)} %bitcast.54), channel_id=1, replica_groups=mesh['far'=8,'near'=2,'core'=2,'mdl'=16] {'near','core'}, dimensions={0} | all-to-all | bytes 81920 | tf_op jit(solution)/shard_map/all_to_all | solution.py:25
  17.4 22.8 %all_to_all.46 = f32[8,16,160]{2,1,0:T(8,128)S(1)} all-to-all(f32[8,16,160]{2,1,0:T(8,128)S(1)} %broadcast_in_dim.15), channel_id=1, replica_groups=mesh['far'=8,'near'=2,'core'=2,'mdl'=16] {'far'}, dimensions={0} | all-to-all | bytes 163840 | tf_op jit(solution)/shard_map/all_to_all | solution.py:17
  40.3 0.6 broadcast_in_dim.16
  40.9 5.9 %all-to-all-start.2 = ((f32[4,16,160]{2,1,0:T(8,128)}), f32[4,16,160]{2,1,0:T(8,128)S(1)}, u32[]{:S(2)}, u32[]{:S(2)}) async-start(f32[4,16,160]{2,1,0:T(8,128)} %broadcast_in_dim.16), calls=%async_computation.2 | async-start | bytes 131072 | tf_op jit(solution)/shard_map/all_to_all | solution.py:17
  46.8 3.3 %all-to-all-done.2 = f32[4,16,160]{2,1,0:T(8,128)S(1)} async-done(((f32[4,16,160]{2,1,0:T(8,128)}), f32[4,16,160]{2,1,0:T(8,128)S(1)}, u32[]{:S(2)}, u32[]{:S(2)}) %all-to-all-start.2) | async-done | bytes 40992 | tf_op jit(solution)/shard_map/all_to_all | solution.py:17
  50.1 0.0 copy-done.1
  50.1 0.0 copy-done.2
  50.1 1.1 %fusion = f32[64,2560]{1,0:T(8,128)S(1)} fusion(f32[64,160]{1,0:T(8,128)S(1)} %bitcast.49, bf16[1,160,2560]{2,1,0:T(8,128)(2,1)S(1)} %copy-done.1, bf16[1,160,2560]{2,1,0:T(8,128)(2,1)S(1)} %copy-done.2), kind=kOutput, calls=%fused_computation.1 | convolution fusion | flops 315801600 | bytes 2334720 | tf_op jit(solution)/shard_map/ac,ka->kc/dot_general | solution.py:36
  51.3 0.1 fusion.13
  51.4 0.1 reshape.63
  51.5 0.1 maximum_bitcast_fusion
  51.6 0.7 copy.11
  52.3 21.1 %all_to_all.47 = f32[64,1,2688]{2,1,0:T(1,128)S(1)} all-to-all(f32[64,1,2688]{2,1,0:T(1,128)S(1)} %copy.11), channel_id=1, replica_groups=mesh['far'=8,'near'=2,'core'=2,'mdl'=16] {'near','core','mdl'}, dimensions={0} | all-to-all | bytes 1376256 | tf_op jit(solution)/shard_map/all_to_all | solution.py:43
  73.6 0.1 broadcast_in_dim.19
  73.6 15.5 %all_to_all.48 = f32[8,1,3072]{2,1,0:T(1,128)S(1)} all-to-all(f32[8,1,3072]{2,1,0:T(1,128)S(1)} %broadcast_in_dim.19), channel_id=1, replica_groups=mesh['far'=8,'near'=2,'core'=2,'mdl'=16] {'far'}, dimensions={0} | all-to-all | bytes 196608 | tf_op jit(solution)/shard_map/all_to_all | solution.py:17
  89.2 1.2 %broadcast_in_dim.21 = f32[64,1,2560]{2,1,0:T(1,128)} broadcast(f32[2560]{0:T(1024)S(1)} %broadcast_multiply_fusion.1), dimensions={2} | broadcast | bytes 665600 | tf_op jit(solution)/shard_map/broadcast_in_dim | solution.py:18
  90.3 7.5 %all-to-all-start.5 = ((f32[64,1,2560]{2,1,0:T(1,128)}), f32[64,1,2560]{2,1,0:T(1,128)S(1)}, u32[]{:S(2)}, u32[]{:S(2)}) async-start(f32[64,1,2560]{2,1,0:T(1,128)} %broadcast_in_dim.21), calls=%async_computation.5 | async-start | bytes 1310720 | tf_op jit(solution)/shard_map/all_to_all | solution.py:17
  97.8 0.1 reshape.62
  97.9 0.1 copy.12
  98.0 5.8 %cholesky.17 = f32[64,64]{1,0:T(8,128)S(1)} custom-call(f32[64,64]{1,0:T(8,128)S(1)} %fusion.12), custom_call_target="Cholesky" | custom-call | tf_op jit(solution)/shard_map/jit(cholesky)/cholesky | solution.py:51
  103.9 0.6 compare_reduce_fusion
  104.5 0.7 fusion.9
  105.2 4.9 %custom-call.7 = f32[1,64,64]{1,2,0:T(8,128)S(1)} custom-call(f32[1,64,64]{2,1,0:T(8,128)S(1)} %fusion.9), custom_call_target="InvertDiagBlocksLowerTriangular" | custom-call | tf_op jit(solution)/shard_map/jit(_solve_triangular)/triangular_solve | solution.py:52
  110.1 0.2 fusion.10
  110.3 0.2 fusion.16
  110.5 0.3 fusion.17
  110.8 0.0 all-to-all-done.5
  110.8 1.5 %fusion.6 = f32[160,2560]{1,0:T(8,128)S(1)} fusion(f32[64,160]{1,0:T(8,128)S(1)} %fusion.17, f32[64,1,2560]{2,1,0:T(1,128)S(1)} %all-to-all-done.5), kind=kOutput, calls=%fused_computation.11 | convolution fusion | flops 314572800 | bytes 2334720 | tf_op jit(solution)/shard_map/ka,kc->ac/dot_general | solution.py:57
  112.3 0.0 copy-start.3
  112.3 1.2 %fusion.5 = bf16[1,160,2560]{2,1,0:T(8,128)(2,1)} fusion(f32[160,2560]{1,0:T(8,128)S(1)} %fusion.6, bf16[1,160,2560]{2,1,0:T(8,128)(2,1)S(1)} %copy-done.1, bf16[1,160,2560]{2,1,0:T(8,128)(2,1)S(1)} %copy-done.2), kind=kLoop, calls=%fused_computation.7 | loop fusion | flops 2048000 | bytes 4096000 | tf_op jit(solution)/shard_map/broadcast_in_dim | solution.py:58
  113.5 0.0 copy-done.3
  113.5 0.8 add_multiply_fusion
  (15 shorter events, 0.3 us)
Async XLA Ops:
  0.6 1.1 copy-start
  0.6 49.4 %copy-start.1 = (bf16[1,160,2560]{2,1,0:T(8,128)(2,1)S(1)}, bf16[1,160,2560]{2,1,0:T(8,128)(2,1)}, u32[]{:S(2)}) copy-start(bf16[1,160,2560]{2,1,0:T(8,128)(2,1)} %param.5) | copy-start | bytes 2457604
  0.7 49.4 %copy-start.2 = (bf16[1,160,2560]{2,1,0:T(8,128)(2,1)S(1)}, bf16[1,160,2560]{2,1,0:T(8,128)(2,1)}, u32[]{:S(2)}) copy-start(bf16[1,160,2560]{2,1,0:T(8,128)(2,1)} %param.4) | copy-start | bytes 2457604
  40.9 9.2 %all-to-all-start.2 = ((f32[4,16,160]{2,1,0:T(8,128)}), f32[4,16,160]{2,1,0:T(8,128)S(1)}, u32[]{:S(2)}, u32[]{:S(2)}) async-start(f32[4,16,160]{2,1,0:T(8,128)} %broadcast_in_dim.16), calls=%async_computation.2 | async-start | bytes 131072 | tf_op jit(solution)/shard_map/all_to_all | solution.py:17
  90.3 20.5 %all-to-all-start.5 = ((f32[64,1,2560]{2,1,0:T(1,128)}), f32[64,1,2560]{2,1,0:T(1,128)S(1)}, u32[]{:S(2)}, u32[]{:S(2)}) async-start(f32[64,1,2560]{2,1,0:T(1,128)} %broadcast_in_dim.21), calls=%async_computation.5 | async-start | bytes 1310720 | tf_op jit(solution)/shard_map/all_to_all | solution.py:17
  112.3 1.2 %copy-start.3 = (f32[160,80]{1,0:T(8,128)S(1)}, f32[160,80]{1,0:T(8,128)}, u32[]{:S(2)}) copy-start(f32[160,80]{1,0:T(8,128)} %param.7) | copy-start | bytes 153604

commit v3 on v1

v3 whole, which is shorter than its diff:
```python
import jax
import jax.numpy as jnp
from jax import lax
from jax.experimental import pallas as pl
from jax.experimental.pallas import tpu as pltpu
from jax.sharding import Mesh
from jax.sharding import PartitionSpec as P

REP = ("far", "near", "core")
PAIR = ("near", "core")
WIDE = ("near", "core", "mdl")
CHUNKS = 4


highest = lax.Precision.HIGHEST
ANY = pl.BlockSpec(memory_space=pl.ANY)
VMEM = pl.BlockSpec(memory_space=pltpu.VMEM)
SMEM = pl.BlockSpec(memory_space=pltpu.SMEM)


def held(shape):
    return pltpu.VMEM(shape, jnp.float32)


def near_core(values):
    return pltpu.with_memory_space_constraint(values, pltpu.VMEM)


def pieces_of(values, count):
    found = []
    for _ in range(count):
        piece = values.astype(jnp.bfloat16)
        found.append(piece)
        values = values - piece.astype(jnp.float32)
    return found


def dot(a, b, dims):
    return lax.dot_general(a, b, (dims, ((), ())), preferred_element_type=jnp.float32)


def folded(stack, count):
    rows = stack.shape[0] // count
    return sum(stack[i * rows : (i + 1) * rows] for i in reversed(range(count)))


def left_kernel(deltas, errors, starts, out, d_buf, e_buf, s_buf, sems):
    width = d_buf.shape[1] // CHUNKS
    copies = []
    for j in range(CHUNKS):
        cut = pl.ds(j * width, width)
        three = (
            pltpu.make_async_copy(starts.at[:, cut], s_buf.at[:, cut], sems.at[j, 0]),
            pltpu.make_async_copy(deltas.at[0, :, cut], d_buf.at[:, cut], sems.at[j, 1]),
            pltpu.make_async_copy(errors.at[0, :, cut], e_buf.at[:, cut], sems.at[j, 2]),
        )
        for copy in three:
            copy.start()
        copies.append(three)
    total = None
    for j in range(CHUNKS):
        cut = slice(j * width, (j + 1) * width)
        copies[j][0].wait()
        stack = jnp.concatenate(pieces_of(s_buf[:, cut], 3), axis=0)
        copies[j][1].wait()
        part = dot(stack, d_buf[:, cut], ((1,), (1,)))
        copies[j][2].wait()
        part = part + dot(stack, e_buf[:, cut], ((1,), (1,)))
        total = part if total is None else total + part
    out[...] = folded(total, 3).reshape(out.shape)


def left_part_of(deltas, errors, starts):
    rows, columns = deltas.shape[1:]
    rank = starts.shape[0]
    count = lax.axis_size(PAIR)
    return pl.pallas_call(
        left_kernel,
        out_shape=held((count, rank // count, rows)),
        in_specs=[ANY, ANY, ANY],
        out_specs=VMEM,
        scratch_shapes=[
            pltpu.VMEM((rows, columns), jnp.bfloat16),
            pltpu.VMEM((rows, columns), jnp.bfloat16),
            pltpu.VMEM((rank, columns), jnp.float32),
            pltpu.SemaphoreType.DMA((CHUNKS, 3)),
        ],
        name="left_part",
    )(deltas, errors, starts)


def gram_line(left, place):
    rank = left.shape[0]
    share = 128 // rank
    index = lax.broadcasted_iota(jnp.int32, left.shape, 0)
    nothing = jnp.zeros_like(left)
    line = None
    for i in range(share):
        own = jnp.sum(jnp.where(index == place * share + i, left, nothing), axis=0, keepdims=True)
        lanes = jnp.concatenate([nothing] * i + [left] + [nothing] * (share - 1 - i), axis=0)
        part = lax.dot_general(
            own, lanes, (((1,), (1,)), ((), ())), precision=highest, preferred_element_type=jnp.float32
        )
        line = part if line is None else line + part
    return line


def right_kernel(place, left, deltas, errors, out):
    columns = deltas.shape[2]
    width = columns // CHUNKS
    rank = left.shape[0] * left.shape[1]
    whole = left[...].reshape(rank, left.shape[2])
    line = gram_line(whole, place[0])
    stack = jnp.concatenate(pieces_of(whole, 3), axis=0)
    for j in range(CHUNKS):
        cut = slice(j * width, (j + 1) * width)
        part = dot(stack, deltas[0, :, cut], ((1,), (0,)))
        part = part + dot(stack, errors[0, :, cut], ((1,), (0,)))
        out[:, 0, cut] = folded(part, 3)
    out[:, 0, columns:] = jnp.broadcast_to(line, (rank, line.shape[1]))


def right_part_of(place, left, deltas, errors):
    rank = left.shape[0] * left.shape[1]
    columns = deltas.shape[2]
    return pl.pallas_call(
        right_kernel,
        out_shape=held((rank, 1, columns + 128)),
        in_specs=[SMEM, VMEM, VMEM, VMEM],
        out_specs=VMEM,
        name="right_part",
    )(place, near_core(left), near_core(deltas), near_core(errors))


def out_kernel(place, turned, flipped, right, deltas, errors, momentum, new_errors, new_momentum, outer_step, buf, sems):
    columns = right.shape[2]
    owned = momentum.shape[1]
    width = columns // CHUNKS
    copies = []
    for j in range(CHUNKS):
        cut = slice(j * width, (j + 1) * width)
        big, small = pieces_of(right[:, 0, cut], 2)
        approx = dot(flipped[...], jnp.concatenate([big, small, big, small], axis=0), ((1,), (0,)))
        merged = deltas[0, :, cut].astype(jnp.float32) + errors[0, :, cut].astype(jnp.float32)
        buf[:, cut] = (merged - approx).astype(jnp.bfloat16)
        cut = pl.ds(j * width, width)
        copy = pltpu.make_async_copy(buf.at[:, cut], new_errors.at[0, :, cut], sems.at[j])
        copy.start()
        copies.append(copy)
    first = place[0] * owned
    base = jnp.minimum(first // 128, columns // 128 - 2) * 128
    window = right[:, 0, pl.ds(pl.multiple_of(base, 128), 256)]
    window = pltpu.roll(window, lax.rem(256 - (first - base), 256), 1)[:, :128]
    mine = lax.dot_general(
        turned[...], window, (((0,), (0,)), ((), ())), precision=highest, preferred_element_type=jnp.float32
    )[:, :owned]
    fresh = 0.9 * momentum[...] + mine
    new_momentum[...] = fresh
    outer_step[...] = 0.7 * (mine + 0.9 * fresh)
    for copy in copies:
        copy.wait()


def outputs_of(place, turned, right, deltas, errors, momentum):
    big, small = pieces_of(turned, 2)
    flipped = jnp.concatenate([big, big, small, small], axis=0).T
    f32 = jnp.float32
    return pl.pallas_call(
        out_kernel,
        out_shape=(
            jax.ShapeDtypeStruct(deltas.shape, jnp.bfloat16),
            jax.ShapeDtypeStruct(momentum.shape, f32),
            jax.ShapeDtypeStruct(momentum.shape, f32),
        ),
        in_specs=[SMEM, VMEM, VMEM, VMEM, VMEM, VMEM, VMEM],
        out_specs=(ANY, VMEM, VMEM),
        scratch_shapes=[
            pltpu.VMEM(deltas.shape[1:], jnp.bfloat16),
            pltpu.SemaphoreType.DMA((CHUNKS,)),
        ],
        name="outputs",
    )(place, near_core(turned), near_core(flipped), near_core(right), near_core(deltas), near_core(errors), near_core(momentum))


def to_each(shard, axes):
    count = lax.axis_size(axes)
    return lax.all_to_all(
        jnp.broadcast_to(shard[None], (count, *shard.shape)), axes, 0, 0, tiled=True
    )


def body(deltas, errors, starts, momentum):
    replicas = lax.axis_size(REP)
    rank = starts.shape[1]
    columns = deltas.shape[2]
    place = lax.axis_index(REP)[None]
    left_part, place = lax.optimization_barrier((left_part_of(deltas, errors, starts.T), place))
    own = lax.all_to_all(left_part, PAIR, 0, 0, tiled=True).sum(axis=0)
    own = to_each(own, "far").sum(axis=0) / replicas
    tiles = to_each(own, PAIR)
    left = tiles.reshape(rank, -1)
    load = right_part_of(place, tiles, deltas, errors)
    seen = lax.all_to_all(load, WIDE, 0, 0, tiled=True)
    row = seen[:, :, :columns].sum(axis=0)
    pairs = lax.axis_size(PAIR)
    lines = seen[:, 0, columns:].reshape(pairs, -1, 128).sum(axis=1)
    far = to_each(jnp.concatenate([row, lines.reshape(1, -1)], axis=1), "far")
    row = far[:, :, :columns].sum(axis=0) / replicas
    right = to_each(row, WIDE)
    gram = far[:, 0, columns:].reshape(rank, rank)
    lower = jnp.linalg.cholesky(gram)
    inverse = jax.scipy.linalg.solve_triangular(
        lower, jnp.eye(rank, dtype=jnp.float32), lower=True
    )
    basis = jnp.einsum("kl,la->ka", inverse, left, precision=highest)
    turned = jnp.einsum("kl,ka->la", inverse, basis, precision=highest)
    return outputs_of(place, turned, right, deltas, errors, momentum)


def solution(mesh):
    torus = Mesh(mesh.devices.reshape(8, 2, 2, 16), ("far", "near", "core", "mdl"))
    in_specs = (P(REP, "mdl", None), P(REP, "mdl", None), P(), P("mdl", REP))
    out_specs = (P(REP, "mdl", None), P("mdl", REP), P("mdl", REP))
    return jax.shard_map(body, mesh=torus, in_specs=in_specs, out_specs=out_specs, check_vma=False)
```

time: 128 us -> 113 us (0.88)
  waiting for transfers between devices: 12.6 us -> 0.01 us
  Pallas kernels: 0 us -> 7.82 us
  matrix products: 7.17 us -> 0.68 us
  other arithmetic: 16.2 us -> 12.6 us
    all_to_all x1, waiting for transfers between devices: 12.6 us -> 0.01 us  [to_each(): lax.all_to_all(jnp.broadcast_to(shard[None], (count, *shard.shape)), axes...]
    pallas_call x0 -> x3, Pallas kernels: none -> 7.82 us  [the longest x1 3.83 us: outputs_of(): pl.pallas_call(out_kernel, out_shape=(jax.ShapeDtypeStruct(deltas.shape,...]
    dot_general x4 -> x0, matrix products: 6.49 us -> none  [the longest x1 3.19 us: body(): left_part = jnp.einsum('ac,ck->ka', merged, starts, precision=highest)]
    div x2, other arithmetic: 1.66 us -> 0.01 us  [the longest x1 0.01 us: body(): own = to_each(own, 'far').sum(axis=0) / replicas]
  transfers between devices with their start and end apart: 1 -> 1, of which waited for: 1 -> 0; matrix products, arithmetic and copies ran while one was open for 0% -> 12% of each run, Pallas kernels for 0% -> 0%
where the time goes in v3:
time: 113 us; the launch traced here: 112 us
  blocking collectives  80.3 us (71%)
  other arithmetic  12.6 us (11%)
  Pallas kernels  7.82 us (7%)
  starting transfers between devices  7.49 us (7%)
  local copies, waits for them, and re-layouts  2.45 us (2%)
    all_to_all x3, blocking collectives, to_each(): lax.all_to_all(jnp.broadcast_to(shard[None], (count, *shard.shape)), axes...  46.6 us
    all_to_all x1, blocking collectives, body(): seen = lax.all_to_all(load, WIDE, 0, 0, tiled=True)  21.1 us
    all_to_all x1, blocking collectives, body(): own = lax.all_to_all(left_part, PAIR, 0, 0, tiled=True).sum(axis=0)  12.6 us
    all_to_all x1, starting transfers between devices, to_each(): lax.all_to_all(jnp.broadcast_to(shard[None], (count, *shard.shape)), axes...  7.49 us
    another operation x3, other arithmetic, body(): lower = jnp.linalg.cholesky(gram)  6.52 us
    another operation x2, other arithmetic, body(): jax.scipy.linalg.solve_triangular(lower, jnp.eye(rank, dtype=jnp.float32)...  5.55 us
    pallas_call x1, Pallas kernels, outputs_of(): pl.pallas_call(out_kernel, out_shape=(jax.ShapeDtypeStruct(deltas.shape,...  3.83 us
    pallas_call x1, Pallas kernels, left_part_of(): pl.pallas_call(left_kernel, out_shape=held((count, rank // count, rows)),...  3.05 us
  transfers between devices with their start and end apart: 1, of which 0 were waited for; matrix products, arithmetic and copies ran while one was open for 12% of the time, Pallas kernels for 0%

profile of v3, /device:TPU:1, one launch (start us, length us, event | category | flops | bytes accessed | tf_op | source)
XLA Modules:
  0.0 112.2 jit_solution(9173273385777699157)
XLA Ops:
  0.6 0.0 copy-start.1
  0.6 3.0 %left_part.1 = f32[4,16,160]{2,1,0:T(8,128)S(1)} custom-call(bf16[1,160,2560]{2,1,0:T(8,128)(2,1)} %deltas.5, bf16[1,160,2560]{2,1,0:T(8,128)(2,1)} %errors.5, f32[64,2560]{1,0:T(8,128)} %bitcast.24), custom_call_target="tpu_custom_call" | custom-call | tf_op jit(solution)/shard_map/left_part/pallas_call | solution.py:77
  3.7 0.0 copy-start
  3.7 12.6 %all_to_all.30 = f32[4,16,160]{2,1,0:T(8,128)S(1)} all-to-all(f32[4,16,160]{2,1,0:T(8,128)S(1)} %left_part.1), channel_id=1, replica_groups=mesh['far'=8,'near'=2,'core'=2,'mdl'=16] {'near','core'}, dimensions={0} | all-to-all | bytes 81920 | tf_op jit(solution)/shard_map/all_to_all | solution.py:198
  16.3 22.8 %all_to_all.31 = f32[8,16,160]{2,1,0:T(8,128)S(1)} all-to-all(f32[8,16,160]{2,1,0:T(8,128)S(1)} %broadcast_in_dim.14), channel_id=1, replica_groups=mesh['far'=8,'near'=2,'core'=2,'mdl'=16] {'far'}, dimensions={0} | all-to-all | bytes 163840 | tf_op jit(solution)/shard_map/all_to_all | solution.py:187
  39.2 8.3 %all_to_all.32.left = f32[4,16,160]{2,1,0:T(8,128)S(1)} all-to-all(f32[4,16,160]{2,1,0:T(8,128)S(1)} %broadcast_in_dim.15), channel_id=1, replica_groups=mesh['far'=8,'near'=2,'core'=2,'mdl'=16] {'near','core'}, dimensions={0} | all-to-all | bytes 81920 | tf_op jit(solution)/shard_map/all_to_all | solution.py:187
  47.5 0.0 copy-done.1
  47.5 0.0 copy-done
  47.5 0.9 right_part.1
  48.5 21.1 %all_to_all.33 = f32[64,1,2688]{2,1,0:T(1,128)S(1)} all-to-all(f32[64,1,2688]{2,1,0:T(1,128)S(1)} %right_part.1), channel_id=1, replica_groups=mesh['far'=8,'near'=2,'core'=2,'mdl'=16] {'near','core','mdl'}, dimensions={0} | all-to-all | bytes 1376256 | tf_op jit(solution)/shard_map/all_to_all | solution.py:203
  69.6 0.3 slice_reduce_fusion
  70.0 0.1 broadcast_in_dim.17
  70.0 15.5 %all_to_all.34 = f32[8,1,3072]{2,1,0:T(1,128)S(1)} all-to-all(f32[8,1,3072]{2,1,0:T(1,128)S(1)} %broadcast_in_dim.17), channel_id=1, replica_groups=mesh['far'=8,'near'=2,'core'=2,'mdl'=16] {'far'}, dimensions={0} | all-to-all | bytes 196608 | tf_op jit(solution)/shard_map/all_to_all | solution.py:187
  85.5 0.1 slice_reduce_fusion.1
  85.6 1.2 %broadcast_in_dim.36 = f32[64,1,2560]{2,1,0:T(1,128)} broadcast(f32[2560]{0:T(1024)S(1)} %broadcast_multiply_fusion.1), dimensions={2} | broadcast | bytes 665600 | tf_op jit(solution)/shard_map/broadcast_in_dim | solution.py:188
  86.7 7.5 %all-to-all-start.5 = ((f32[64,1,2560]{2,1,0:T(1,128)}), f32[64,1,2560]{2,1,0:T(1,128)S(1)}, u32[]{:S(2)}, u32[]{:S(2)}) async-start(f32[64,1,2560]{2,1,0:T(1,128)} %broadcast_in_dim.36), calls=%async_computation.5 | async-start | bytes 1310720 | tf_op jit(solution)/shard_map/all_to_all | solution.py:187
  94.3 0.1 reshape_squeeze.7
  94.3 0.1 copy.19
  94.4 5.8 %cholesky.17 = f32[64,64]{1,0:T(8,128)S(1)} custom-call(f32[64,64]{1,0:T(8,128)S(1)} %fusion.3), custom_call_target="Cholesky" | custom-call | tf_op jit(solution)/shard_map/jit(cholesky)/cholesky | solution.py:211
  100.3 0.6 compare_reduce_fusion
  101.0 0.7 fusion
  101.6 4.9 %custom-call.7 = f32[1,64,64]{1,2,0:T(8,128)S(1)} custom-call(f32[1,64,64]{2,1,0:T(8,128)S(1)} %fusion), custom_call_target="InvertDiagBlocksLowerTriangular" | custom-call | tf_op jit(solution)/shard_map/jit(_solve_triangular)/triangular_solve | solution.py:212
  106.5 0.2 fusion.1
  106.8 0.2 fusion.5
  107.0 0.3 fusion.4
  107.2 0.1 copy.22
  107.3 0.1 copy.21
  107.5 0.0 copy-start.2
  107.5 0.1 maximum_bitcast_fusion.flipped
  107.6 0.0 all-to-all-done.5.right
  107.6 0.8 copy-done.2
  108.4 3.8 %outputs.1 = (bf16[1,160,2560]{2,1,0:T(8,128)(2,1)}, f32[160,80]{1,0:T(8,128)}, f32[160,80]{1,0:T(8,128)}) custom-call(s32[1]{0:T(128)} %bitcast.1.place, f32[64,160]{1,0:T(8,128)S(1)} %get-tuple-element.8.turned, bf16[160,256]{1,0:T(8,128)(2,1)S(1)} %maximum_bitcast_fusion.flipped, f32[64,1,2560]{2,1,0:T(1,128)S(1)} %all-to-all-done.5.right, ...), custom_call_target="tpu_custom_call" | custom-call | tf_op jit(solution)/shard_map/outputs/pallas_call | solution.py:168
  (14 shorter events, 0.2 us)
Async XLA Ops:
  0.6 46.9 %copy-start.1 = (bf16[1,160,2560]{2,1,0:T(8,128)(2,1)S(1)}, bf16[1,160,2560]{2,1,0:T(8,128)(2,1)}, u32[]{:S(2)}) copy-start(bf16[1,160,2560]{2,1,0:T(8,128)(2,1)} %errors.5) | copy-start | bytes 2457604
  3.7 43.8 %copy-start = (bf16[1,160,2560]{2,1,0:T(8,128)(2,1)S(1)}, bf16[1,160,2560]{2,1,0:T(8,128)(2,1)}, u32[]{:S(2)}) copy-start(bf16[1,160,2560]{2,1,0:T(8,128)(2,1)} %deltas.5) | copy-start | bytes 2457604
  86.7 20.9 %all-to-all-start.5 = ((f32[64,1,2560]{2,1,0:T(1,128)}), f32[64,1,2560]{2,1,0:T(1,128)S(1)}, u32[]{:S(2)}, u32[]{:S(2)}) async-start(f32[64,1,2560]{2,1,0:T(1,128)} %broadcast_in_dim.36), calls=%async_computation.5 | async-start | bytes 1310720 | tf_op jit(solution)/shard_map/all_to_all | solution.py:187
  107.5 0.9 copy-start.2

commit v4 on v3

v4 whole, which is shorter than its diff:
```python
import jax
import jax.numpy as jnp
from jax import lax
from jax.experimental import pallas as pl
from jax.experimental.pallas import tpu as pltpu
from jax.sharding import Mesh
from jax.sharding import PartitionSpec as P

REP = ("far", "near", "core")
PAIR = ("near", "core")
NODES = ("near", "mdl")
WIDE = ("core", "near", "mdl")
CHUNKS = 4


highest = lax.Precision.HIGHEST
ANY = pl.BlockSpec(memory_space=pl.ANY)
HBM = pl.BlockSpec(memory_space=pltpu.HBM)
VMEM = pl.BlockSpec(memory_space=pltpu.VMEM)
SMEM = pl.BlockSpec(memory_space=pltpu.SMEM)
SMALL = pltpu.CompilerParams(vmem_limit_bytes=24 << 20)


def held(shape):
    return pltpu.VMEM(shape, jnp.float32)


def near_core(values):
    return pltpu.with_memory_space_constraint(values, pltpu.VMEM)


def far_off(values):
    return pltpu.with_memory_space_constraint(values, pltpu.HBM)


def pieces_of(values, count):
    found = []
    for _ in range(count):
        piece = values.astype(jnp.bfloat16)
        found.append(piece)
        values = values - piece.astype(jnp.float32)
    return found


def dot(a, b, dims):
    return lax.dot_general(a, b, (dims, ((), ())), preferred_element_type=jnp.float32)


def folded(stack, count):
    rows = stack.shape[0] // count
    return sum(stack[i * rows : (i + 1) * rows] for i in reversed(range(count)))


def left_kernel(place, deltas, errors, starts, out, partner, d_buf, e_buf, s_buf, sems):
    width = d_buf.shape[1] // CHUNKS
    copies = []
    for j in range(CHUNKS):
        cut = pl.ds(j * width, width)
        three = (
            pltpu.make_async_copy(starts.at[:, cut], s_buf.at[:, cut], sems.at[j, 0]),
            pltpu.make_async_copy(deltas.at[0, :, cut], d_buf.at[:, cut], sems.at[j, 1]),
            pltpu.make_async_copy(errors.at[0, :, cut], e_buf.at[:, cut], sems.at[j, 2]),
        )
        for copy in three:
            copy.start()
        copies.append(three)
    total = None
    for j in range(CHUNKS):
        cut = slice(j * width, (j + 1) * width)
        copies[j][0].wait()
        stack = jnp.concatenate(pieces_of(s_buf[:, cut], 3), axis=0)
        copies[j][1].wait()
        part = dot(stack, d_buf[:, cut], ((1,), (1,)))
        copies[j][2].wait()
        part = part + dot(stack, e_buf[:, cut], ((1,), (1,)))
        total = part if total is None else total + part
    share = partner.shape[1]
    cut = pl.ds(pl.multiple_of((1 - place[0] % 2) * share, 128), share)
    partner[...] = d_buf[:, cut].astype(jnp.float32) + e_buf[:, cut].astype(jnp.float32)
    out[...] = folded(total, 3).reshape(out.shape)


def left_part_of(place, deltas, errors, starts):
    rows, columns = deltas.shape[1:]
    rank = starts.shape[0]
    count = lax.axis_size(PAIR)
    return pl.pallas_call(
        left_kernel,
        out_shape=(
            held((count, rank // count, rows)),
            held((rows, columns // 2)),
        ),
        in_specs=[SMEM, HBM, HBM, HBM],
        out_specs=(VMEM, VMEM),
        scratch_shapes=[
            pltpu.VMEM((rows, columns), jnp.bfloat16),
            pltpu.VMEM((rows, columns), jnp.bfloat16),
            held((rank, columns)),
            pltpu.SemaphoreType.DMA((CHUNKS, 3)),
        ],
        compiler_params=SMALL,
        name="left_part",
    )(place, far_off(deltas), far_off(errors), far_off(starts))


def gram_lines(left, first, count):
    rank = left.shape[0]
    share = 128 // rank
    index = lax.broadcasted_iota(jnp.int32, left.shape, 0)
    nothing = jnp.zeros_like(left)
    lines = None
    for i in range(share):
        own = jnp.concatenate(
            [
                jnp.sum(jnp.where(index == first + share * n + i, left, nothing), axis=0, keepdims=True)
                for n in range(count)
            ],
            axis=0,
        )
        lanes = jnp.concatenate([nothing] * i + [left] + [nothing] * (share - 1 - i), axis=0)
        part = lax.dot_general(
            own, lanes, (((1,), (1,)), ((), ())), precision=highest, preferred_element_type=jnp.float32
        )
        lines = part if lines is None else lines + part
    return lines


def right_kernel(place, left, partner, deltas, errors, out):
    columns = partner.shape[1]
    chunks = CHUNKS // 2
    width = columns // chunks
    rank = left.shape[0] * left.shape[1]
    whole = left[...].reshape(rank, left.shape[2])
    stack = jnp.concatenate(pieces_of(whole, 3), axis=0)
    base = place[0] % 2 * columns
    for j in range(chunks):
        cut = slice(j * width, (j + 1) * width)
        own = pl.ds(pl.multiple_of(base + j * width, 128), width)
        merged = deltas[0, :, own].astype(jnp.float32) + errors[0, :, own].astype(jnp.float32)
        pieces = pieces_of(merged + partner[:, cut], 3)
        part = None
        for piece in reversed(pieces):
            term = dot(stack, piece, ((1,), (0,)))
            part = term if part is None else part + term
        out[:, 0, cut] = folded(part, 3)
    lines = gram_lines(whole, place[0] // 2 * 4, 2)
    parity = lax.broadcasted_iota(jnp.int32, (rank, lines.shape[1]), 0) % 2
    out[:, 0, columns:] = jnp.where(parity == 0, lines[0:1], lines[1:2])


def right_part_of(place, left, partner, deltas, errors):
    rank = left.shape[0] * left.shape[1]
    return pl.pallas_call(
        right_kernel,
        out_shape=held((rank, 1, partner.shape[1] + 128)),
        in_specs=[SMEM, VMEM, VMEM, VMEM, VMEM],
        out_specs=VMEM,
        compiler_params=SMALL,
        name="right_part",
    )(place, near_core(left), near_core(partner), near_core(deltas), near_core(errors))


def out_kernel(place, turned, flipped, right, deltas, errors, momentum, new_errors, new_momentum, outer_step, buf, fresh, step, sems):
    half = right.shape[3]
    owned = momentum.shape[1]
    each = half // owned
    first = place[0] % each * owned
    base = pl.multiple_of(jnp.minimum(first // 128, half // 128 - 2) * 128, 128)
    window = right[place[0] // each, :, 0, pl.ds(base, 256)]
    window = pltpu.roll(window, lax.rem(256 - (first - base), 256), 1)[:, :128]
    mine = lax.dot_general(
        turned[...], window, (((0,), (0,)), ((), ())), precision=highest, preferred_element_type=jnp.float32
    )[:, :owned]
    fresh[...] = 0.9 * momentum[...] + mine
    step[...] = 0.7 * (mine + 0.9 * fresh[...])
    copies = [
        pltpu.make_async_copy(fresh, new_momentum, sems.at[CHUNKS]),
        pltpu.make_async_copy(step, outer_step, sems.at[CHUNKS + 1]),
    ]
    for copy in copies:
        copy.start()
    width = 2 * half // CHUNKS
    for j in range(CHUNKS):
        side, start = divmod(j * width, half)
        big, small = pieces_of(right[side, :, 0, start : start + width], 2)
        approx = dot(flipped[...], jnp.concatenate([big, small, big, small], axis=0), ((1,), (0,)))
        cut = pl.ds(j * width, width)
        merged = deltas[0, :, cut].astype(jnp.float32) + errors[0, :, cut].astype(jnp.float32)
        buf[:, cut] = (merged - approx).astype(jnp.bfloat16)
        copy = pltpu.make_async_copy(buf.at[:, cut], new_errors.at[0, :, cut], sems.at[j])
        copy.start()
        copies.append(copy)
    for copy in copies:
        copy.wait()


def outputs_of(place, turned, right, deltas, errors, momentum):
    big, small = pieces_of(turned, 2)
    flipped = jnp.concatenate([big, big, small, small], axis=0).T
    f32 = jnp.float32
    return pl.pallas_call(
        out_kernel,
        out_shape=(
            jax.ShapeDtypeStruct(deltas.shape, jnp.bfloat16),
            jax.ShapeDtypeStruct(momentum.shape, f32),
            jax.ShapeDtypeStruct(momentum.shape, f32),
        ),
        in_specs=[SMEM, VMEM, VMEM, VMEM, VMEM, VMEM, VMEM],
        out_specs=(HBM, HBM, HBM),
        scratch_shapes=[
            pltpu.VMEM(deltas.shape[1:], jnp.bfloat16),
            held(momentum.shape),
            held(momentum.shape),
            pltpu.SemaphoreType.DMA((CHUNKS + 2,)),
        ],
        compiler_params=SMALL,
        name="outputs",
    )(place, near_core(turned), near_core(flipped), near_core(right), near_core(deltas), near_core(errors), near_core(momentum))


def to_each(shard, axes):
    count = lax.axis_size(axes)
    return lax.all_to_all(
        jnp.broadcast_to(shard[None], (count, *shard.shape)), axes, 0, 0, tiled=True
    )


def body(deltas, errors, starts, momentum):
    replicas = lax.axis_size(REP)
    rank = starts.shape[1]
    columns = deltas.shape[2]
    place = lax.axis_index(REP)[None]
    left_part, other = left_part_of(place, deltas, errors, starts.T)
    own = lax.all_to_all(left_part, PAIR, 0, 0, tiled=True).sum(axis=0)
    partner = lax.ppermute(other, "core", [(0, 1), (1, 0)])
    own = to_each(own, "far").sum(axis=0) / replicas
    own, partner = lax.optimization_barrier((own, partner))
    tiles = to_each(own, PAIR)
    left = tiles.reshape(rank, -1)
    load = right_part_of(place, tiles, partner, deltas, errors)
    half = columns // 2
    nodes = lax.axis_size(NODES)
    load = load.reshape(nodes, rank // nodes, 1, -1)
    seen = lax.all_to_all(load, NODES, 0, 0, tiled=True)
    row = seen[..., :half].sum(axis=0)
    lines = seen[..., half:].reshape(lax.axis_size("near"), -1, rank // nodes, 128).sum(axis=1)
    far = to_each(jnp.concatenate([row.reshape(1, -1), lines.reshape(1, -1)], axis=1), "far")
    row = far[:, :, :columns].sum(axis=0) / replicas
    right = to_each(row, WIDE).reshape(2, rank, 1, half)
    gram = far[:, 0, columns:].reshape(rank, rank)
    lower = jnp.linalg.cholesky(gram)
    inverse = jax.scipy.linalg.solve_triangular(
        lower, jnp.eye(rank, dtype=jnp.float32), lower=True
    )
    basis = jnp.einsum("kl,la->ka", inverse, left, precision=highest)
    turned = jnp.einsum("kl,ka->la", inverse, basis, precision=highest)
    return outputs_of(place, turned, right, deltas, errors, momentum)


def solution(mesh):
    torus = Mesh(mesh.devices.reshape(8, 2, 2, 16), ("far", "near", "core", "mdl"))
    in_specs = (P(REP, "mdl", None), P(REP, "mdl", None), P(), P("mdl", REP))
    out_specs = (P(REP, "mdl", None), P("mdl", REP), P("mdl", REP))
    return jax.shard_map(body, mesh=torus, in_specs=in_specs, out_specs=out_specs, check_vma=False)
```

time: 113 us -> 108 us (0.956)
  blocking collectives: 80.3 us -> 67.4 us
  starting transfers between devices: 7.49 us -> 16.9 us
    ppermute x0 -> x1, starting transfers between devices: none -> 8.88 us  [body(): partner = lax.ppermute(other, 'core', [(0, 1), (1, 0)])]
    all_to_all x1, blocking collectives: 12.6 us -> 5.63 us  [body(): own = lax.all_to_all(left_part, PAIR, 0, 0, tiled=True).sum(axis=0)]
    all_to_all x1, blocking collectives: 21.1 us -> 15.4 us  [body(): seen = lax.all_to_all(load, NODES, 0, 0, tiled=True)]
  transfers between devices with their start and end apart: 1 -> 2, of which waited for: 0 -> 1; matrix products, arithmetic and copies ran while one was open for 12% -> 12% of each run, Pallas kernels for 0% -> 0%
where the time goes in v4:
time: 108 us
  blocking collectives  67.4 us (62%)
  starting transfers between devices  16.9 us (16%)
  other arithmetic  12.5 us (12%)
  Pallas kernels  7.25 us (7%)
  local copies, waits for them, and re-layouts  1.9 us (2%)
    all_to_all x3, blocking collectives, to_each(): lax.all_to_all(jnp.broadcast_to(shard[None], (count, *shard.shape)), axes...  46.4 us
    all_to_all x1, blocking collectives, body(): seen = lax.all_to_all(load, NODES, 0, 0, tiled=True)  15.4 us
    ppermute x1, starting transfers between devices, body(): partner = lax.ppermute(other, 'core', [(0, 1), (1, 0)])  8.88 us
    all_to_all x1, starting transfers between devices, to_each(): lax.all_to_all(jnp.broadcast_to(shard[None], (count, *shard.shape)), axes...  7.98 us
    another operation x3, other arithmetic, body(): lower = jnp.linalg.cholesky(gram)  6.52 us
    all_to_all x1, blocking collectives, body(): own = lax.all_to_all(left_part, PAIR, 0, 0, tiled=True).sum(axis=0)  5.63 us
    another operation x2, other arithmetic, body(): jax.scipy.linalg.solve_triangular(lower, jnp.eye(rank, dtype=jnp.float32)...  5.55 us
    pallas_call x1, Pallas kernels, outputs_of(): pl.pallas_call(out_kernel, out_shape=(jax.ShapeDtypeStruct(deltas.shape,...  3.23 us
  transfers between devices with their start and end apart: 2, of which 1 were waited for; matrix products, arithmetic and copies ran while one was open for 12% of the time, Pallas kernels for 0%

profile of v4, /device:TPU:1, one launch (start us, length us, event | category | flops | bytes accessed | tf_op | source)
XLA Modules:
  0.0 108.0 jit_solution(13084562963812753164)
XLA Ops:
  0.6 0.0 copy-start.1
  0.6 3.2 %left_part.1 = (f32[4,16,160]{2,1,0:T(8,128)S(1)}, f32[160,1280]{1,0:T(8,128)S(1)}) custom-call(s32[1]{0:T(128)} %bitcast.place, bf16[1,160,2560]{2,1,0:T(8,128)(2,1)} %deltas.5, bf16[1,160,2560]{2,1,0:T(8,128)(2,1)} %errors.5, f32[64,2560]{1,0:T(8,128)} %bitcast.29), custom_call_target="tpu_custom_call" | custom-call | tf_op jit(solution)/shard_map/left_part/pallas_call | solution.py:87
  3.8 0.0 copy-start
  3.8 8.9 %collective-permute-start = (f32[160,1280]{1,0:T(8,128)S(1)}, f32[160,1280]{1,0:T(8,128)S(1)}, u32[]{:S(2)}, u32[]{:S(2)}) collective-permute-start(f32[160,1280]{1,0:T(8,128)S(1)} %get-tuple-element.8), channel_id=1, source_target_pairs={{0,16},{16,0},{1,17},{17,1},{2,18},{18,2},{3,19},{19,3},{4,20},{20... | collective-permute-start | bytes 2457608 | tf_op jit(solution)/shard_map/ppermute | solution.py:235
  12.7 5.6 %all_to_all.30 = f32[4,16,160]{2,1,0:T(8,128)S(1)} all-to-all(f32[4,16,160]{2,1,0:T(8,128)S(1)} %get-tuple-element.7), channel_id=1, replica_groups=mesh['far'=8,'near'=2,'core'=2,'mdl'=16] {'near','core'}, dimensions={0} | all-to-all | bytes 81920 | tf_op jit(solution)/shard_map/all_to_all | solution.py:234
  18.4 22.8 %all_to_all.31 = f32[8,16,160]{2,1,0:T(8,128)S(1)} all-to-all(f32[8,16,160]{2,1,0:T(8,128)S(1)} %broadcast_in_dim.14), channel_id=1, replica_groups=mesh['far'=8,'near'=2,'core'=2,'mdl'=16] {'far'}, dimensions={0} | all-to-all | bytes 163840 | tf_op jit(solution)/shard_map/all_to_all | solution.py:223
  41.2 0.0 collective-permute-done.partner
  41.2 8.3 %all_to_all.32.left = f32[4,16,160]{2,1,0:T(8,128)S(1)} all-to-all(f32[4,16,160]{2,1,0:T(8,128)S(1)} %broadcast_in_dim.15), channel_id=1, replica_groups=mesh['far'=8,'near'=2,'core'=2,'mdl'=16] {'near','core'}, dimensions={0} | all-to-all | bytes 81920 | tf_op jit(solution)/shard_map/all_to_all | solution.py:223
  49.6 0.0 copy-done.1
  49.6 0.0 copy-done
  49.6 0.9 right_part.1
  50.4 15.4 %all_to_all.33 = f32[32,2,1,1408]{3,2,1,0:T(1,128)S(1)} all-to-all(f32[32,2,1,1408]{3,2,1,0:T(1,128)S(1)} %bitcast.27), channel_id=1, replica_groups=mesh['far'=8,'near'=2,'core'=2,'mdl'=16] {'near','mdl'}, dimensions={0} | all-to-all | bytes 720896 | tf_op jit(solution)/shard_map/all_to_all | solution.py:244
  65.8 0.1 slice_reduce_fusion
  66.0 0.1 broadcast_in_dim.17
  66.1 15.3 %all_to_all.34 = f32[8,1,3072]{2,1,0:T(1,128)S(1)} all-to-all(f32[8,1,3072]{2,1,0:T(1,128)S(1)} %broadcast_in_dim.17), channel_id=1, replica_groups=mesh['far'=8,'near'=2,'core'=2,'mdl'=16] {'far'}, dimensions={0} | all-to-all | bytes 196608 | tf_op jit(solution)/shard_map/all_to_all | solution.py:223
  81.4 0.1 slice_reduce_fusion.1
  81.5 1.2 %broadcast_in_dim.36 = f32[64,1,2560]{2,1,0:T(1,128)} broadcast(f32[2560]{0:T(1024)S(1)} %broadcast_multiply_fusion.1), dimensions={2} | broadcast | bytes 665600 | tf_op jit(solution)/shard_map/broadcast_in_dim | solution.py:224
  82.7 8.0 %all-to-all-start.5 = ((f32[64,1,2560]{2,1,0:T(1,128)}), f32[64,1,2560]{2,1,0:T(1,128)S(1)}, u32[]{:S(2)}, u32[]{:S(2)}) async-start(f32[64,1,2560]{2,1,0:T(1,128)} %broadcast_in_dim.36), calls=%async_computation.5 | async-start | bytes 1310720 | tf_op jit(solution)/shard_map/all_to_all | solution.py:223
  90.7 0.1 reshape_squeeze.3
  90.8 0.1 copy.19
  90.9 5.8 %cholesky.17 = f32[64,64]{1,0:T(8,128)S(1)} custom-call(f32[64,64]{1,0:T(8,128)S(1)} %fusion.3), custom_call_target="Cholesky" | custom-call | tf_op jit(solution)/shard_map/jit(cholesky)/cholesky | solution.py:251
  96.8 0.6 compare_reduce_fusion
  97.4 0.7 fusion
  98.1 4.9 %custom-call.7 = f32[1,64,64]{1,2,0:T(8,128)S(1)} custom-call(f32[1,64,64]{2,1,0:T(8,128)S(1)} %fusion), custom_call_target="InvertDiagBlocksLowerTriangular" | custom-call | tf_op jit(solution)/shard_map/jit(_solve_triangular)/triangular_solve | solution.py:252
  103.0 0.2 fusion.1
  103.2 0.2 fusion.5
  103.4 0.3 fusion.4
  103.7 0.1 copy.22
  103.8 0.1 copy.21
  103.9 0.0 copy-start.2
  103.9 0.1 maximum_bitcast_fusion.flipped
  104.0 0.6 all-to-all-done.5
  104.6 0.2 copy-done.2
  104.8 3.2 %outputs.1 = (bf16[1,160,2560]{2,1,0:T(8,128)(2,1)}, f32[160,80]{1,0:T(8,128)}, f32[160,80]{1,0:T(8,128)}) custom-call(s32[1]{0:T(128)} %bitcast.place, f32[64,160]{1,0:T(8,128)S(1)} %get-tuple-element.12.turned, bf16[160,256]{1,0:T(8,128)(2,1)S(1)} %maximum_bitcast_fusion.flipped, f32[2,64,1,1280]{3,2,1,0:T(1,128)S(1)} %bitcast.26, ...), custom_call_target="tpu_custom_call" | custom-call | tf_op jit(solution)/shard_map/outputs/pallas_call | solution.py:201
  (14 shorter events, 0.2 us)
Async XLA Ops:
  0.6 48.9 %copy-start.1 = (bf16[1,160,2560]{2,1,0:T(8,128)(2,1)S(1)}, bf16[1,160,2560]{2,1,0:T(8,128)(2,1)}, u32[]{:S(2)}) copy-start(bf16[1,160,2560]{2,1,0:T(8,128)(2,1)} %errors.5) | copy-start | bytes 2457604
  3.8 45.8 %copy-start = (bf16[1,160,2560]{2,1,0:T(8,128)(2,1)S(1)}, bf16[1,160,2560]{2,1,0:T(8,128)(2,1)}, u32[]{:S(2)}) copy-start(bf16[1,160,2560]{2,1,0:T(8,128)(2,1)} %deltas.5) | copy-start | bytes 2457604
  3.8 37.4 %collective-permute-start = (f32[160,1280]{1,0:T(8,128)S(1)}, f32[160,1280]{1,0:T(8,128)S(1)}, u32[]{:S(2)}, u32[]{:S(2)}) collective-permute-start(f32[160,1280]{1,0:T(8,128)S(1)} %get-tuple-element.8), channel_id=1, source_target_pairs={{0,16},{16,0},{1,17},{17,1},{2,18},{18,2},{3,19},{19,3},{4,20},{20... | collective-permute-start | bytes 2457608 | tf_op jit(solution)/shard_map/ppermute | solution.py:235
  82.7 21.9 %all-to-all-start.5 = ((f32[64,1,2560]{2,1,0:T(1,128)}), f32[64,1,2560]{2,1,0:T(1,128)S(1)}, u32[]{:S(2)}, u32[]{:S(2)}) async-start(f32[64,1,2560]{2,1,0:T(1,128)} %broadcast_in_dim.36), calls=%async_computation.5 | async-start | bytes 1310720 | tf_op jit(solution)/shard_map/all_to_all | solution.py:223
  103.9 0.9 copy-start.2

commit v5 on v4

--- a/solution.py
+++ b/solution.py
@@ -9,8 +9,9 @@
 REP = ("far", "near", "core")
 PAIR = ("near", "core")
 NODES = ("near", "mdl")
-WIDE = ("core", "near", "mdl")
+SWAP = [(0, 1), (1, 0)]
 CHUNKS = 4
+BLOCK = 4
 
 
 highest = lax.Precision.HIGHEST
@@ -160,43 +161,118 @@
     )(place, near_core(left), near_core(partner), near_core(deltas), near_core(errors))
 
 
-def out_kernel(place, turned, flipped, right, deltas, errors, momentum, new_errors, new_momentum, outer_step, buf, fresh, step, sems):
-    half = right.shape[3]
+def lower_inverse_of(gram):
+    rank = gram.shape[0]
+    ident = jnp.where(
+        lax.broadcasted_iota(jnp.int32, (rank, rank), 0) == lax.broadcasted_iota(jnp.int32, (rank, rank), 1), 1.0, 0.0
+    )
+    table = jnp.concatenate([gram, ident], axis=1)
+    index = lax.broadcasted_iota(jnp.int32, table.shape, 0)
+    for k in range(0, rank, BLOCK):
+        cols = [jnp.broadcast_to(table[:, k + j : k + j + 1], table.shape) for j in range(BLOCK)]
+        for j in range(BLOCK):
+            at = k + j
+            scale = 1.0 / cols[j][at : at + 1]
+            ratio = jnp.where(index > at, cols[j] * scale, 0.0)
+            for n in range(j + 1, BLOCK):
+                cols[n] = cols[n] - ratio * cols[n][at : at + 1]
+            line = table[at : at + 1]
+            table = jnp.where(index == at, line * jnp.sqrt(scale), table - ratio * line)
+    lane = lax.broadcasted_iota(jnp.int32, table.shape, 1)
+    return jnp.where(lane < rank, pltpu.roll(table, rank, 1), table)
+
+
+def factor_kernel(gram, left, out):
+    rank = gram.shape[0]
+    whole = left[...].reshape(rank, left.shape[2])
+    inverse = lower_inverse_of(gram[...])
+    basis = lax.dot_general(
+        inverse[:, :rank], whole, (((1,), (0,)), ((), ())), precision=highest, preferred_element_type=jnp.float32
+    )
+    twice = lax.dot_general(
+        basis, inverse, (((0,), (0,)), ((), ())), precision=highest, preferred_element_type=jnp.float32
+    )
+    out[...] = jnp.concatenate(pieces_of(twice, 2), axis=1)
+
+
+def factor_of(gram, left):
+    return pl.pallas_call(
+        factor_kernel,
+        out_shape=pltpu.VMEM((left.shape[2], 4 * gram.shape[0]), jnp.bfloat16),
+        in_specs=[VMEM, VMEM],
+        out_specs=VMEM,
+        compiler_params=SMALL,
+        cost_estimate=pl.CostEstimate(flops=40_000_000, transcendentals=0, bytes_accessed=200_000),
+        name="factor",
+    )(near_core(gram), near_core(left))
+
+
+def product(flipped, right):
+    big, small = pieces_of(right, 2)
+    return dot(flipped, jnp.concatenate([big, small, big, small], axis=0), ((1,), (0,)))
+
+
+def residue(flipped, right, deltas, errors, base, j, width):
+    approx = product(flipped[...], right[:, 0, j * width : (j + 1) * width])
+    cut = pl.ds(pl.multiple_of(base + j * width, 128), width)
+    merged = deltas[0, :, cut].astype(jnp.float32) + errors[0, :, cut].astype(jnp.float32)
+    return (merged - approx).astype(jnp.bfloat16)
+
+
+def near_kernel(place, flipped, right, deltas, errors, out):
+    half = right.shape[2]
+    width = half // (CHUNKS // 2)
+    base = place[0] % 2 * half
+    for j in range(CHUNKS // 2):
+        out[:, j * width : (j + 1) * width] = residue(flipped, right, deltas, errors, base, j, width)
+
+
+def near_half_of(place, flipped, right, deltas, errors):
+    return pl.pallas_call(
+        near_kernel,
+        out_shape=pltpu.VMEM((deltas.shape[1], right.shape[2]), jnp.bfloat16),
+        in_specs=[SMEM, VMEM, VMEM, VMEM, VMEM],
+        out_specs=VMEM,
+        compiler_params=SMALL,
+        cost_estimate=pl.CostEstimate(flops=40_000_000, transcendentals=0, bytes_accessed=2_000_000),
+        name="near_half",
+    )(place, near_core(flipped), near_core(right), near_core(deltas), near_core(errors))
+
+
+def out_kernel(place, flipped, right, other, ready, deltas, errors, momentum, new_errors, new_momentum, outer_step, buf, fresh, step, sems):
+    half = right.shape[2]
     owned = momentum.shape[1]
     each = half // owned
+    core = place[0] % 2
+    own = pl.ds(pl.multiple_of(core * half, 128), half)
+    copies = [pltpu.make_async_copy(ready, new_errors.at[0, :, own], sems.at[0])]
+    copies[0].start()
     first = place[0] % each * owned
     base = pl.multiple_of(jnp.minimum(first // 128, half // 128 - 2) * 128, 128)
-    window = right[place[0] // each, :, 0, pl.ds(base, 256)]
+    cut = pl.ds(base, 256)
+    window = jnp.where(place[0] // each == core, right[:, 0, cut], other[:, 0, cut])
     window = pltpu.roll(window, lax.rem(256 - (first - base), 256), 1)[:, :128]
-    mine = lax.dot_general(
-        turned[...], window, (((0,), (0,)), ((), ())), precision=highest, preferred_element_type=jnp.float32
-    )[:, :owned]
+    mine = product(flipped[...], window)[:, :owned]
     fresh[...] = 0.9 * momentum[...] + mine
     step[...] = 0.7 * (mine + 0.9 * fresh[...])
-    copies = [
-        pltpu.make_async_copy(fresh, new_momentum, sems.at[CHUNKS]),
-        pltpu.make_async_copy(step, outer_step, sems.at[CHUNKS + 1]),
-    ]
-    for copy in copies:
+    copies.append(pltpu.make_async_copy(fresh, new_momentum, sems.at[1]))
+    copies.append(pltpu.make_async_copy(step, outer_step, sems.at[2]))
+    for copy in copies[1:]:
         copy.start()
-    width = 2 * half // CHUNKS
-    for j in range(CHUNKS):
-        side, start = divmod(j * width, half)
-        big, small = pieces_of(right[side, :, 0, start : start + width], 2)
-        approx = dot(flipped[...], jnp.concatenate([big, small, big, small], axis=0), ((1,), (0,)))
-        cut = pl.ds(j * width, width)
-        merged = deltas[0, :, cut].astype(jnp.float32) + errors[0, :, cut].astype(jnp.float32)
-        buf[:, cut] = (merged - approx).astype(jnp.bfloat16)
-        copy = pltpu.make_async_copy(buf.at[:, cut], new_errors.at[0, :, cut], sems.at[j])
+    width = half // (CHUNKS // 2)
+    base = (1 - core) * half
+    for j in range(CHUNKS // 2):
+        cut = slice(j * width, (j + 1) * width)
+        buf[:, cut] = residue(flipped, other, deltas, errors, base, j, width)
+        there = pl.ds(pl.multiple_of(base + j * width, 128), width)
+        copy = pltpu.make_async_copy(buf.at[:, pl.ds(j * width, width)], new_errors.at[0, :, there], sems.at[3 + j])
         copy.start()
         copies.append(copy)
     for copy in copies:
         copy.wait()
 
 
-def outputs_of(place, turned, right, deltas, errors, momentum):
-    big, small = pieces_of(turned, 2)
-    flipped = jnp.concatenate([big, big, small, small], axis=0).T
+def outputs_of(place, flipped, right, other, ready, deltas, errors, momentum):
     f32 = jnp.float32
     return pl.pallas_call(
         out_kernel,
@@ -205,17 +281,17 @@
             jax.ShapeDtypeStruct(momentum.shape, f32),
             jax.ShapeDtypeStruct(momentum.shape, f32),
         ),
-        in_specs=[SMEM, VMEM, VMEM, VMEM, VMEM, VMEM, VMEM],
+        in_specs=[SMEM] + [VMEM] * 7,
         out_specs=(HBM, HBM, HBM),
         scratch_shapes=[
-            pltpu.VMEM(deltas.shape[1:], jnp.bfloat16),
+            pltpu.VMEM(ready.shape, jnp.bfloat16),
             held(momentum.shape),
             held(momentum.shape),
-            pltpu.SemaphoreType.DMA((CHUNKS + 2,)),
+            pltpu.SemaphoreType.DMA((3 + CHUNKS // 2,)),
         ],
         compiler_params=SMALL,
         name="outputs",
-    )(place, near_core(turned), near_core(flipped), near_core(right), near_core(deltas), near_core(errors), near_core(momentum))
+    )(place, *(near_core(a) for a in (flipped, right, other, ready, deltas, errors, momentum)))
 
 
 def to_each(shard, axes):
@@ -232,11 +308,10 @@
     place = lax.axis_index(REP)[None]
     left_part, other = left_part_of(place, deltas, errors, starts.T)
     own = lax.all_to_all(left_part, PAIR, 0, 0, tiled=True).sum(axis=0)
-    partner = lax.ppermute(other, "core", [(0, 1), (1, 0)])
+    partner = lax.ppermute(other, "core", SWAP)
     own = to_each(own, "far").sum(axis=0) / replicas
     own, partner = lax.optimization_barrier((own, partner))
     tiles = to_each(own, PAIR)
-    left = tiles.reshape(rank, -1)
     load = right_part_of(place, tiles, partner, deltas, errors)
     half = columns // 2
     nodes = lax.axis_size(NODES)
@@ -246,15 +321,13 @@
     lines = seen[..., half:].reshape(lax.axis_size("near"), -1, rank // nodes, 128).sum(axis=1)
     far = to_each(jnp.concatenate([row.reshape(1, -1), lines.reshape(1, -1)], axis=1), "far")
     row = far[:, :, :columns].sum(axis=0) / replicas
-    right = to_each(row, WIDE).reshape(2, rank, 1, half)
+    right = to_each(row, NODES).reshape(rank, 1, half)
     gram = far[:, 0, columns:].reshape(rank, rank)
-    lower = jnp.linalg.cholesky(gram)
-    inverse = jax.scipy.linalg.solve_triangular(
-        lower, jnp.eye(rank, dtype=jnp.float32), lower=True
-    )
-    basis = jnp.einsum("kl,la->ka", inverse, left, precision=highest)
-    turned = jnp.einsum("kl,ka->la", inverse, basis, precision=highest)
-    return outputs_of(place, turned, right, deltas, errors, momentum)
+    flipped = factor_of(0.5 * (gram + gram.T), tiles)
+    right, flipped = lax.optimization_barrier((right, flipped))
+    other = lax.ppermute(right, "core", SWAP)
+    ready = near_half_of(place, flipped, right, deltas, errors)
+    return outputs_of(place, flipped, right, other, ready, deltas, errors, momentum)
 
 
 def solution(mesh):

time: 108 us -> 105 us (0.972)
  other arithmetic: 12.5 us -> 0.29 us
  waiting for transfers between devices: 0.56 us -> 4.66 us
  Pallas kernels: 7.25 us -> 10.6 us
  starting transfers between devices: 16.9 us -> 19.8 us
    another operation x5 -> x0, other arithmetic: 12.1 us -> none  [the longest x3 6.52 us: body(): lower = jnp.linalg.cholesky(gram)]
    ppermute x1 -> x2, starting transfers between devices: 8.88 us -> 15.9 us  [the longest x1 8.88 us: body(): partner = lax.ppermute(other, 'core', SWAP)]
    pallas_call x0 -> x2, Pallas kernels: none -> 4.52 us  [the longest x1 3.3 us: factor_of(): pl.pallas_call(factor_kernel, out_shape=pltpu.VMEM((left.shape[2], 4 * gr...]
    all_to_all x1, starting transfers between devices: 7.98 us -> 3.88 us  [to_each(): lax.all_to_all(jnp.broadcast_to(shard[None], (count, *shard.shape)), axes...]
    all_to_all x1, waiting for transfers between devices: 0.56 us -> 4.64 us  [to_each(): lax.all_to_all(jnp.broadcast_to(shard[None], (count, *shard.shape)), axes...]
    pallas_call x1, Pallas kernels: 3.23 us -> 2.03 us  [outputs_of(): pl.pallas_call(out_kernel, out_shape=(jax.ShapeDtypeStruct(deltas.shape,...]
  transfers between devices with their start and end apart: 2 -> 3, of which waited for: 1 -> 1; matrix products, arithmetic and copies ran while one was open for 12% -> 0% of each run, Pallas kernels for 0% -> 4%
where the time goes in v5:
time: 105 us
  blocking collectives  67.4 us (64%)
  starting transfers between devices  19.8 us (19%)
  Pallas kernels  10.6 us (10%)
  waiting for transfers between devices  4.66 us (4%)
  local copies, waits for them, and re-layouts  1.21 us (1%)
    all_to_all x3, blocking collectives, to_each(): lax.all_to_all(jnp.broadcast_to(shard[None], (count, *shard.shape)), axes...  46.4 us
    all_to_all x1, blocking collectives, body(): seen = lax.all_to_all(load, NODES, 0, 0, tiled=True)  15.4 us
    ppermute x1, starting transfers between devices, body(): partner = lax.ppermute(other, 'core', SWAP)  8.88 us
    ppermute x1, starting transfers between devices, body(): other = lax.ppermute(right, 'core', SWAP)  7.01 us
    all_to_all x1, blocking collectives, body(): own = lax.all_to_all(left_part, PAIR, 0, 0, tiled=True).sum(axis=0)  5.63 us
    all_to_all x1, waiting for transfers between devices, to_each(): lax.all_to_all(jnp.broadcast_to(shard[None], (count, *shard.shape)), axes...  4.64 us
    all_to_all x1, starting transfers between devices, to_each(): lax.all_to_all(jnp.broadcast_to(shard[None], (count, *shard.shape)), axes...  3.88 us
    pallas_call x1, Pallas kernels, factor_of(): pl.pallas_call(factor_kernel, out_shape=pltpu.VMEM((left.shape[2], 4 * gr...  3.3 us
  transfers between devices with their start and end apart: 3, of which 1 were waited for; matrix products, arithmetic and copies ran while one was open for 0% of the time, Pallas kernels for 4%

profile of v5, /device:TPU:1, one launch (start us, length us, event | category | flops | bytes accessed | tf_op | source)
XLA Modules:
  0.0 104.7 jit_solution(9729783481526803132)
XLA Ops:
  0.6 0.0 copy-start.1
  0.6 3.2 %left_part.1 = (f32[4,16,160]{2,1,0:T(8,128)S(1)}, f32[160,1280]{1,0:T(8,128)S(1)}) custom-call(s32[1]{0:T(128)} %bitcast.place, bf16[1,160,2560]{2,1,0:T(8,128)(2,1)} %deltas.7, bf16[1,160,2560]{2,1,0:T(8,128)(2,1)} %errors.7, f32[64,2560]{1,0:T(8,128)} %bitcast.18), custom_call_target="tpu_custom_call" | custom-call | tf_op jit(solution)/shard_map/left_part/pallas_call | solution.py:88
  3.8 0.0 copy-start
  3.8 8.9 %collective-permute-start = (f32[160,1280]{1,0:T(8,128)S(1)}, f32[160,1280]{1,0:T(8,128)S(1)}, u32[]{:S(2)}, u32[]{:S(2)}) collective-permute-start(f32[160,1280]{1,0:T(8,128)S(1)} %get-tuple-element.10), channel_id=1, source_target_pairs={{0,16},{16,0},{1,17},{17,1},{2,18},{18,2},{3,19},{19,3},{4,20},{20... | collective-permute-start | bytes 2457608 | tf_op jit(solution)/shard_map/ppermute | solution.py:311
  12.7 5.6 %all_to_all.30 = f32[4,16,160]{2,1,0:T(8,128)S(1)} all-to-all(f32[4,16,160]{2,1,0:T(8,128)S(1)} %get-tuple-element.9), channel_id=1, replica_groups=mesh['far'=8,'near'=2,'core'=2,'mdl'=16] {'near','core'}, dimensions={0} | all-to-all | bytes 81920 | tf_op jit(solution)/shard_map/all_to_all | solution.py:310
  18.4 22.8 %all_to_all.31 = f32[8,16,160]{2,1,0:T(8,128)S(1)} all-to-all(f32[8,16,160]{2,1,0:T(8,128)S(1)} %broadcast_in_dim.13), channel_id=1, replica_groups=mesh['far'=8,'near'=2,'core'=2,'mdl'=16] {'far'}, dimensions={0} | all-to-all | bytes 163840 | tf_op jit(solution)/shard_map/all_to_all | solution.py:299
  41.2 0.0 collective-permute-done.partner
  41.2 8.3 %all_to_all.32.left = f32[4,16,160]{2,1,0:T(8,128)S(1)} all-to-all(f32[4,16,160]{2,1,0:T(8,128)S(1)} %broadcast_in_dim.14), channel_id=1, replica_groups=mesh['far'=8,'near'=2,'core'=2,'mdl'=16] {'near','core'}, dimensions={0} | all-to-all | bytes 81920 | tf_op jit(solution)/shard_map/all_to_all | solution.py:299
  49.6 0.0 copy-done.1
  49.6 0.0 copy-done
  49.6 0.9 right_part.1
  50.4 15.4 %all_to_all.33 = f32[32,2,1,1408]{3,2,1,0:T(1,128)S(1)} all-to-all(f32[32,2,1,1408]{3,2,1,0:T(1,128)S(1)} %bitcast.17), channel_id=1, replica_groups=mesh['far'=8,'near'=2,'core'=2,'mdl'=16] {'near','mdl'}, dimensions={0} | all-to-all | bytes 720896 | tf_op jit(solution)/shard_map/all_to_all | solution.py:319
  65.8 0.1 slice_reduce_fusion
  66.0 0.1 broadcast_in_dim.16
  66.1 15.3 %all_to_all.34 = f32[8,1,3072]{2,1,0:T(1,128)S(1)} all-to-all(f32[8,1,3072]{2,1,0:T(1,128)S(1)} %broadcast_in_dim.16), channel_id=1, replica_groups=mesh['far'=8,'near'=2,'core'=2,'mdl'=16] {'far'}, dimensions={0} | all-to-all | bytes 196608 | tf_op jit(solution)/shard_map/all_to_all | solution.py:299
  81.4 0.1 slice_reduce_fusion.1
  81.5 0.9 broadcast_in_dim.34
  82.4 3.9 %all-to-all-start.5 = ((f32[32,1,2560]{2,1,0:T(1,128)}), f32[32,1,2560]{2,1,0:T(1,128)S(1)}, u32[]{:S(2)}, u32[]{:S(2)}) async-start(f32[32,1,2560]{2,1,0:T(1,128)} %broadcast_in_dim.34), calls=%async_computation.5 | async-start | bytes 655360 | tf_op jit(solution)/shard_map/all_to_all | solution.py:299
  86.3 0.1 reshape_squeeze.3
  86.4 0.1 copy.10
  86.5 3.3 %factor.1.flipped = bf16[160,256]{1,0:T(8,128)(2,1)S(1)} custom-call(f32[64,64]{1,0:T(8,128)S(1)} %fusion.gram, f32[4,16,160]{2,1,0:T(8,128)S(1)} %all_to_all.32.left), custom_call_target="tpu_custom_call" | custom-call | flops 40000000 | bytes 200000 | tf_op jit(solution)/shard_map/factor/pallas_call | solution.py:199
  89.8 4.6 %all-to-all-done.5 = f32[32,1,2560]{2,1,0:T(1,128)S(1)} async-done(((f32[32,1,2560]{2,1,0:T(1,128)}), f32[32,1,2560]{2,1,0:T(1,128)S(1)}, u32[]{:S(2)}, u32[]{:S(2)}) %all-to-all-start.5) | async-done | bytes 327712 | tf_op jit(solution)/shard_map/all_to_all | solution.py:299
  94.4 0.0 copy-start.2
  94.4 7.0 %collective-permute-start.1 = (f32[64,1,1280]{2,1,0:T(1,128)S(1)}, f32[64,1,1280]{2,1,0:T(1,128)S(1)}, u32[]{:S(2)}, u32[]{:S(2)}) collective-permute-start(f32[64,1,1280]{2,1,0:T(1,128)S(1)} %bitcast.14), channel_id=1, source_target_pairs={{0,16},{16,0},{1,17},{17,1},{2,18},{18,2},{3,19},{19,3},{4,20},{20... | collective-permute-start | bytes 983048 | tf_op jit(solution)/shard_map/ppermute | solution.py:328
  101.5 1.2 %near_half.1.ready = bf16[160,1280]{1,0:T(8,128)(2,1)S(1)} custom-call(s32[1]{0:T(128)} %bitcast.place, bf16[160,256]{1,0:T(8,128)(2,1)S(1)} %factor.1.flipped, f32[64,1,1280]{2,1,0:T(1,128)S(1)} %bitcast.15, bf16[1,160,2560]{2,1,0:T(8,128)(2,1)S(1)} %copy-done, bf16[1,160,2560]{2,1,0:T(8,128)(2,1)S(1)} %copy-done.1), custom_call_target="tpu_custom_call" | custom-call | flops 40000000 | bytes 2000000 | tf_op jit(solution)/shard_map/near_half/pallas_call | solution.py:231
  102.7 0.0 collective-permute-done.1.other
  102.7 0.0 copy-done.2
  102.7 2.0 %outputs.1 = (bf16[1,160,2560]{2,1,0:T(8,128)(2,1)}, f32[160,80]{1,0:T(8,128)}, f32[160,80]{1,0:T(8,128)}) custom-call(s32[1]{0:T(128)} %bitcast.place, bf16[160,256]{1,0:T(8,128)(2,1)S(1)} %factor.1.flipped, f32[64,1,1280]{2,1,0:T(1,128)S(1)} %bitcast.16, f32[64,1,1280]{2,1,0:T(1,128)S(1)} %collective-permute-done.1.other, ...), custom_call_target="tpu_custom_call" | custom-call | tf_op jit(solution)/shard_map/outputs/pallas_call | solution.py:277
  (12 shorter events, 0.2 us)
Async XLA Ops:
  0.6 48.9 %copy-start.1 = (bf16[1,160,2560]{2,1,0:T(8,128)(2,1)S(1)}, bf16[1,160,2560]{2,1,0:T(8,128)(2,1)}, u32[]{:S(2)}) copy-start(bf16[1,160,2560]{2,1,0:T(8,128)(2,1)} %errors.7) | copy-start | bytes 2457604
  3.8 45.8 %copy-start = (bf16[1,160,2560]{2,1,0:T(8,128)(2,1)S(1)}, bf16[1,160,2560]{2,1,0:T(8,128)(2,1)}, u32[]{:S(2)}) copy-start(bf16[1,160,2560]{2,1,0:T(8,128)(2,1)} %deltas.7) | copy-start | bytes 2457604
  3.8 37.4 %collective-permute-start = (f32[160,1280]{1,0:T(8,128)S(1)}, f32[160,1280]{1,0:T(8,128)S(1)}, u32[]{:S(2)}, u32[]{:S(2)}) collective-permute-start(f32[160,1280]{1,0:T(8,128)S(1)} %get-tuple-element.10), channel_id=1, source_target_pairs={{0,16},{16,0},{1,17},{17,1},{2,18},{18,2},{3,19},{19,3},{4,20},{20... | collective-permute-start | bytes 2457608 | tf_op jit(solution)/shard_map/ppermute | solution.py:311
  82.4 12.1 %all-to-all-start.5 = ((f32[32,1,2560]{2,1,0:T(1,128)}), f32[32,1,2560]{2,1,0:T(1,128)S(1)}, u32[]{:S(2)}, u32[]{:S(2)}) async-start(f32[32,1,2560]{2,1,0:T(1,128)} %broadcast_in_dim.34), calls=%async_computation.5 | async-start | bytes 655360 | tf_op jit(solution)/shard_map/all_to_all | solution.py:299
  94.4 8.3 %copy-start.2 = (f32[160,80]{1,0:T(8,128)S(1)}, f32[160,80]{1,0:T(8,128)}, u32[]{:S(2)}) copy-start(f32[160,80]{1,0:T(8,128)} %momentum.1) | copy-start | bytes 153604
  94.4 8.3 %collective-permute-start.1 = (f32[64,1,1280]{2,1,0:T(1,128)S(1)}, f32[64,1,1280]{2,1,0:T(1,128)S(1)}, u32[]{:S(2)}, u32[]{:S(2)}) collective-permute-start(f32[64,1,1280]{2,1,0:T(1,128)S(1)} %bitcast.14), channel_id=1, source_target_pairs={{0,16},{16,0},{1,17},{17,1},{2,18},{18,2},{3,19},{19,3},{4,20},{20... | collective-permute-start | bytes 983048 | tf_op jit(solution)/shard_map/ppermute | solution.py:328

commit v6 on v5

--- a/solution.py
+++ b/solution.py
@@ -52,56 +52,67 @@
     return sum(stack[i * rows : (i + 1) * rows] for i in reversed(range(count)))
 
 
-def left_kernel(place, deltas, errors, starts, out, partner, d_buf, e_buf, s_buf, sems):
-    width = d_buf.shape[1] // CHUNKS
-    copies = []
-    for j in range(CHUNKS):
-        cut = pl.ds(j * width, width)
-        three = (
-            pltpu.make_async_copy(starts.at[:, cut], s_buf.at[:, cut], sems.at[j, 0]),
-            pltpu.make_async_copy(deltas.at[0, :, cut], d_buf.at[:, cut], sems.at[j, 1]),
-            pltpu.make_async_copy(errors.at[0, :, cut], e_buf.at[:, cut], sems.at[j, 2]),
-        )
-        for copy in three:
-            copy.start()
-        copies.append(three)
-    total = None
-    for j in range(CHUNKS):
-        cut = slice(j * width, (j + 1) * width)
-        copies[j][0].wait()
-        stack = jnp.concatenate(pieces_of(s_buf[:, cut], 3), axis=0)
-        copies[j][1].wait()
-        part = dot(stack, d_buf[:, cut], ((1,), (1,)))
-        copies[j][2].wait()
-        part = part + dot(stack, e_buf[:, cut], ((1,), (1,)))
-        total = part if total is None else total + part
-    share = partner.shape[1]
-    cut = pl.ds(pl.multiple_of((1 - place[0] % 2) * share, 128), share)
-    partner[...] = d_buf[:, cut].astype(jnp.float32) + e_buf[:, cut].astype(jnp.float32)
-    out[...] = folded(total, 3).reshape(out.shape)
-
-
-def left_part_of(place, deltas, errors, starts):
+def packed(rows):
+    lanes = rows.shape[1] - 128
+    count = 128 // lanes
+    share = rows.shape[0] // count
+    tails = [rows[i * share : (i + 1) * share, 128:] for i in range(count)]
+    return rows[:, :128], jnp.concatenate(tails, axis=1)
+
+
+def unpacked(tiles, lanes):
+    count = 128 // lanes
+    share = tiles.shape[0] // (count + 1)
+    tails = tiles[count * share :]
+    tails = [tails[:, i * lanes : (i + 1) * lanes] for i in range(count)]
+    return jnp.concatenate([tiles[: count * share], jnp.concatenate(tails, axis=0)], axis=1)
+
+
+def left_kernel(deltas, errors, starts, out, d_buf, e_buf, s_buf, sems):
+    copies = [
+        pltpu.make_async_copy(starts, s_buf, sems.at[0]),
+        pltpu.make_async_copy(deltas, d_buf, sems.at[1]),
+        pltpu.make_async_copy(errors, e_buf, sems.at[2]),
+    ]
+    for copy in copies:
+        copy.start()
+    copies[0].wait()
+    stack = jnp.concatenate(pieces_of(s_buf[...], 3), axis=0)
+    copies[1].wait()
+    total = dot(stack, d_buf[0], ((1,), (1,)))
+    copies[2].wait()
+    total = folded(total + dot(stack, e_buf[0], ((1,), (1,))), 3)
+    rank, rows = total.shape
+    half = d_buf.shape[2] // 2
+    for p in range(2):
+        head, tail = packed(total[p * (rank // 2) : (p + 1) * (rank // 2)])
+        out[p, : rank // 2] = head
+        at = rank // 2 + tail.shape[0]
+        out[p, rank // 2 : at] = tail
+        for j in range(half // 128):
+            cut = slice(p * half + j * 128, p * half + (j + 1) * 128)
+            out[p, at + j * rows : at + (j + 1) * rows] = d_buf[0, :, cut].astype(jnp.float32) + e_buf[
+                0, :, cut
+            ].astype(jnp.float32)
+
+
+def left_part_of(deltas, errors, starts):
     rows, columns = deltas.shape[1:]
     rank = starts.shape[0]
-    count = lax.axis_size(PAIR)
+    size = rank // 2 * rows // 128 + columns // 2 // 128 * rows
     return pl.pallas_call(
         left_kernel,
         out_shape=(
-            held((count, rank // count, rows)),
-            held((rows, columns // 2)),
+            held((2, size, 128)),
+            pltpu.VMEM(deltas.shape, jnp.bfloat16),
+            pltpu.VMEM(errors.shape, jnp.bfloat16),
         ),
-        in_specs=[SMEM, HBM, HBM, HBM],
-        out_specs=(VMEM, VMEM),
-        scratch_shapes=[
-            pltpu.VMEM((rows, columns), jnp.bfloat16),
-            pltpu.VMEM((rows, columns), jnp.bfloat16),
-            held((rank, columns)),
-            pltpu.SemaphoreType.DMA((CHUNKS, 3)),
-        ],
+        in_specs=[HBM, HBM, HBM],
+        out_specs=(VMEM, VMEM, VMEM),
+        scratch_shapes=[held((rank, columns)), pltpu.SemaphoreType.DMA((3,))],
         compiler_params=SMALL,
         name="left_part",
-    )(place, far_off(deltas), far_off(errors), far_off(starts))
+    )(far_off(deltas), far_off(errors), far_off(starts))
 
 
 def gram_lines(left, first, count):
@@ -126,39 +137,39 @@
     return lines
 
 
-def right_kernel(place, left, partner, deltas, errors, out):
-    columns = partner.shape[1]
+def right_kernel(place, halves, merged, out, left):
+    rank, rows = left.shape
+    columns = out.shape[2] - 128
     chunks = CHUNKS // 2
     width = columns // chunks
-    rank = left.shape[0] * left.shape[1]
-    whole = left[...].reshape(rank, left.shape[2])
+    tiles = width // 128
+    skip = halves.shape[1]
+    whole = jnp.concatenate([unpacked(halves[c] + halves[2 + c], rows - 128) for c in range(2)], axis=0)
+    left[...] = whole
     stack = jnp.concatenate(pieces_of(whole, 3), axis=0)
-    base = place[0] % 2 * columns
     for j in range(chunks):
-        cut = slice(j * width, (j + 1) * width)
-        own = pl.ds(pl.multiple_of(base + j * width, 128), width)
-        merged = deltas[0, :, own].astype(jnp.float32) + errors[0, :, own].astype(jnp.float32)
-        pieces = pieces_of(merged + partner[:, cut], 3)
+        spans = [slice(skip + (j * tiles + t) * rows, skip + (j * tiles + t + 1) * rows) for t in range(tiles)]
+        both = jnp.concatenate([merged[0, span] + merged[1, span] for span in spans], axis=1)
         part = None
-        for piece in reversed(pieces):
+        for piece in reversed(pieces_of(both, 3)):
             term = dot(stack, piece, ((1,), (0,)))
             part = term if part is None else part + term
-        out[:, 0, cut] = folded(part, 3)
+        out[:, 0, j * width : (j + 1) * width] = folded(part, 3)
     lines = gram_lines(whole, place[0] // 2 * 4, 2)
     parity = lax.broadcasted_iota(jnp.int32, (rank, lines.shape[1]), 0) % 2
     out[:, 0, columns:] = jnp.where(parity == 0, lines[0:1], lines[1:2])
 
 
-def right_part_of(place, left, partner, deltas, errors):
-    rank = left.shape[0] * left.shape[1]
+def right_part_of(place, halves, merged, rank, rows):
+    columns = (merged.shape[1] - halves.shape[1]) * 128 // rows
     return pl.pallas_call(
         right_kernel,
-        out_shape=held((rank, 1, partner.shape[1] + 128)),
-        in_specs=[SMEM, VMEM, VMEM, VMEM, VMEM],
-        out_specs=VMEM,
+        out_shape=(held((rank, 1, columns + 128)), held((rank, rows))),
+        in_specs=[SMEM, VMEM, VMEM],
+        out_specs=(VMEM, VMEM),
         compiler_params=SMALL,
         name="right_part",
-    )(place, near_core(left), near_core(partner), near_core(deltas), near_core(errors))
+    )(place, near_core(halves), near_core(merged))
 
 
 def lower_inverse_of(gram):
@@ -184,7 +195,7 @@
 
 def factor_kernel(gram, left, out):
     rank = gram.shape[0]
-    whole = left[...].reshape(rank, left.shape[2])
+    whole = left[...]
     inverse = lower_inverse_of(gram[...])
     basis = lax.dot_general(
         inverse[:, :rank], whole, (((1,), (0,)), ((), ())), precision=highest, preferred_element_type=jnp.float32
@@ -198,7 +209,7 @@
 def factor_of(gram, left):
     return pl.pallas_call(
         factor_kernel,
-        out_shape=pltpu.VMEM((left.shape[2], 4 * gram.shape[0]), jnp.bfloat16),
+        out_shape=pltpu.VMEM((left.shape[1], 4 * gram.shape[0]), jnp.bfloat16),
         in_specs=[VMEM, VMEM],
         out_specs=VMEM,
         compiler_params=SMALL,
@@ -306,13 +317,12 @@
     rank = starts.shape[1]
     columns = deltas.shape[2]
     place = lax.axis_index(REP)[None]
-    left_part, other = left_part_of(place, deltas, errors, starts.T)
-    own = lax.all_to_all(left_part, PAIR, 0, 0, tiled=True).sum(axis=0)
-    partner = lax.ppermute(other, "core", SWAP)
-    own = to_each(own, "far").sum(axis=0) / replicas
-    own, partner = lax.optimization_barrier((own, partner))
-    tiles = to_each(own, PAIR)
-    load = right_part_of(place, tiles, partner, deltas, errors)
+    load, deltas, errors = left_part_of(deltas, errors, starts.T)
+    load, place = lax.optimization_barrier((load, place))
+    merged = lax.all_to_all(load, "core", 0, 0, tiled=True)
+    size = rank // 2 * deltas.shape[1] // 128
+    own = to_each(merged[:, :size].sum(axis=0), "far").sum(axis=0) / replicas
+    load, left = right_part_of(place, to_each(own, PAIR), merged, rank, deltas.shape[1])
     half = columns // 2
     nodes = lax.axis_size(NODES)
     load = load.reshape(nodes, rank // nodes, 1, -1)
@@ -323,7 +333,7 @@
     row = far[:, :, :columns].sum(axis=0) / replicas
     right = to_each(row, NODES).reshape(rank, 1, half)
     gram = far[:, 0, columns:].reshape(rank, rank)
-    flipped = factor_of(0.5 * (gram + gram.T), tiles)
+    flipped = factor_of(0.5 * (gram + gram.T), left)
     right, flipped = lax.optimization_barrier((right, flipped))
     other = lax.ppermute(right, "core", SWAP)
     ready = near_half_of(place, flipped, right, deltas, errors)

time: 105 us -> 103 us (0.981)
  starting transfers between devices: 19.8 us -> 10.7 us
  blocking collectives: 67.4 us -> 75.3 us
    ppermute x1 -> x0, starting transfers between devices: 8.88 us -> none  [body(): partner = lax.ppermute(other, 'core', SWAP)]
    all_to_all x1, blocking collectives: 5.63 us -> 11.5 us  [body(): merged = lax.all_to_all(load, 'core', 0, 0, tiled=True)]
    all_to_all x3, blocking collectives: 46.4 us -> 48.3 us  [to_each(): lax.all_to_all(jnp.broadcast_to(shard[None], (count, *shard.shape)), axes...]
  transfers between devices with their start and end apart: 3 -> 2, of which waited for: 1 -> 1; matrix products, arithmetic and copies ran while one was open for 0% -> 0% of each run, Pallas kernels for 4% -> 4%
where the time goes in v6:
time: 103 us
  blocking collectives  75.3 us (73%)
  starting transfers between devices  10.7 us (10%)
  Pallas kernels  9.93 us (10%)
  waiting for transfers between devices  4.75 us (5%)
  local copies, waits for them, and re-layouts  1.2 us (1%)
    all_to_all x3, blocking collectives, to_each(): lax.all_to_all(jnp.broadcast_to(shard[None], (count, *shard.shape)), axes...  48.3 us
    all_to_all x1, blocking collectives, body(): seen = lax.all_to_all(load, NODES, 0, 0, tiled=True)  15.4 us
    all_to_all x1, blocking collectives, body(): merged = lax.all_to_all(load, 'core', 0, 0, tiled=True)  11.5 us
    ppermute x1, starting transfers between devices, body(): other = lax.ppermute(right, 'core', SWAP)  6.7 us
    all_to_all x1, waiting for transfers between devices, to_each(): lax.all_to_all(jnp.broadcast_to(shard[None], (count, *shard.shape)), axes...  4.74 us
    all_to_all x1, starting transfers between devices, to_each(): lax.all_to_all(jnp.broadcast_to(shard[None], (count, *shard.shape)), axes...  4.01 us
    pallas_call x1, Pallas kernels, factor_of(): pl.pallas_call(factor_kernel, out_shape=pltpu.VMEM((left.shape[1], 4 * gr...  3.3 us
    pallas_call x1, Pallas kernels, left_part_of(): pl.pallas_call(left_kernel, out_shape=(held((2, size, 128)), pltpu.VMEM(d...  2.54 us
  transfers between devices with their start and end apart: 2, of which 1 were waited for; matrix products, arithmetic and copies ran while one was open for 0% of the time, Pallas kernels for 4%

profile of v6, /device:TPU:1, one launch (start us, length us, event | category | flops | bytes accessed | tf_op | source)
XLA Modules:
  0.0 102.9 jit_solution(3129202766947337230)
XLA Ops:
  0.6 2.5 %left_part.1 = (f32[2,1640,128]{2,1,0:T(8,128)S(1)}, bf16[1,160,2560]{2,1,0:T(8,128)(2,1)S(1)}, bf16[1,160,2560]{2,1,0:T(8,128)(2,1)S(1)}) custom-call(bf16[1,160,2560]{2,1,0:T(8,128)(2,1)} %deltas.1, bf16[1,160,2560]{2,1,0:T(8,128)(2,1)} %errors.1, f32[64,2560]{1,0:T(8,128)} %bitcast.18), custom_call_target="tpu_custom_call" | custom-call | tf_op jit(solution)/shard_map/left_part/pallas_call | solution.py:103
  3.2 11.5 %all_to_all.30.merged = f32[2,1640,128]{2,1,0:T(8,128)S(1)} all-to-all(f32[2,1640,128]{2,1,0:T(8,128)S(1)} %get-tuple-element.14), channel_id=1, replica_groups=mesh['far'=8,'near'=2,'core'=2,'mdl'=16] {'core'}, dimensions={0} | all-to-all | bytes 3358720 | tf_op jit(solution)/shard_map/all_to_all | solution.py:322
  14.7 24.1 %all_to_all.31 = f32[8,40,128]{2,1,0:T(8,128)S(1)} all-to-all(f32[8,40,128]{2,1,0:T(8,128)S(1)} %broadcast_in_dim.13), channel_id=1, replica_groups=mesh['far'=8,'near'=2,'core'=2,'mdl'=16] {'far'}, dimensions={0} | all-to-all | bytes 327680 | tf_op jit(solution)/shard_map/all_to_all | solution.py:310
  38.9 9.1 %all_to_all.32.halves = f32[4,40,128]{2,1,0:T(8,128)S(1)} all-to-all(f32[4,40,128]{2,1,0:T(8,128)S(1)} %broadcast_in_dim.14), channel_id=1, replica_groups=mesh['far'=8,'near'=2,'core'=2,'mdl'=16] {'near','core'}, dimensions={0} | all-to-all | bytes 163840 | tf_op jit(solution)/shard_map/all_to_all | solution.py:310
  48.0 0.8 right_part.1
  48.8 15.4 %all_to_all.33 = f32[32,2,1,1408]{3,2,1,0:T(1,128)S(1)} all-to-all(f32[32,2,1,1408]{3,2,1,0:T(1,128)S(1)} %bitcast.17), channel_id=1, replica_groups=mesh['far'=8,'near'=2,'core'=2,'mdl'=16] {'near','mdl'}, dimensions={0} | all-to-all | bytes 720896 | tf_op jit(solution)/shard_map/all_to_all | solution.py:329
  64.3 0.1 slice_reduce_fusion
  64.5 0.1 broadcast_in_dim.16
  64.5 15.1 %all_to_all.34 = f32[8,1,3072]{2,1,0:T(1,128)S(1)} all-to-all(f32[8,1,3072]{2,1,0:T(1,128)S(1)} %broadcast_in_dim.16), channel_id=1, replica_groups=mesh['far'=8,'near'=2,'core'=2,'mdl'=16] {'far'}, dimensions={0} | all-to-all | bytes 196608 | tf_op jit(solution)/shard_map/all_to_all | solution.py:310
  79.7 0.1 slice_reduce_fusion.1
  79.7 0.9 broadcast_in_dim.34
  80.6 0.0 copy-start
  80.6 4.0 %all-to-all-start.5 = ((f32[32,1,2560]{2,1,0:T(1,128)}), f32[32,1,2560]{2,1,0:T(1,128)S(1)}, u32[]{:S(2)}, u32[]{:S(2)}) async-start(f32[32,1,2560]{2,1,0:T(1,128)} %broadcast_in_dim.34), calls=%async_computation.5 | async-start | bytes 655360 | tf_op jit(solution)/shard_map/all_to_all | solution.py:310
  84.7 0.1 reshape_squeeze.3
  84.8 0.1 copy.10
  84.9 3.3 %factor.1.flipped = bf16[160,256]{1,0:T(8,128)(2,1)S(1)} custom-call(f32[64,64]{1,0:T(8,128)S(1)} %fusion.gram, f32[64,160]{1,0:T(8,128)S(1)} %get-tuple-element.16.left), custom_call_target="tpu_custom_call" | custom-call | flops 40000000 | bytes 200000 | tf_op jit(solution)/shard_map/factor/pallas_call | solution.py:210
  88.2 4.7 %all-to-all-done.5 = f32[32,1,2560]{2,1,0:T(1,128)S(1)} async-done(((f32[32,1,2560]{2,1,0:T(1,128)}), f32[32,1,2560]{2,1,0:T(1,128)S(1)}, u32[]{:S(2)}, u32[]{:S(2)}) %all-to-all-start.5) | async-done | bytes 327712 | tf_op jit(solution)/shard_map/all_to_all | solution.py:310
  92.9 6.7 %collective-permute-start = (f32[64,1,1280]{2,1,0:T(1,128)S(1)}, f32[64,1,1280]{2,1,0:T(1,128)S(1)}, u32[]{:S(2)}, u32[]{:S(2)}) collective-permute-start(f32[64,1,1280]{2,1,0:T(1,128)S(1)} %bitcast.14), channel_id=1, source_target_pairs={{0,16},{16,0},{1,17},{17,1},{2,18},{18,2},{3,19},{19,3},{4,20},{20... | collective-permute-start | bytes 983048 | tf_op jit(solution)/shard_map/ppermute | solution.py:338
  99.6 1.2 %near_half.1.ready = bf16[160,1280]{1,0:T(8,128)(2,1)S(1)} custom-call(s32[1]{0:T(128)} %bitcast.1.place, bf16[160,256]{1,0:T(8,128)(2,1)S(1)} %factor.1.flipped, f32[64,1,1280]{2,1,0:T(1,128)S(1)} %bitcast.15, bf16[1,160,2560]{2,1,0:T(8,128)(2,1)S(1)} %get-tuple-element.19.deltas, bf16[1,160,2560]{2,1,0:T(8,128)(2,1)S(1)} %get-tuple-element.20.errors), custom_call_target="tpu_custom_call" | custom-call | flops 40000000 | bytes 2000000 | tf_op jit(solution)/shard_map/near_half/pallas_call | solution.py:242
  100.8 0.0 collective-permute-done.other
  100.8 0.0 copy-done
  100.9 2.0 %outputs.1 = (bf16[1,160,2560]{2,1,0:T(8,128)(2,1)}, f32[160,80]{1,0:T(8,128)}, f32[160,80]{1,0:T(8,128)}) custom-call(s32[1]{0:T(128)} %bitcast.1.place, bf16[160,256]{1,0:T(8,128)(2,1)S(1)} %factor.1.flipped, f32[64,1,1280]{2,1,0:T(1,128)S(1)} %bitcast.16, f32[64,1,1280]{2,1,0:T(1,128)S(1)} %collective-permute-done.other, ...), custom_call_target="tpu_custom_call" | custom-call | tf_op jit(solution)/shard_map/outputs/pallas_call | solution.py:288
  (12 shorter events, 0.2 us)
Async XLA Ops:
  80.6 20.2 %copy-start = (f32[160,80]{1,0:T(8,128)S(1)}, f32[160,80]{1,0:T(8,128)}, u32[]{:S(2)}) copy-start(f32[160,80]{1,0:T(8,128)} %momentum.1) | copy-start | bytes 153604
  80.6 12.3 %all-to-all-start.5 = ((f32[32,1,2560]{2,1,0:T(1,128)}), f32[32,1,2560]{2,1,0:T(1,128)S(1)}, u32[]{:S(2)}, u32[]{:S(2)}) async-start(f32[32,1,2560]{2,1,0:T(1,128)} %broadcast_in_dim.34), calls=%async_computation.5 | async-start | bytes 655360 | tf_op jit(solution)/shard_map/all_to_all | solution.py:310
  92.9 7.9 %collective-permute-start = (f32[64,1,1280]{2,1,0:T(1,128)S(1)}, f32[64,1,1280]{2,1,0:T(1,128)S(1)}, u32[]{:S(2)}, u32[]{:S(2)}) collective-permute-start(f32[64,1,1280]{2,1,0:T(1,128)S(1)} %bitcast.14), channel_id=1, source_target_pairs={{0,16},{16,0},{1,17},{17,1},{2,18},{18,2},{3,19},{19,3},{4,20},{20... | collective-permute-start | bytes 983048 | tf_op jit(solution)/shard_map/ppermute | solution.py:338

commit v7 on v6

--- a/solution.py
+++ b/solution.py
@@ -116,55 +116,44 @@
 
 
 def gram_lines(left, first, count):
-    rank = left.shape[0]
-    share = 128 // rank
     index = lax.broadcasted_iota(jnp.int32, left.shape, 0)
-    nothing = jnp.zeros_like(left)
-    lines = None
-    for i in range(share):
-        own = jnp.concatenate(
-            [
-                jnp.sum(jnp.where(index == first + share * n + i, left, nothing), axis=0, keepdims=True)
-                for n in range(count)
-            ],
-            axis=0,
-        )
-        lanes = jnp.concatenate([nothing] * i + [left] + [nothing] * (share - 1 - i), axis=0)
-        part = lax.dot_general(
-            own, lanes, (((1,), (1,)), ((), ())), precision=highest, preferred_element_type=jnp.float32
-        )
-        lines = part if lines is None else lines + part
-    return lines
+    own = [jnp.sum(jnp.where(index == first + i, left, 0.0), axis=0, keepdims=True) for i in range(count)]
+    return lax.dot_general(
+        jnp.concatenate(own, axis=0), left, (((1,), (1,)), ((), ())), precision=highest, preferred_element_type=jnp.float32
+    )
 
 
 def right_kernel(place, halves, merged, out, left):
     rank, rows = left.shape
-    columns = out.shape[2] - 128
-    chunks = CHUNKS // 2
-    width = columns // chunks
+    share = out.shape[1]
+    groups = rank // share
+    width = out.shape[2] - rank
     tiles = width // 128
     skip = halves.shape[1]
     whole = jnp.concatenate([unpacked(halves[c] + halves[2 + c], rows - 128) for c in range(2)], axis=0)
     left[...] = whole
     stack = jnp.concatenate(pieces_of(whole, 3), axis=0)
-    for j in range(chunks):
+    for j in range(out.shape[0] // groups):
         spans = [slice(skip + (j * tiles + t) * rows, skip + (j * tiles + t + 1) * rows) for t in range(tiles)]
         both = jnp.concatenate([merged[0, span] + merged[1, span] for span in spans], axis=1)
         part = None
         for piece in reversed(pieces_of(both, 3)):
             term = dot(stack, piece, ((1,), (0,)))
             part = term if part is None else part + term
-        out[:, 0, j * width : (j + 1) * width] = folded(part, 3)
-    lines = gram_lines(whole, place[0] // 2 * 4, 2)
-    parity = lax.broadcasted_iota(jnp.int32, (rank, lines.shape[1]), 0) % 2
-    out[:, 0, columns:] = jnp.where(parity == 0, lines[0:1], lines[1:2])
+        part = folded(part, 3)
+        for g in range(groups):
+            out[j * groups + g, :, :width] = part[g * share : (g + 1) * share]
+    lines = gram_lines(whole, place[0] // 2 * share, share)
+    for p in range(out.shape[0]):
+        out[p, :, width:] = lines
 
 
 def right_part_of(place, halves, merged, rank, rows):
-    columns = (merged.shape[1] - halves.shape[1]) * 128 // rows
+    width = (merged.shape[1] - halves.shape[1]) * 128 // rows // 2
+    share = rank * 2 // lax.axis_size(NODES)
     return pl.pallas_call(
         right_kernel,
-        out_shape=(held((rank, 1, columns + 128)), held((rank, rows))),
+        out_shape=(held((rank * 2 // share, share, width + rank)), held((rank, rows))),
         in_specs=[SMEM, VMEM, VMEM],
         out_specs=(VMEM, VMEM),
         compiler_params=SMALL,
@@ -223,62 +212,75 @@
     return dot(flipped, jnp.concatenate([big, small, big, small], axis=0), ((1,), (0,)))
 
 
-def residue(flipped, right, deltas, errors, base, j, width):
-    approx = product(flipped[...], right[:, 0, j * width : (j + 1) * width])
+def flatten(right, flat):
+    share, width = right.shape[1:]
+    groups = flat.shape[0] // share
+    for j in range(right.shape[0] // groups):
+        for g in range(groups):
+            flat[g * share : (g + 1) * share, j * width : (j + 1) * width] = right[j * groups + g]
+
+
+def residue(flipped, flat, deltas, errors, base, j, width):
+    approx = product(flipped[...], flat[:, j * width : (j + 1) * width])
     cut = pl.ds(pl.multiple_of(base + j * width, 128), width)
     merged = deltas[0, :, cut].astype(jnp.float32) + errors[0, :, cut].astype(jnp.float32)
     return (merged - approx).astype(jnp.bfloat16)
 
 
-def near_kernel(place, flipped, right, deltas, errors, out):
-    half = right.shape[2]
+def near_kernel(place, flipped, right, deltas, errors, out, flat):
+    flatten(right, flat)
+    half = flat.shape[1]
     width = half // (CHUNKS // 2)
     base = place[0] % 2 * half
     for j in range(CHUNKS // 2):
-        out[:, j * width : (j + 1) * width] = residue(flipped, right, deltas, errors, base, j, width)
+        out[:, j * width : (j + 1) * width] = residue(flipped, flat, deltas, errors, base, j, width)
 
 
 def near_half_of(place, flipped, right, deltas, errors):
+    rows, columns = deltas.shape[1:]
+    rank = right.size * 2 // columns
     return pl.pallas_call(
         near_kernel,
-        out_shape=pltpu.VMEM((deltas.shape[1], right.shape[2]), jnp.bfloat16),
+        out_shape=(pltpu.VMEM((rows, columns // 2), jnp.bfloat16), held((rank, columns // 2))),
         in_specs=[SMEM, VMEM, VMEM, VMEM, VMEM],
-        out_specs=VMEM,
+        out_specs=(VMEM, VMEM),
         compiler_params=SMALL,
         cost_estimate=pl.CostEstimate(flops=40_000_000, transcendentals=0, bytes_accessed=2_000_000),
         name="near_half",
     )(place, near_core(flipped), near_core(right), near_core(deltas), near_core(errors))
 
 
-def out_kernel(place, flipped, right, other, ready, deltas, errors, momentum, new_errors, new_momentum, outer_step, buf, fresh, step, sems):
-    half = right.shape[2]
+def out_kernel(place, flipped, right, other, ready, deltas, errors, momentum, new_errors, new_momentum, outer_step, flat, buf, fresh, step, sems):
+    half = right.shape[1]
     owned = momentum.shape[1]
     each = half // owned
     core = place[0] % 2
     own = pl.ds(pl.multiple_of(core * half, 128), half)
     copies = [pltpu.make_async_copy(ready, new_errors.at[0, :, own], sems.at[0])]
     copies[0].start()
-    first = place[0] % each * owned
-    base = pl.multiple_of(jnp.minimum(first // 128, half // 128 - 2) * 128, 128)
-    cut = pl.ds(base, 256)
-    window = jnp.where(place[0] // each == core, right[:, 0, cut], other[:, 0, cut])
-    window = pltpu.roll(window, lax.rem(256 - (first - base), 256), 1)[:, :128]
-    mine = product(flipped[...], window)[:, :owned]
-    fresh[...] = 0.9 * momentum[...] + mine
-    step[...] = 0.7 * (mine + 0.9 * fresh[...])
-    copies.append(pltpu.make_async_copy(fresh, new_momentum, sems.at[1]))
-    copies.append(pltpu.make_async_copy(step, outer_step, sems.at[2]))
-    for copy in copies[1:]:
-        copy.start()
+    flatten(other, flat)
     width = half // (CHUNKS // 2)
-    base = (1 - core) * half
+    far = (1 - core) * half
     for j in range(CHUNKS // 2):
         cut = slice(j * width, (j + 1) * width)
-        buf[:, cut] = residue(flipped, other, deltas, errors, base, j, width)
-        there = pl.ds(pl.multiple_of(base + j * width, 128), width)
+        buf[:, cut] = residue(flipped, flat, deltas, errors, far, j, width)
+        there = pl.ds(pl.multiple_of(far + j * width, 128), width)
         copy = pltpu.make_async_copy(buf.at[:, pl.ds(j * width, width)], new_errors.at[0, :, there], sems.at[3 + j])
         copy.start()
         copies.append(copy)
+        if j == 0:
+            first = place[0] % each * owned
+            base = pl.multiple_of(jnp.minimum(first // 128, half // 128 - 2) * 128, 128)
+            cut = pl.ds(base, 256)
+            window = jnp.where(place[0] // each == core, right[:, cut], flat[:, cut])
+            window = pltpu.roll(window, lax.rem(256 - (first - base), 256), 1)[:, :128]
+            mine = product(flipped[...], window)[:, :owned]
+            fresh[...] = 0.9 * momentum[...] + mine
+            step[...] = 0.7 * (mine + 0.9 * fresh[...])
+            for k, (source, target) in enumerate(((fresh, new_momentum), (step, outer_step))):
+                copy = pltpu.make_async_copy(source, target, sems.at[1 + k])
+                copy.start()
+                copies.append(copy)
     for copy in copies:
         copy.wait()
 
@@ -295,6 +297,7 @@
         in_specs=[SMEM] + [VMEM] * 7,
         out_specs=(HBM, HBM, HBM),
         scratch_shapes=[
+            held(right.shape),
             pltpu.VMEM(ready.shape, jnp.bfloat16),
             held(momentum.shape),
             held(momentum.shape),
@@ -315,7 +318,6 @@
 def body(deltas, errors, starts, momentum):
     replicas = lax.axis_size(REP)
     rank = starts.shape[1]
-    columns = deltas.shape[2]
     place = lax.axis_index(REP)[None]
     load, deltas, errors = left_part_of(deltas, errors, starts.T)
     load, place = lax.optimization_barrier((load, place))
@@ -323,21 +325,19 @@
     size = rank // 2 * deltas.shape[1] // 128
     own = to_each(merged[:, :size].sum(axis=0), "far").sum(axis=0) / replicas
     load, left = right_part_of(place, to_each(own, PAIR), merged, rank, deltas.shape[1])
-    half = columns // 2
     nodes = lax.axis_size(NODES)
-    load = load.reshape(nodes, rank // nodes, 1, -1)
+    width = load.shape[2] - rank
     seen = lax.all_to_all(load, NODES, 0, 0, tiled=True)
-    row = seen[..., :half].sum(axis=0)
-    lines = seen[..., half:].reshape(lax.axis_size("near"), -1, rank // nodes, 128).sum(axis=1)
-    far = to_each(jnp.concatenate([row.reshape(1, -1), lines.reshape(1, -1)], axis=1), "far")
-    row = far[:, :, :columns].sum(axis=0) / replicas
-    right = to_each(row, NODES).reshape(rank, 1, half)
-    gram = far[:, 0, columns:].reshape(rank, rank)
+    lines = seen[:, :, width:].reshape(lax.axis_size("near"), -1, *seen.shape[1:2], rank).sum(axis=1)
+    far = to_each(jnp.concatenate([seen[:, :, :width].sum(axis=0), *lines], axis=1), "far")
+    part = far[:, :, :width].sum(axis=0) / replicas
+    right = to_each(part, NODES).reshape(nodes, -1, width)
+    gram = jnp.moveaxis(far[:, :, width:].reshape(*far.shape[:2], -1, rank), 2, 1).reshape(rank, rank)
     flipped = factor_of(0.5 * (gram + gram.T), left)
     right, flipped = lax.optimization_barrier((right, flipped))
     other = lax.ppermute(right, "core", SWAP)
-    ready = near_half_of(place, flipped, right, deltas, errors)
-    return outputs_of(place, flipped, right, other, ready, deltas, errors, momentum)
+    ready, flat = near_half_of(place, flipped, right, deltas, errors)
+    return outputs_of(place, flipped, flat, other, ready, deltas, errors, momentum)
 
 
 def solution(mesh):

time: 103 us -> 103 us (level)
  Pallas kernels: 9.93 us -> 8.12 us
  transfers between devices with their start and end apart: 2 -> 2, of which waited for: 1 -> 2; matrix products, arithmetic and copies ran while one was open for 0% -> 0% of each run, Pallas kernels for 4% -> 4%
where the time goes in v7:
time: 103 us; the launch traced here: 102 us
  blocking collectives  75.6 us (73%)
  starting transfers between devices  11 us (11%)
  Pallas kernels  8.12 us (8%)
  waiting for transfers between devices  5.53 us (5%)
    all_to_all x3, blocking collectives, to_each(): lax.all_to_all(jnp.broadcast_to(shard[None], (count, *shard.shape)), axes...  48.6 us
    all_to_all x1, blocking collectives, body(): seen = lax.all_to_all(load, NODES, 0, 0, tiled=True)  15.5 us
    all_to_all x1, blocking collectives, body(): merged = lax.all_to_all(load, 'core', 0, 0, tiled=True)  11.5 us
    ppermute x1, starting transfers between devices, body(): other = lax.ppermute(right, 'core', SWAP)  7.02 us
    all_to_all x1, waiting for transfers between devices, to_each(): lax.all_to_all(jnp.broadcast_to(shard[None], (count, *shard.shape)), axes...  4.63 us
    all_to_all x1, starting transfers between devices, to_each(): lax.all_to_all(jnp.broadcast_to(shard[None], (count, *shard.shape)), axes...  4.01 us
    pallas_call x1, Pallas kernels, factor_of(): pl.pallas_call(factor_kernel, out_shape=pltpu.VMEM((left.shape[1], 4 * gr...  3.3 us
    pallas_call x1, Pallas kernels, left_part_of(): pl.pallas_call(left_kernel, out_shape=(held((2, size, 128)), pltpu.VMEM(d...  2.54 us
  transfers between devices with their start and end apart: 2, of which 2 were waited for; matrix products, arithmetic and copies ran while one was open for 0% of the time, Pallas kernels for 4%

profile of v7, /device:TPU:1, one launch (start us, length us, event | category | flops | bytes accessed | tf_op | source)
XLA Modules:
  0.0 102.3 jit_solution(13902300927681751275)
XLA Ops:
  0.6 2.5 %left_part.1 = (f32[2,1640,128]{2,1,0:T(8,128)S(1)}, bf16[1,160,2560]{2,1,0:T(8,128)(2,1)S(1)}, bf16[1,160,2560]{2,1,0:T(8,128)(2,1)S(1)}) custom-call(bf16[1,160,2560]{2,1,0:T(8,128)(2,1)} %deltas.1, bf16[1,160,2560]{2,1,0:T(8,128)(2,1)} %errors.1, f32[64,2560]{1,0:T(8,128)} %bitcast.16), custom_call_target="tpu_custom_call" | custom-call | tf_op jit(solution)/shard_map/left_part/pallas_call | solution.py:103
  3.2 11.5 %all_to_all.30.merged = f32[2,1640,128]{2,1,0:T(8,128)S(1)} all-to-all(f32[2,1640,128]{2,1,0:T(8,128)S(1)} %get-tuple-element.16), channel_id=1, replica_groups=mesh['far'=8,'near'=2,'core'=2,'mdl'=16] {'core'}, dimensions={0} | all-to-all | bytes 3358720 | tf_op jit(solution)/shard_map/all_to_all | solution.py:324
  14.7 24.1 %all_to_all.31 = f32[8,40,128]{2,1,0:T(8,128)S(1)} all-to-all(f32[8,40,128]{2,1,0:T(8,128)S(1)} %broadcast_in_dim.11), channel_id=1, replica_groups=mesh['far'=8,'near'=2,'core'=2,'mdl'=16] {'far'}, dimensions={0} | all-to-all | bytes 327680 | tf_op jit(solution)/shard_map/all_to_all | solution.py:313
  38.9 9.1 %all_to_all.32.halves = f32[4,40,128]{2,1,0:T(8,128)S(1)} all-to-all(f32[4,40,128]{2,1,0:T(8,128)S(1)} %broadcast_in_dim.12), channel_id=1, replica_groups=mesh['far'=8,'near'=2,'core'=2,'mdl'=16] {'near','core'}, dimensions={0} | all-to-all | bytes 163840 | tf_op jit(solution)/shard_map/all_to_all | solution.py:313
  48.0 0.7 right_part.1
  48.7 15.5 %all_to_all.33 = f32[32,4,704]{2,1,0:T(4,128)S(1)} all-to-all(f32[32,4,704]{2,1,0:T(4,128)S(1)} %get-tuple-element.17), channel_id=1, replica_groups=mesh['far'=8,'near'=2,'core'=2,'mdl'=16] {'near','mdl'}, dimensions={0} | all-to-all | bytes 720896 | tf_op jit(solution)/shard_map/all_to_all | solution.py:330
  64.2 0.1 slice_reduce_fusion
  64.3 0.1 pad_maximum_fusion
  64.3 15.5 %all_to_all.34 = f32[8,4,768]{2,1,0:T(4,128)S(1)} all-to-all(f32[8,4,768]{2,1,0:T(4,128)S(1)} %broadcast_in_dim.13), channel_id=1, replica_groups=mesh['far'=8,'near'=2,'core'=2,'mdl'=16] {'far'}, dimensions={0} | all-to-all | bytes 196608 | tf_op jit(solution)/shard_map/all_to_all | solution.py:313
  79.8 0.8 broadcast_in_dim.14
  80.6 0.0 copy-start
  80.6 4.0 %all-to-all-start.5 = ((f32[32,4,640]{2,1,0:T(4,128)}), f32[32,4,640]{2,1,0:T(4,128)S(1)}, u32[]{:S(2)}, u32[]{:S(2)}) async-start(f32[32,4,640]{2,1,0:T(4,128)} %broadcast_in_dim.14), calls=%async_computation.5 | async-start | bytes 655360 | tf_op jit(solution)/shard_map/all_to_all | solution.py:313
  84.7 0.1 reshape.24
  84.8 0.1 copy.15
  84.9 3.3 %factor.1.flipped = bf16[160,256]{1,0:T(8,128)(2,1)S(1)} custom-call(f32[64,64]{1,0:T(8,128)S(1)} %fusion.gram, f32[64,160]{1,0:T(8,128)S(1)} %get-tuple-element.18.left), custom_call_target="tpu_custom_call" | custom-call | flops 40000000 | bytes 200000 | tf_op jit(solution)/shard_map/factor/pallas_call | solution.py:199
  88.2 4.6 %all-to-all-done.5.right = f32[32,4,640]{2,1,0:T(4,128)S(1)} async-done(((f32[32,4,640]{2,1,0:T(4,128)}), f32[32,4,640]{2,1,0:T(4,128)S(1)}, u32[]{:S(2)}, u32[]{:S(2)}) %all-to-all-start.5) | async-done | bytes 327712 | tf_op jit(solution)/shard_map/all_to_all | solution.py:313
  92.8 7.0 %collective-permute-start = (f32[32,4,640]{2,1,0:T(4,128)S(1)}, f32[32,4,640]{2,1,0:T(4,128)S(1)}, u32[]{:S(2)}, u32[]{:S(2)}) collective-permute-start(f32[32,4,640]{2,1,0:T(4,128)S(1)} %all-to-all-done.5.right), channel_id=1, source_target_pairs={{0,16},{16,0},{1,17},{17,1},{2,18},{18,2},{3,19},{19,3},{4,20},{20... | collective-permute-start | bytes 983048 | tf_op jit(solution)/shard_map/ppermute | solution.py:338
  99.8 0.3 near_half.1
  100.2 0.9 collective-permute-done.other
  101.1 0.0 copy-done
  101.1 1.2 %outputs.1 = (bf16[1,160,2560]{2,1,0:T(8,128)(2,1)}, f32[160,80]{1,0:T(8,128)}, f32[160,80]{1,0:T(8,128)}) custom-call(s32[1]{0:T(128)} %bitcast.1.place, bf16[160,256]{1,0:T(8,128)(2,1)S(1)} %factor.1.flipped, f32[64,1280]{1,0:T(8,128)S(1)} %get-tuple-element.23.right, f32[32,4,640]{2,1,0:T(4,128)S(1)} %collective-permute-done.other, ...), custom_call_target="tpu_custom_call" | custom-call | tf_op jit(solution)/shard_map/outputs/pallas_call | solution.py:290
  (14 shorter events, 0.2 us)
Async XLA Ops:
  80.6 20.5 %copy-start = (f32[160,80]{1,0:T(8,128)S(1)}, f32[160,80]{1,0:T(8,128)}, u32[]{:S(2)}) copy-start(f32[160,80]{1,0:T(8,128)} %momentum.1) | copy-start | bytes 153604
  80.6 12.2 %all-to-all-start.5 = ((f32[32,4,640]{2,1,0:T(4,128)}), f32[32,4,640]{2,1,0:T(4,128)S(1)}, u32[]{:S(2)}, u32[]{:S(2)}) async-start(f32[32,4,640]{2,1,0:T(4,128)} %broadcast_in_dim.14), calls=%async_computation.5 | async-start | bytes 655360 | tf_op jit(solution)/shard_map/all_to_all | solution.py:313
  92.8 8.3 %collective-permute-start = (f32[32,4,640]{2,1,0:T(4,128)S(1)}, f32[32,4,640]{2,1,0:T(4,128)S(1)}, u32[]{:S(2)}, u32[]{:S(2)}) collective-permute-start(f32[32,4,640]{2,1,0:T(4,128)S(1)} %all-to-all-done.5.right), channel_id=1, source_target_pairs={{0,16},{16,0},{1,17},{17,1},{2,18},{18,2},{3,19},{19,3},{4,20},{20... | collective-permute-start | bytes 983048 | tf_op jit(solution)/shard_map/ppermute | solution.py:338

commit v8 on v7

--- a/solution.py
+++ b/solution.py
@@ -11,7 +11,7 @@
 NODES = ("near", "mdl")
 SWAP = [(0, 1), (1, 0)]
 CHUNKS = 4
-BLOCK = 4
+BLOCK = 16
 
 
 highest = lax.Precision.HIGHEST
@@ -115,15 +115,7 @@
     )(far_off(deltas), far_off(errors), far_off(starts))
 
 
-def gram_lines(left, first, count):
-    index = lax.broadcasted_iota(jnp.int32, left.shape, 0)
-    own = [jnp.sum(jnp.where(index == first + i, left, 0.0), axis=0, keepdims=True) for i in range(count)]
-    return lax.dot_general(
-        jnp.concatenate(own, axis=0), left, (((1,), (1,)), ((), ())), precision=highest, preferred_element_type=jnp.float32
-    )
-
-
-def right_kernel(place, halves, merged, out, left):
+def right_kernel(halves, merged, out, left):
     rank, rows = left.shape
     share = out.shape[1]
     groups = rank // share
@@ -143,22 +135,26 @@
         part = folded(part, 3)
         for g in range(groups):
             out[j * groups + g, :, :width] = part[g * share : (g + 1) * share]
-    lines = gram_lines(whole, place[0] // 2 * share, share)
+    gram = lax.dot_general(
+        whole, whole, (((1,), (1,)), ((), ())), precision=highest, preferred_element_type=jnp.float32
+    )
+    lines = rank // out.shape[0]
     for p in range(out.shape[0]):
-        out[p, :, width:] = lines
-
-
-def right_part_of(place, halves, merged, rank, rows):
+        out[p, :lines, width:] = gram[p * lines : (p + 1) * lines]
+        out[p, lines:, width:] = jnp.zeros((share - lines, rank), jnp.float32)
+
+
+def right_part_of(halves, merged, rank, rows):
     width = (merged.shape[1] - halves.shape[1]) * 128 // rows // 2
     share = rank * 2 // lax.axis_size(NODES)
     return pl.pallas_call(
         right_kernel,
         out_shape=(held((rank * 2 // share, share, width + rank)), held((rank, rows))),
-        in_specs=[SMEM, VMEM, VMEM],
+        in_specs=[VMEM, VMEM],
         out_specs=(VMEM, VMEM),
         compiler_params=SMALL,
         name="right_part",
-    )(place, near_core(halves), near_core(merged))
+    )(near_core(halves), near_core(merged))
 
 
 def lower_inverse_of(gram):
@@ -182,12 +178,16 @@
     return jnp.where(lane < rank, pltpu.roll(table, rank, 1), table)
 
 
-def factor_kernel(gram, left, out):
-    rank = gram.shape[0]
-    whole = left[...]
-    inverse = lower_inverse_of(gram[...])
+def factor_kernel(right, left, out, gram):
+    rank = left.shape[0]
+    width = right.shape[2] - rank
+    lines = rank // right.shape[0]
+    for p in range(right.shape[0]):
+        gram[p * lines : (p + 1) * lines] = right[p, :lines, width:]
+    table = gram[...]
+    inverse = lower_inverse_of(0.5 * (table + table.T))
     basis = lax.dot_general(
-        inverse[:, :rank], whole, (((1,), (0,)), ((), ())), precision=highest, preferred_element_type=jnp.float32
+        inverse[:, :rank], left[...], (((1,), (0,)), ((), ())), precision=highest, preferred_element_type=jnp.float32
     )
     twice = lax.dot_general(
         basis, inverse, (((0,), (0,)), ((), ())), precision=highest, preferred_element_type=jnp.float32
@@ -195,16 +195,18 @@
     out[...] = jnp.concatenate(pieces_of(twice, 2), axis=1)
 
 
-def factor_of(gram, left):
+def factor_of(right, left):
+    rank, rows = left.shape
     return pl.pallas_call(
         factor_kernel,
-        out_shape=pltpu.VMEM((left.shape[1], 4 * gram.shape[0]), jnp.bfloat16),
+        out_shape=pltpu.VMEM((rows, 4 * rank), jnp.bfloat16),
         in_specs=[VMEM, VMEM],
         out_specs=VMEM,
+        scratch_shapes=[held((rank, rank))],
         compiler_params=SMALL,
         cost_estimate=pl.CostEstimate(flops=40_000_000, transcendentals=0, bytes_accessed=200_000),
         name="factor",
-    )(near_core(gram), near_core(left))
+    )(near_core(right), near_core(left))
 
 
 def product(flipped, right):
@@ -213,11 +215,13 @@
 
 
 def flatten(right, flat):
-    share, width = right.shape[1:]
+    share = right.shape[1]
     groups = flat.shape[0] // share
-    for j in range(right.shape[0] // groups):
+    blocks = right.shape[0] // groups
+    width = flat.shape[1] // blocks
+    for j in range(blocks):
         for g in range(groups):
-            flat[g * share : (g + 1) * share, j * width : (j + 1) * width] = right[j * groups + g]
+            flat[g * share : (g + 1) * share, j * width : (j + 1) * width] = right[j * groups + g, :, :width]
 
 
 def residue(flipped, flat, deltas, errors, base, j, width):
@@ -238,7 +242,7 @@
 
 def near_half_of(place, flipped, right, deltas, errors):
     rows, columns = deltas.shape[1:]
-    rank = right.size * 2 // columns
+    rank = flipped.shape[1] // 4
     return pl.pallas_call(
         near_kernel,
         out_shape=(pltpu.VMEM((rows, columns // 2), jnp.bfloat16), held((rank, columns // 2))),
@@ -324,17 +328,14 @@
     merged = lax.all_to_all(load, "core", 0, 0, tiled=True)
     size = rank // 2 * deltas.shape[1] // 128
     own = to_each(merged[:, :size].sum(axis=0), "far").sum(axis=0) / replicas
-    load, left = right_part_of(place, to_each(own, PAIR), merged, rank, deltas.shape[1])
+    load, left = right_part_of(to_each(own, PAIR), merged, rank, deltas.shape[1])
     nodes = lax.axis_size(NODES)
     width = load.shape[2] - rank
-    seen = lax.all_to_all(load, NODES, 0, 0, tiled=True)
-    lines = seen[:, :, width:].reshape(lax.axis_size("near"), -1, *seen.shape[1:2], rank).sum(axis=1)
-    far = to_each(jnp.concatenate([seen[:, :, :width].sum(axis=0), *lines], axis=1), "far")
-    part = far[:, :, :width].sum(axis=0) / replicas
-    right = to_each(part, NODES).reshape(nodes, -1, width)
-    gram = jnp.moveaxis(far[:, :, width:].reshape(*far.shape[:2], -1, rank), 2, 1).reshape(rank, rank)
-    flipped = factor_of(0.5 * (gram + gram.T), left)
-    right, flipped = lax.optimization_barrier((right, flipped))
+    total = lax.all_to_all(load, NODES, 0, 0, tiled=True).sum(axis=0)
+    part, gram = lax.optimization_barrier((total[:, :width], total[:, width:] / lax.axis_size("near")))
+    part = to_each(part, "far").sum(axis=0) / replicas
+    right = to_each(jnp.concatenate([part, gram], axis=1), NODES).reshape(nodes, *total.shape)
+    flipped = factor_of(right, left)
     other = lax.ppermute(right, "core", SWAP)
     ready, flat = near_half_of(place, flipped, right, deltas, errors)
     return outputs_of(place, flipped, flat, other, ready, deltas, errors, momentum)

time: 103 us -> 103 us (level)
  blocking collectives: 75.6 us -> 87.4 us
  waiting for transfers between devices: 5.53 us -> 0.01 us
  starting transfers between devices: 11 us -> 7.41 us
  Pallas kernels: 8.12 us -> 7.02 us
    all_to_all x3 -> x4, blocking collectives: 48.6 us -> 60.4 us  [to_each(): lax.all_to_all(jnp.broadcast_to(shard[None], (count, *shard.shape)), axes...]
    all_to_all x1 -> x0, waiting for transfers between devices: 4.63 us -> none  [to_each(): lax.all_to_all(jnp.broadcast_to(shard[None], (count, *shard.shape)), axes...]
    all_to_all x1 -> x0, starting transfers between devices: 4.01 us -> none  [to_each(): lax.all_to_all(jnp.broadcast_to(shard[None], (count, *shard.shape)), axes...]
    pallas_call x1, Pallas kernels: 3.3 us -> 2.21 us  [factor_of(): pl.pallas_call(factor_kernel, out_shape=pltpu.VMEM((rows, 4 * rank), jnp....]
  transfers between devices with their start and end apart: 2 -> 1, of which waited for: 2 -> 0; matrix products, arithmetic and copies ran while one was open for 0% -> 0% of each run, Pallas kernels for 4% -> 2%
where the time goes in v8:
time: 103 us
  blocking collectives  87.4 us (85%)
  starting transfers between devices  7.41 us (7%)
  Pallas kernels  7.02 us (7%)
    all_to_all x4, blocking collectives, to_each(): lax.all_to_all(jnp.broadcast_to(shard[None], (count, *shard.shape)), axes...  60.4 us
    all_to_all x1, blocking collectives, body(): total = lax.all_to_all(load, NODES, 0, 0, tiled=True).sum(axis=0)  15.5 us
    all_to_all x1, blocking collectives, body(): merged = lax.all_to_all(load, 'core', 0, 0, tiled=True)  11.5 us
    ppermute x1, starting transfers between devices, body(): other = lax.ppermute(right, 'core', SWAP)  7.41 us
    pallas_call x1, Pallas kernels, left_part_of(): pl.pallas_call(left_kernel, out_shape=(held((2, size, 128)), pltpu.VMEM(d...  2.54 us
    pallas_call x1, Pallas kernels, factor_of(): pl.pallas_call(factor_kernel, out_shape=pltpu.VMEM((rows, 4 * rank), jnp....  2.21 us
  transfers between devices with their start and end apart: 1, of which 0 were waited for; matrix products, arithmetic and copies ran while one was open for 0% of the time, Pallas kernels for 2%

profile of v8, /device:TPU:1, one launch (start us, length us, event | category | flops | bytes accessed | tf_op | source)
XLA Modules:
  0.0 102.8 jit_solution(13926291593638350499)
XLA Ops:
  0.6 2.5 %left_part.1 = (f32[2,1640,128]{2,1,0:T(8,128)S(1)}, bf16[1,160,2560]{2,1,0:T(8,128)(2,1)S(1)}, bf16[1,160,2560]{2,1,0:T(8,128)(2,1)S(1)}) custom-call(bf16[1,160,2560]{2,1,0:T(8,128)(2,1)} %deltas.1, bf16[1,160,2560]{2,1,0:T(8,128)(2,1)} %errors.1, f32[64,2560]{1,0:T(8,128)} %bitcast.2), custom_call_target="tpu_custom_call" | custom-call | tf_op jit(solution)/shard_map/left_part/pallas_call | solution.py:103
  3.2 11.5 %all_to_all.30.merged = f32[2,1640,128]{2,1,0:T(8,128)S(1)} all-to-all(f32[2,1640,128]{2,1,0:T(8,128)S(1)} %get-tuple-element.16), channel_id=1, replica_groups=mesh['far'=8,'near'=2,'core'=2,'mdl'=16] {'core'}, dimensions={0} | all-to-all | bytes 3358720 | tf_op jit(solution)/shard_map/all_to_all | solution.py:328
  14.7 24.1 %all_to_all.31 = f32[8,40,128]{2,1,0:T(8,128)S(1)} all-to-all(f32[8,40,128]{2,1,0:T(8,128)S(1)} %broadcast_in_dim.11), channel_id=1, replica_groups=mesh['far'=8,'near'=2,'core'=2,'mdl'=16] {'far'}, dimensions={0} | all-to-all | bytes 327680 | tf_op jit(solution)/shard_map/all_to_all | solution.py:317
  38.9 9.1 %all_to_all.32.halves = f32[4,40,128]{2,1,0:T(8,128)S(1)} all-to-all(f32[4,40,128]{2,1,0:T(8,128)S(1)} %broadcast_in_dim.12), channel_id=1, replica_groups=mesh['far'=8,'near'=2,'core'=2,'mdl'=16] {'near','core'}, dimensions={0} | all-to-all | bytes 163840 | tf_op jit(solution)/shard_map/all_to_all | solution.py:317
  48.0 0.7 right_part.1
  48.7 15.5 %all_to_all.33 = f32[32,4,704]{2,1,0:T(4,128)S(1)} all-to-all(f32[32,4,704]{2,1,0:T(4,128)S(1)} %get-tuple-element.17), channel_id=1, replica_groups=mesh['far'=8,'near'=2,'core'=2,'mdl'=16] {'near','mdl'}, dimensions={0} | all-to-all | bytes 720896 | tf_op jit(solution)/shard_map/all_to_all | solution.py:334
  64.2 0.1 reduce_sum.38
  64.3 15.1 %all_to_all.34 = f32[8,4,640]{2,1,0:T(4,128)S(1)} all-to-all(f32[8,4,640]{2,1,0:T(4,128)S(1)} %broadcast_in_dim.13), channel_id=1, replica_groups=mesh['far'=8,'near'=2,'core'=2,'mdl'=16] {'far'}, dimensions={0} | all-to-all | bytes 163840 | tf_op jit(solution)/shard_map/all_to_all | solution.py:317
  79.4 0.1 broadcast_in_dim.14
  79.5 0.0 copy-start
  79.5 12.1 %all_to_all.35.right = f32[32,4,704]{2,1,0:T(4,128)S(1)} all-to-all(f32[32,4,704]{2,1,0:T(4,128)S(1)} %broadcast_in_dim.14), channel_id=1, replica_groups=mesh['far'=8,'near'=2,'core'=2,'mdl'=16] {'near','mdl'}, dimensions={0} | all-to-all | bytes 720896 | tf_op jit(solution)/shard_map/all_to_all | solution.py:317
  91.6 7.4 %collective-permute-start = (f32[32,4,704]{2,1,0:T(4,128)S(1)}, f32[32,4,704]{2,1,0:T(4,128)S(1)}, u32[]{:S(2)}, u32[]{:S(2)}) collective-permute-start(f32[32,4,704]{2,1,0:T(4,128)S(1)} %all_to_all.35.right), channel_id=1, source_target_pairs={{0,16},{16,0},{1,17},{17,1},{2,18},{18,2},{3,19},{19,3},{4,20},{20... | collective-permute-start | bytes 1081352 | tf_op jit(solution)/shard_map/ppermute | solution.py:339
  99.0 2.2 %factor.1.flipped = bf16[160,256]{1,0:T(8,128)(2,1)S(1)} custom-call(f32[32,4,704]{2,1,0:T(4,128)S(1)} %all_to_all.35.right, f32[64,160]{1,0:T(8,128)S(1)} %get-tuple-element.20.left), custom_call_target="tpu_custom_call" | custom-call | flops 40000000 | bytes 200000 | tf_op jit(solution)/shard_map/factor/pallas_call | solution.py:200
  101.2 0.3 near_half.1
  101.6 0.0 collective-permute-done.other
  101.6 0.0 copy-done
  101.6 1.2 %outputs.1 = (bf16[1,160,2560]{2,1,0:T(8,128)(2,1)}, f32[160,80]{1,0:T(8,128)}, f32[160,80]{1,0:T(8,128)}) custom-call(s32[1]{0:T(128)} %bitcast.1.place, bf16[160,256]{1,0:T(8,128)(2,1)S(1)} %factor.1.flipped, f32[64,1280]{1,0:T(8,128)S(1)} %get-tuple-element.23.right, f32[32,4,704]{2,1,0:T(4,128)S(1)} %collective-permute-done.other, ...), custom_call_target="tpu_custom_call" | custom-call | tf_op jit(solution)/shard_map/outputs/pallas_call | solution.py:294
  (11 shorter events, 0.1 us)
Async XLA Ops:
  79.5 22.1 %copy-start = (f32[160,80]{1,0:T(8,128)S(1)}, f32[160,80]{1,0:T(8,128)}, u32[]{:S(2)}) copy-start(f32[160,80]{1,0:T(8,128)} %momentum.1) | copy-start | bytes 153604
  91.6 10.0 %collective-permute-start = (f32[32,4,704]{2,1,0:T(4,128)S(1)}, f32[32,4,704]{2,1,0:T(4,128)S(1)}, u32[]{:S(2)}, u32[]{:S(2)}) collective-permute-start(f32[32,4,704]{2,1,0:T(4,128)S(1)} %all_to_all.35.right), channel_id=1, source_target_pairs={{0,16},{16,0},{1,17},{17,1},{2,18},{18,2},{3,19},{19,3},{4,20},{20... | collective-permute-start | bytes 1081352 | tf_op jit(solution)/shard_map/ppermute | solution.py:339

commit v9 on v7

--- a/solution.py
+++ b/solution.py
@@ -11,7 +11,7 @@
 NODES = ("near", "mdl")
 SWAP = [(0, 1), (1, 0)]
 CHUNKS = 4
-BLOCK = 4
+BLOCK = 16
 
 
 highest = lax.Precision.HIGHEST
@@ -52,20 +52,20 @@
     return sum(stack[i * rows : (i + 1) * rows] for i in reversed(range(count)))
 
 
-def packed(rows):
-    lanes = rows.shape[1] - 128
+def pack(rows, out):
+    share = out.shape[0]
+    count = rows.shape[0] // share
+    parts = [rows[i * share : (i + 1) * share] for i in range(count)]
+    for i in range(count):
+        out[:, i * 128 : (i + 1) * 128] = parts[i][:, :128]
+    out[:, count * 128 :] = jnp.concatenate([part[:, 128:] for part in parts], axis=1)
+
+
+def unpack(tiles, lanes):
     count = 128 // lanes
-    share = rows.shape[0] // count
-    tails = [rows[i * share : (i + 1) * share, 128:] for i in range(count)]
-    return rows[:, :128], jnp.concatenate(tails, axis=1)
-
-
-def unpacked(tiles, lanes):
-    count = 128 // lanes
-    share = tiles.shape[0] // (count + 1)
-    tails = tiles[count * share :]
-    tails = [tails[:, i * lanes : (i + 1) * lanes] for i in range(count)]
-    return jnp.concatenate([tiles[: count * share], jnp.concatenate(tails, axis=0)], axis=1)
+    heads = [tiles[:, i * 128 : (i + 1) * 128] for i in range(count)]
+    tails = [tiles[:, count * 128 + i * lanes : count * 128 + (i + 1) * lanes] for i in range(count)]
+    return jnp.concatenate([jnp.concatenate(heads, axis=0), jnp.concatenate(tails, axis=0)], axis=1)
 
 
 def left_kernel(deltas, errors, starts, out, d_buf, e_buf, s_buf, sems):
@@ -82,28 +82,20 @@
     total = dot(stack, d_buf[0], ((1,), (1,)))
     copies[2].wait()
     total = folded(total + dot(stack, e_buf[0], ((1,), (1,))), 3)
-    rank, rows = total.shape
-    half = d_buf.shape[2] // 2
-    for p in range(2):
-        head, tail = packed(total[p * (rank // 2) : (p + 1) * (rank // 2)])
-        out[p, : rank // 2] = head
-        at = rank // 2 + tail.shape[0]
-        out[p, rank // 2 : at] = tail
-        for j in range(half // 128):
-            cut = slice(p * half + j * 128, p * half + (j + 1) * 128)
-            out[p, at + j * rows : at + (j + 1) * rows] = d_buf[0, :, cut].astype(jnp.float32) + e_buf[
-                0, :, cut
-            ].astype(jnp.float32)
+    share = total.shape[0] // out.shape[0]
+    for q in range(out.shape[0]):
+        pack(total[q * share : (q + 1) * share], out.at[q])
 
 
 def left_part_of(deltas, errors, starts):
     rows, columns = deltas.shape[1:]
     rank = starts.shape[0]
-    size = rank // 2 * rows // 128 + columns // 2 // 128 * rows
+    pairs = lax.axis_size(PAIR)
+    share = rank // pairs * (rows - 128) // 128
     return pl.pallas_call(
         left_kernel,
         out_shape=(
-            held((2, size, 128)),
+            held((pairs, share, rank // pairs * rows // share)),
             pltpu.VMEM(deltas.shape, jnp.bfloat16),
             pltpu.VMEM(errors.shape, jnp.bfloat16),
         ),
@@ -123,21 +115,39 @@
     )
 
 
-def right_kernel(place, halves, merged, out, left):
+def half_kernel(place, deltas, errors, out):
+    width = out.shape[1]
+    cut = pl.ds(pl.multiple_of((1 - place[0] % 2) * width, 128), width)
+    out[...] = deltas[0, :, cut].astype(jnp.float32) + errors[0, :, cut].astype(jnp.float32)
+
+
+def partner_half_of(place, deltas, errors):
+    rows, columns = deltas.shape[1:]
+    return pl.pallas_call(
+        half_kernel,
+        out_shape=held((rows, columns // 2)),
+        in_specs=[SMEM, VMEM, VMEM],
+        out_specs=VMEM,
+        compiler_params=SMALL,
+        cost_estimate=pl.CostEstimate(flops=40_000_000, transcendentals=0, bytes_accessed=2_000_000),
+        name="partner_half",
+    )(place, near_core(deltas), near_core(errors))
+
+
+def right_kernel(place, quarters, partner, deltas, errors, out, left):
     rank, rows = left.shape
     share = out.shape[1]
     groups = rank // share
     width = out.shape[2] - rank
-    tiles = width // 128
-    skip = halves.shape[1]
-    whole = jnp.concatenate([unpacked(halves[c] + halves[2 + c], rows - 128) for c in range(2)], axis=0)
+    whole = jnp.concatenate([unpack(quarters[q], rows - 128) for q in range(quarters.shape[0])], axis=0)
     left[...] = whole
     stack = jnp.concatenate(pieces_of(whole, 3), axis=0)
+    base = place[0] % 2 * partner.shape[1]
     for j in range(out.shape[0] // groups):
-        spans = [slice(skip + (j * tiles + t) * rows, skip + (j * tiles + t + 1) * rows) for t in range(tiles)]
-        both = jnp.concatenate([merged[0, span] + merged[1, span] for span in spans], axis=1)
+        own = pl.ds(pl.multiple_of(base + j * width, 128), width)
+        merged = deltas[0, :, own].astype(jnp.float32) + errors[0, :, own].astype(jnp.float32)
         part = None
-        for piece in reversed(pieces_of(both, 3)):
+        for piece in reversed(pieces_of(merged + partner[:, j * width : (j + 1) * width], 3)):
             term = dot(stack, piece, ((1,), (0,)))
             part = term if part is None else part + term
         part = folded(part, 3)
@@ -148,17 +158,17 @@
         out[p, :, width:] = lines
 
 
-def right_part_of(place, halves, merged, rank, rows):
-    width = (merged.shape[1] - halves.shape[1]) * 128 // rows // 2
+def right_part_of(place, quarters, partner, deltas, errors, rank):
+    rows, width = partner.shape[0], partner.shape[1] // 2
     share = rank * 2 // lax.axis_size(NODES)
     return pl.pallas_call(
         right_kernel,
         out_shape=(held((rank * 2 // share, share, width + rank)), held((rank, rows))),
-        in_specs=[SMEM, VMEM, VMEM],
+        in_specs=[SMEM, VMEM, VMEM, VMEM, VMEM],
         out_specs=(VMEM, VMEM),
         compiler_params=SMALL,
         name="right_part",
-    )(place, near_core(halves), near_core(merged))
+    )(place, near_core(quarters), near_core(partner), near_core(deltas), near_core(errors))
 
 
 def lower_inverse_of(gram):
@@ -321,10 +331,15 @@
     place = lax.axis_index(REP)[None]
     load, deltas, errors = left_part_of(deltas, errors, starts.T)
     load, place = lax.optimization_barrier((load, place))
-    merged = lax.all_to_all(load, "core", 0, 0, tiled=True)
-    size = rank // 2 * deltas.shape[1] // 128
-    own = to_each(merged[:, :size].sum(axis=0), "far").sum(axis=0) / replicas
-    load, left = right_part_of(place, to_each(own, PAIR), merged, rank, deltas.shape[1])
+    own = lax.all_to_all(load, PAIR, 0, 0, tiled=True).sum(axis=0)
+    own, spot = lax.optimization_barrier((own, place))
+    other = partner_half_of(spot, deltas, errors)
+    partner = lax.ppermute(other, "core", SWAP)
+    own = to_each(own, "far")
+    own = own.sum(axis=0) / replicas
+    own, partner = lax.optimization_barrier((own, partner))
+    quarters = to_each(own, PAIR).reshape(load.shape)
+    load, left = right_part_of(place, quarters, partner, deltas, errors, rank)
     nodes = lax.axis_size(NODES)
     width = load.shape[2] - rank
     seen = lax.all_to_all(load, NODES, 0, 0, tiled=True)

time: 103 us -> 102 us (level)
  blocking collectives: 75.6 us -> 72.3 us
  starting transfers between devices: 11 us -> 13.3 us
  waiting for transfers between devices: 5.53 us -> 6.74 us
  Pallas kernels: 8.12 us -> 6.98 us
    all_to_all x3, blocking collectives: 48.6 us -> 44.5 us  [to_each(): lax.all_to_all(jnp.broadcast_to(shard[None], (count, *shard.shape)), axes...]
    ppermute x0 -> x1, starting transfers between devices: none -> 2.71 us  [body(): partner = lax.ppermute(other, 'core', SWAP)]
    all_to_all x1, waiting for transfers between devices: 4.63 us -> 5.84 us  [to_each(): lax.all_to_all(jnp.broadcast_to(shard[None], (count, *shard.shape)), axes...]
    pallas_call x1, Pallas kernels: 3.3 us -> 2.19 us  [factor_of(): pl.pallas_call(factor_kernel, out_shape=pltpu.VMEM((left.shape[1], 4 * gr...]
    pallas_call x1 -> x2, Pallas kernels: 2.54 us -> 2.47 us  [the longest x1 2.37 us: left_part_of(): pl.pallas_call(left_kernel, out_shape=(held((pairs, share, rank // pairs...]
  transfers between devices with their start and end apart: 2 -> 3, of which waited for: 2 -> 2; matrix products, arithmetic and copies ran while one was open for 0% -> 0% of each run, Pallas kernels for 4% -> 2%
where the time goes in v9:
time: 102 us; the launch traced here: 101 us
  blocking collectives  72.3 us (71%)
  starting transfers between devices  13.3 us (13%)
  Pallas kernels  6.98 us (7%)
  waiting for transfers between devices  6.74 us (7%)
    all_to_all x3, blocking collectives, to_each(): lax.all_to_all(jnp.broadcast_to(shard[None], (count, *shard.shape)), axes...  44.5 us
    all_to_all x1, blocking collectives, body(): seen = lax.all_to_all(load, NODES, 0, 0, tiled=True)  15.5 us
    all_to_all x1, blocking collectives, body(): own = lax.all_to_all(load, PAIR, 0, 0, tiled=True).sum(axis=0)  12.4 us
    ppermute x1, starting transfers between devices, body(): other = lax.ppermute(right, 'core', SWAP)  6.71 us
    all_to_all x1, waiting for transfers between devices, to_each(): lax.all_to_all(jnp.broadcast_to(shard[None], (count, *shard.shape)), axes...  5.84 us
    all_to_all x1, starting transfers between devices, to_each(): lax.all_to_all(jnp.broadcast_to(shard[None], (count, *shard.shape)), axes...  3.88 us
    ppermute x1, starting transfers between devices, body(): partner = lax.ppermute(other, 'core', SWAP)  2.71 us
    pallas_call x1, Pallas kernels, left_part_of(): pl.pallas_call(left_kernel, out_shape=(held((pairs, share, rank // pairs...  2.37 us
  transfers between devices with their start and end apart: 3, of which 2 were waited for; matrix products, arithmetic and copies ran while one was open for 0% of the time, Pallas kernels for 2%

profile of v9, /device:TPU:1, one launch (start us, length us, event | category | flops | bytes accessed | tf_op | source)
XLA Modules:
  0.0 101.4 jit_solution(2032867769587596228)
XLA Ops:
  0.6 2.4 %left_part.1 = (f32[4,4,640]{2,1,0:T(4,128)S(1)}, bf16[1,160,2560]{2,1,0:T(8,128)(2,1)S(1)}, bf16[1,160,2560]{2,1,0:T(8,128)(2,1)S(1)}) custom-call(bf16[1,160,2560]{2,1,0:T(8,128)(2,1)} %deltas.1, bf16[1,160,2560]{2,1,0:T(8,128)(2,1)} %errors.1, f32[64,2560]{1,0:T(8,128)} %bitcast.16), custom_call_target="tpu_custom_call" | custom-call | tf_op jit(solution)/shard_map/left_part/pallas_call | solution.py:95
  3.0 12.4 %all_to_all.30 = f32[4,4,640]{2,1,0:T(4,128)S(1)} all-to-all(f32[4,4,640]{2,1,0:T(4,128)S(1)} %get-tuple-element.20), channel_id=1, replica_groups=mesh['far'=8,'near'=2,'core'=2,'mdl'=16] {'near','core'}, dimensions={0} | all-to-all | bytes 81920 | tf_op jit(solution)/shard_map/all_to_all | solution.py:334
  15.4 0.1 partner_half.1
  15.5 2.7 %collective-permute-start = (f32[160,1280]{1,0:T(8,128)S(1)}, f32[160,1280]{1,0:T(8,128)S(1)}, u32[]{:S(2)}, u32[]{:S(2)}) collective-permute-start(f32[160,1280]{1,0:T(8,128)S(1)} %partner_half.1), channel_id=1, source_target_pairs={{0,16},{16,0},{1,17},{17,1},{2,18},{18,2},{3,19},{19,3},{4,20},{20... | collective-permute-start | bytes 2457608 | tf_op jit(solution)/shard_map/ppermute | solution.py:337
  18.3 21.4 %all_to_all.31 = f32[8,4,640]{2,1,0:T(4,128)S(1)} all-to-all(f32[8,4,640]{2,1,0:T(4,128)S(1)} %broadcast_in_dim.11), channel_id=1, replica_groups=mesh['far'=8,'near'=2,'core'=2,'mdl'=16] {'far'}, dimensions={0} | all-to-all | bytes 163840 | tf_op jit(solution)/shard_map/all_to_all | solution.py:323
  39.7 0.0 collective-permute-done.partner
  39.7 7.5 %all_to_all.32.quarters = f32[4,4,640]{2,1,0:T(4,128)S(1)} all-to-all(f32[4,4,640]{2,1,0:T(4,128)S(1)} %broadcast_in_dim.12), channel_id=1, replica_groups=mesh['far'=8,'near'=2,'core'=2,'mdl'=16] {'near','core'}, dimensions={0} | all-to-all | bytes 81920 | tf_op jit(solution)/shard_map/all_to_all | solution.py:323
  47.2 0.8 right_part.1
  48.0 15.5 %all_to_all.33 = f32[32,4,704]{2,1,0:T(4,128)S(1)} all-to-all(f32[32,4,704]{2,1,0:T(4,128)S(1)} %get-tuple-element.27), channel_id=1, replica_groups=mesh['far'=8,'near'=2,'core'=2,'mdl'=16] {'near','mdl'}, dimensions={0} | all-to-all | bytes 720896 | tf_op jit(solution)/shard_map/all_to_all | solution.py:345
  63.5 0.1 slice_reduce_fusion
  63.6 0.1 pad_maximum_fusion
  63.7 15.6 %all_to_all.34 = f32[8,4,768]{2,1,0:T(4,128)S(1)} all-to-all(f32[8,4,768]{2,1,0:T(4,128)S(1)} %broadcast_in_dim.13), channel_id=1, replica_groups=mesh['far'=8,'near'=2,'core'=2,'mdl'=16] {'far'}, dimensions={0} | all-to-all | bytes 196608 | tf_op jit(solution)/shard_map/all_to_all | solution.py:323
  79.3 0.8 broadcast_in_dim.14
  80.1 3.9 %all-to-all-start.5 = ((f32[32,4,640]{2,1,0:T(4,128)}), f32[32,4,640]{2,1,0:T(4,128)S(1)}, u32[]{:S(2)}, u32[]{:S(2)}) async-start(f32[32,4,640]{2,1,0:T(4,128)} %broadcast_in_dim.14), calls=%async_computation.5 | async-start | bytes 655360 | tf_op jit(solution)/shard_map/all_to_all | solution.py:323
  84.0 0.1 reshape.22
  84.1 0.1 copy.19
  84.2 2.2 %factor.1.flipped = bf16[160,256]{1,0:T(8,128)(2,1)S(1)} custom-call(f32[64,64]{1,0:T(8,128)S(1)} %fusion.gram, f32[64,160]{1,0:T(8,128)S(1)} %get-tuple-element.28.left), custom_call_target="tpu_custom_call" | custom-call | flops 40000000 | bytes 200000 | tf_op jit(solution)/shard_map/factor/pallas_call | solution.py:209
  86.4 0.0 copy-start
  86.4 5.8 %all-to-all-done.5.right = f32[32,4,640]{2,1,0:T(4,128)S(1)} async-done(((f32[32,4,640]{2,1,0:T(4,128)}), f32[32,4,640]{2,1,0:T(4,128)S(1)}, u32[]{:S(2)}, u32[]{:S(2)}) %all-to-all-start.5) | async-done | bytes 327712 | tf_op jit(solution)/shard_map/all_to_all | solution.py:323
  92.2 6.7 %collective-permute-start.1 = (f32[32,4,640]{2,1,0:T(4,128)S(1)}, f32[32,4,640]{2,1,0:T(4,128)S(1)}, u32[]{:S(2)}, u32[]{:S(2)}) collective-permute-start(f32[32,4,640]{2,1,0:T(4,128)S(1)} %all-to-all-done.5.right), channel_id=1, source_target_pairs={{0,16},{16,0},{1,17},{17,1},{2,18},{18,2},{3,19},{19,3},{4,20},{20... | collective-permute-start | bytes 983048 | tf_op jit(solution)/shard_map/ppermute | solution.py:353
  98.9 0.3 near_half.1
  99.3 0.9 collective-permute-done.1.other
  100.2 0.0 copy-done
  100.2 1.2 %outputs.1 = (bf16[1,160,2560]{2,1,0:T(8,128)(2,1)}, f32[160,80]{1,0:T(8,128)}, f32[160,80]{1,0:T(8,128)}) custom-call(s32[1]{0:T(128)} %bitcast.1.place, bf16[160,256]{1,0:T(8,128)(2,1)S(1)} %factor.1.flipped, f32[64,1280]{1,0:T(8,128)S(1)} %get-tuple-element.31.right, f32[32,4,640]{2,1,0:T(4,128)S(1)} %collective-permute-done.1.other, ...), custom_call_target="tpu_custom_call" | custom-call | tf_op jit(solution)/shard_map/outputs/pallas_call | solution.py:300
  (14 shorter events, 0.2 us)
Async XLA Ops:
  15.5 24.2 %collective-permute-start = (f32[160,1280]{1,0:T(8,128)S(1)}, f32[160,1280]{1,0:T(8,128)S(1)}, u32[]{:S(2)}, u32[]{:S(2)}) collective-permute-start(f32[160,1280]{1,0:T(8,128)S(1)} %partner_half.1), channel_id=1, source_target_pairs={{0,16},{16,0},{1,17},{17,1},{2,18},{18,2},{3,19},{19,3},{4,20},{20... | collective-permute-start | bytes 2457608 | tf_op jit(solution)/shard_map/ppermute | solution.py:337
  80.1 12.2 %all-to-all-start.5 = ((f32[32,4,640]{2,1,0:T(4,128)}), f32[32,4,640]{2,1,0:T(4,128)S(1)}, u32[]{:S(2)}, u32[]{:S(2)}) async-start(f32[32,4,640]{2,1,0:T(4,128)} %broadcast_in_dim.14), calls=%async_computation.5 | async-start | bytes 655360 | tf_op jit(solution)/shard_map/all_to_all | solution.py:323
  86.4 13.8 %copy-start = (f32[160,80]{1,0:T(8,128)S(1)}, f32[160,80]{1,0:T(8,128)}, u32[]{:S(2)}) copy-start(f32[160,80]{1,0:T(8,128)} %momentum.1) | copy-start | bytes 153604
  92.2 8.0 %collective-permute-start.1 = (f32[32,4,640]{2,1,0:T(4,128)S(1)}, f32[32,4,640]{2,1,0:T(4,128)S(1)}, u32[]{:S(2)}, u32[]{:S(2)}) collective-permute-start(f32[32,4,640]{2,1,0:T(4,128)S(1)} %all-to-all-done.5.right), channel_id=1, source_target_pairs={{0,16},{16,0},{1,17},{17,1},{2,18},{18,2},{3,19},{19,3},{4,20},{20... | collective-permute-start | bytes 983048 | tf_op jit(solution)/shard_map/ppermute | solution.py:353

commit v10 on v9

--- a/solution.py
+++ b/solution.py
@@ -134,41 +134,62 @@
     )(place, near_core(deltas), near_core(errors))
 
 
-def right_kernel(place, quarters, partner, deltas, errors, out, left):
+def quarter_kernel(place, partner, deltas, errors, own, other):
+    width = own.shape[1]
+    near = place[0] // 2 % 2
+    base = place[0] % 2 * partner.shape[1]
+    for n, out in ((near, own), (1 - near, other)):
+        cut = pl.ds(pl.multiple_of(base + n * width, 128), width)
+        here = pl.ds(pl.multiple_of(n * width, 128), width)
+        out[...] = (
+            deltas[0, :, cut].astype(jnp.float32) + errors[0, :, cut].astype(jnp.float32) + partner[:, here]
+        )
+
+
+def quarters_of(place, partner, deltas, errors):
+    rows, columns = partner.shape
+    return pl.pallas_call(
+        quarter_kernel,
+        out_shape=(held((rows, columns // 2)), held((rows, columns // 2))),
+        in_specs=[SMEM, VMEM, VMEM, VMEM],
+        out_specs=(VMEM, VMEM),
+        compiler_params=SMALL,
+        name="merged_quarters",
+    )(place, near_core(partner), near_core(deltas), near_core(errors))
+
+
+def right_kernel(place, quarters, own, other, out, left):
     rank, rows = left.shape
     share = out.shape[1]
     groups = rank // share
-    width = out.shape[2] - rank
     whole = jnp.concatenate([unpack(quarters[q], rows - 128) for q in range(quarters.shape[0])], axis=0)
     left[...] = whole
     stack = jnp.concatenate(pieces_of(whole, 3), axis=0)
-    base = place[0] % 2 * partner.shape[1]
-    for j in range(out.shape[0] // groups):
-        own = pl.ds(pl.multiple_of(base + j * width, 128), width)
-        merged = deltas[0, :, own].astype(jnp.float32) + errors[0, :, own].astype(jnp.float32)
-        part = None
-        for piece in reversed(pieces_of(merged + partner[:, j * width : (j + 1) * width], 3)):
-            term = dot(stack, piece, ((1,), (0,)))
-            part = term if part is None else part + term
-        part = folded(part, 3)
-        for g in range(groups):
-            out[j * groups + g, :, :width] = part[g * share : (g + 1) * share]
-    lines = gram_lines(whole, place[0] // 2 * share, share)
+    width = own.shape[1]
+    part = None
+    for piece in reversed(pieces_of(own[...] + other[...], 3)):
+        term = dot(stack, piece, ((1,), (0,)))
+        part = term if part is None else part + term
+    part = folded(part, 3)
+    for g in range(groups):
+        out[g, :, :width] = part[g * share : (g + 1) * share]
+    lines = gram_lines(whole, place[0] // 4 * 2 * share, 2 * share)
     for p in range(out.shape[0]):
-        out[p, :, width:] = lines
-
-
-def right_part_of(place, quarters, partner, deltas, errors, rank):
-    rows, width = partner.shape[0], partner.shape[1] // 2
-    share = rank * 2 // lax.axis_size(NODES)
+        out[p, :, width : width + rank] = lines[:share]
+        out[p, :, width + rank :] = lines[share:]
+
+
+def right_part_of(place, quarters, own, other, rank):
+    rows, width = own.shape
+    groups = lax.axis_size("mdl")
     return pl.pallas_call(
         right_kernel,
-        out_shape=(held((rank * 2 // share, share, width + rank)), held((rank, rows))),
-        in_specs=[SMEM, VMEM, VMEM, VMEM, VMEM],
+        out_shape=(held((groups, rank // groups, width + 2 * rank)), held((rank, rows))),
+        in_specs=[SMEM, VMEM, VMEM, VMEM],
         out_specs=(VMEM, VMEM),
         compiler_params=SMALL,
         name="right_part",
-    )(place, near_core(quarters), near_core(partner), near_core(deltas), near_core(errors))
+    )(place, near_core(quarters), near_core(own), near_core(other))
 
 
 def lower_inverse_of(gram):
@@ -337,14 +358,14 @@
     partner = lax.ppermute(other, "core", SWAP)
     own = to_each(own, "far")
     own = own.sum(axis=0) / replicas
-    own, partner = lax.optimization_barrier((own, partner))
+    mine, other = quarters_of(place, partner, deltas, errors)
+    other = lax.ppermute(other, "near", SWAP)
     quarters = to_each(own, PAIR).reshape(load.shape)
-    load, left = right_part_of(place, quarters, partner, deltas, errors, rank)
+    load, left = right_part_of(place, quarters, mine, other, rank)
     nodes = lax.axis_size(NODES)
-    width = load.shape[2] - rank
-    seen = lax.all_to_all(load, NODES, 0, 0, tiled=True)
-    lines = seen[:, :, width:].reshape(lax.axis_size("near"), -1, *seen.shape[1:2], rank).sum(axis=1)
-    far = to_each(jnp.concatenate([seen[:, :, :width].sum(axis=0), *lines], axis=1), "far")
+    width = load.shape[2] - 2 * rank
+    total = lax.all_to_all(load, "mdl", 0, 0, tiled=True).sum(axis=0)
+    far = to_each(total, "far")
     part = far[:, :, :width].sum(axis=0) / replicas
     right = to_each(part, NODES).reshape(nodes, -1, width)
     gram = jnp.moveaxis(far[:, :, width:].reshape(*far.shape[:2], -1, rank), 2, 1).reshape(rank, rank)

time: 102 us -> 103 us (level)
  blocking collectives: 72.3 us -> 51.5 us
  starting transfers between devices: 13.3 us -> 24.6 us
  waiting for transfers between devices: 6.74 us -> 16.7 us
    all_to_all x3 -> x2, blocking collectives: 44.5 us -> 25.3 us  [to_each(): lax.all_to_all(jnp.broadcast_to(shard[None], (count, *shard.shape)), axes...]
    all_to_all x1 -> x2, waiting for transfers between devices: 5.84 us -> 15.9 us  [to_each(): lax.all_to_all(jnp.broadcast_to(shard[None], (count, *shard.shape)), axes...]
    all_to_all x1 -> x2, starting transfers between devices: 3.88 us -> 13.4 us  [to_each(): lax.all_to_all(jnp.broadcast_to(shard[None], (count, *shard.shape)), axes...]
    ppermute x0 -> x1, starting transfers between devices: none -> 1.92 us  [body(): other = lax.ppermute(other, 'near', SWAP)]
    all_to_all x1, blocking collectives: 15.5 us -> 13.8 us  [body(): total = lax.all_to_all(load, 'mdl', 0, 0, tiled=True).sum(axis=0)]
  transfers between devices with their start and end apart: 3 -> 5, of which waited for: 2 -> 3; matrix products, arithmetic and copies ran while one was open for 0% -> 1% of each run, Pallas kernels for 2% -> 3%
where the time goes in v10:
time: 103 us; the launch traced here: 102 us
  blocking collectives  51.5 us (50%)
  starting transfers between devices  24.6 us (24%)
  waiting for transfers between devices  16.7 us (16%)
  Pallas kernels  6.93 us (7%)
  local copies, waits for them, and re-layouts  1.63 us (2%)
    all_to_all x2, blocking collectives, to_each(): lax.all_to_all(jnp.broadcast_to(shard[None], (count, *shard.shape)), axes...  25.3 us
    all_to_all x2, waiting for transfers between devices, to_each(): lax.all_to_all(jnp.broadcast_to(shard[None], (count, *shard.shape)), axes...  15.9 us
    all_to_all x1, blocking collectives, body(): total = lax.all_to_all(load, 'mdl', 0, 0, tiled=True).sum(axis=0)  13.8 us
    all_to_all x2, starting transfers between devices, to_each(): lax.all_to_all(jnp.broadcast_to(shard[None], (count, *shard.shape)), axes...  13.4 us
    all_to_all x1, blocking collectives, body(): own = lax.all_to_all(load, PAIR, 0, 0, tiled=True).sum(axis=0)  12.4 us
    ppermute x1, starting transfers between devices, body(): other = lax.ppermute(right, 'core', SWAP)  6.64 us
    ppermute x1, starting transfers between devices, body(): partner = lax.ppermute(other, 'core', SWAP)  2.71 us
    pallas_call x1, Pallas kernels, left_part_of(): pl.pallas_call(left_kernel, out_shape=(held((pairs, share, rank // pairs...  2.37 us
  transfers between devices with their start and end apart: 5, of which 3 were waited for; matrix products, arithmetic and copies ran while one was open for 1% of the time, Pallas kernels for 3%

profile of v10, /device:TPU:1, one launch (start us, length us, event | category | flops | bytes accessed | tf_op | source)
XLA Modules:
  0.0 102.4 jit_solution(1798613687868000610)
XLA Ops:
  0.6 2.4 %left_part.1 = (f32[4,4,640]{2,1,0:T(4,128)S(1)}, bf16[1,160,2560]{2,1,0:T(8,128)(2,1)S(1)}, bf16[1,160,2560]{2,1,0:T(8,128)(2,1)S(1)}) custom-call(bf16[1,160,2560]{2,1,0:T(8,128)(2,1)} %deltas.1, bf16[1,160,2560]{2,1,0:T(8,128)(2,1)} %errors.1, f32[64,2560]{1,0:T(8,128)} %bitcast.10), custom_call_target="tpu_custom_call" | custom-call | tf_op jit(solution)/shard_map/left_part/pallas_call | solution.py:95
  3.0 12.4 %all_to_all.30 = f32[4,4,640]{2,1,0:T(4,128)S(1)} all-to-all(f32[4,4,640]{2,1,0:T(4,128)S(1)} %get-tuple-element.20), channel_id=1, replica_groups=mesh['far'=8,'near'=2,'core'=2,'mdl'=16] {'near','core'}, dimensions={0} | all-to-all | bytes 81920 | tf_op jit(solution)/shard_map/all_to_all | solution.py:355
  15.4 0.1 partner_half.1
  15.5 2.7 %collective-permute-start = (f32[160,1280]{1,0:T(8,128)S(1)}, f32[160,1280]{1,0:T(8,128)S(1)}, u32[]{:S(2)}, u32[]{:S(2)}) collective-permute-start(f32[160,1280]{1,0:T(8,128)S(1)} %partner_half.1), channel_id=1, source_target_pairs={{0,16},{16,0},{1,17},{17,1},{2,18},{18,2},{3,19},{19,3},{4,20},{20... | collective-permute-start | bytes 2457608 | tf_op jit(solution)/shard_map/ppermute | solution.py:358
  18.2 0.6 broadcast_in_dim.11
  18.9 9.5 %all-to-all-start.1 = ((f32[8,4,640]{2,1,0:T(4,128)}), f32[8,4,640]{2,1,0:T(4,128)S(1)}, u32[]{:S(2)}, u32[]{:S(2)}) async-start(f32[8,4,640]{2,1,0:T(4,128)} %broadcast_in_dim.11), calls=%async_computation.1 | async-start | bytes 163840 | tf_op jit(solution)/shard_map/all_to_all | solution.py:344
  28.4 0.0 collective-permute-done.partner
  28.4 0.2 merged_quarters.1
  28.5 1.9 %collective-permute-start.1 = (f32[160,640]{1,0:T(8,128)S(1)}, f32[160,640]{1,0:T(8,128)S(1)}, u32[]{:S(2)}, u32[]{:S(2)}) collective-permute-start(f32[160,640]{1,0:T(8,128)S(1)} %get-tuple-element.26), channel_id=1, source_target_pairs={{0,32},{32,0},{1,33},{33,1},{2,34},{34,2},{3,35},{35,3},{4,36},{36... | collective-permute-start | bytes 1228808 | tf_op jit(solution)/shard_map/ppermute | solution.py:362
  30.4 10.0 %all-to-all-done.1 = f32[8,4,640]{2,1,0:T(4,128)S(1)} async-done(((f32[8,4,640]{2,1,0:T(4,128)}), f32[8,4,640]{2,1,0:T(4,128)S(1)}, u32[]{:S(2)}, u32[]{:S(2)}) %all-to-all-start.1) | async-done | bytes 81952 | tf_op jit(solution)/shard_map/all_to_all | solution.py:344
  40.5 7.6 %all_to_all.31.quarters = f32[4,4,640]{2,1,0:T(4,128)S(1)} all-to-all(f32[4,4,640]{2,1,0:T(4,128)S(1)} %broadcast_in_dim.12), channel_id=1, replica_groups=mesh['far'=8,'near'=2,'core'=2,'mdl'=16] {'near','core'}, dimensions={0} | all-to-all | bytes 81920 | tf_op jit(solution)/shard_map/all_to_all | solution.py:344
  48.2 0.0 collective-permute-done.1.other
  48.2 0.6 right_part.1
  48.7 13.8 %all_to_all.32 = f32[16,4,768]{2,1,0:T(4,128)S(1)} all-to-all(f32[16,4,768]{2,1,0:T(4,128)S(1)} %get-tuple-element.27), channel_id=1, replica_groups=mesh['far'=8,'near'=2,'core'=2,'mdl'=16] {'mdl'}, dimensions={0} | all-to-all | bytes 393216 | tf_op jit(solution)/shard_map/all_to_all | solution.py:367
  62.6 17.7 %all_to_all.33 = f32[8,4,768]{2,1,0:T(4,128)S(1)} all-to-all(f32[8,4,768]{2,1,0:T(4,128)S(1)} %broadcast_in_dim.13), channel_id=1, replica_groups=mesh['far'=8,'near'=2,'core'=2,'mdl'=16] {'far'}, dimensions={0} | all-to-all | bytes 196608 | tf_op jit(solution)/shard_map/all_to_all | solution.py:344
  80.3 0.8 broadcast_in_dim.14
  81.1 3.9 %all-to-all-start.5 = ((f32[32,4,640]{2,1,0:T(4,128)}), f32[32,4,640]{2,1,0:T(4,128)S(1)}, u32[]{:S(2)}, u32[]{:S(2)}) async-start(f32[32,4,640]{2,1,0:T(4,128)} %broadcast_in_dim.14), calls=%async_computation.5 | async-start | bytes 655360 | tf_op jit(solution)/shard_map/all_to_all | solution.py:344
  85.0 0.1 reshape.20
  85.1 0.1 copy.19
  85.2 2.2 %factor.1.flipped = bf16[160,256]{1,0:T(8,128)(2,1)S(1)} custom-call(f32[64,64]{1,0:T(8,128)S(1)} %fusion.gram, f32[64,160]{1,0:T(8,128)S(1)} %get-tuple-element.28.left), custom_call_target="tpu_custom_call" | custom-call | flops 40000000 | bytes 200000 | tf_op jit(solution)/shard_map/factor/pallas_call | solution.py:230
  87.4 0.0 copy-start
  87.4 5.8 %all-to-all-done.5.right = f32[32,4,640]{2,1,0:T(4,128)S(1)} async-done(((f32[32,4,640]{2,1,0:T(4,128)}), f32[32,4,640]{2,1,0:T(4,128)S(1)}, u32[]{:S(2)}, u32[]{:S(2)}) %all-to-all-start.5) | async-done | bytes 327712 | tf_op jit(solution)/shard_map/all_to_all | solution.py:344
  93.3 6.6 %collective-permute-start.2 = (f32[32,4,640]{2,1,0:T(4,128)S(1)}, f32[32,4,640]{2,1,0:T(4,128)S(1)}, u32[]{:S(2)}, u32[]{:S(2)}) collective-permute-start(f32[32,4,640]{2,1,0:T(4,128)S(1)} %all-to-all-done.5.right), channel_id=1, source_target_pairs={{0,16},{16,0},{1,17},{17,1},{2,18},{18,2},{3,19},{19,3},{4,20},{20... | collective-permute-start | bytes 983048 | tf_op jit(solution)/shard_map/ppermute | solution.py:374
  99.9 0.3 near_half.1
  100.3 0.9 collective-permute-done.2.other
  101.2 0.0 copy-done
  101.2 1.2 %outputs.1 = (bf16[1,160,2560]{2,1,0:T(8,128)(2,1)}, f32[160,80]{1,0:T(8,128)}, f32[160,80]{1,0:T(8,128)}) custom-call(s32[1]{0:T(128)} %bitcast.1.place, bf16[160,256]{1,0:T(8,128)(2,1)S(1)} %factor.1.flipped, f32[64,1280]{1,0:T(8,128)S(1)} %get-tuple-element.31.right, f32[32,4,640]{2,1,0:T(4,128)S(1)} %collective-permute-done.2.other, ...), custom_call_target="tpu_custom_call" | custom-call | tf_op jit(solution)/shard_map/outputs/pallas_call | solution.py:321
  (12 shorter events, 0.2 us)
Async XLA Ops:
  15.5 12.8 %collective-permute-start = (f32[160,1280]{1,0:T(8,128)S(1)}, f32[160,1280]{1,0:T(8,128)S(1)}, u32[]{:S(2)}, u32[]{:S(2)}) collective-permute-start(f32[160,1280]{1,0:T(8,128)S(1)} %partner_half.1), channel_id=1, source_target_pairs={{0,16},{16,0},{1,17},{17,1},{2,18},{18,2},{3,19},{19,3},{4,20},{20... | collective-permute-start | bytes 2457608 | tf_op jit(solution)/shard_map/ppermute | solution.py:358
  18.9 21.6 %all-to-all-start.1 = ((f32[8,4,640]{2,1,0:T(4,128)}), f32[8,4,640]{2,1,0:T(4,128)S(1)}, u32[]{:S(2)}, u32[]{:S(2)}) async-start(f32[8,4,640]{2,1,0:T(4,128)} %broadcast_in_dim.11), calls=%async_computation.1 | async-start | bytes 163840 | tf_op jit(solution)/shard_map/all_to_all | solution.py:344
  28.5 19.7 %collective-permute-start.1 = (f32[160,640]{1,0:T(8,128)S(1)}, f32[160,640]{1,0:T(8,128)S(1)}, u32[]{:S(2)}, u32[]{:S(2)}) collective-permute-start(f32[160,640]{1,0:T(8,128)S(1)} %get-tuple-element.26), channel_id=1, source_target_pairs={{0,32},{32,0},{1,33},{33,1},{2,34},{34,2},{3,35},{35,3},{4,36},{36... | collective-permute-start | bytes 1228808 | tf_op jit(solution)/shard_map/ppermute | solution.py:362
  81.1 12.2 %all-to-all-start.5 = ((f32[32,4,640]{2,1,0:T(4,128)}), f32[32,4,640]{2,1,0:T(4,128)S(1)}, u32[]{:S(2)}, u32[]{:S(2)}) async-start(f32[32,4,640]{2,1,0:T(4,128)} %broadcast_in_dim.14), calls=%async_computation.5 | async-start | bytes 655360 | tf_op jit(solution)/shard_map/all_to_all | solution.py:344
  87.4 13.7 %copy-start = (f32[160,80]{1,0:T(8,128)S(1)}, f32[160,80]{1,0:T(8,128)}, u32[]{:S(2)}) copy-start(f32[160,80]{1,0:T(8,128)} %momentum.1) | copy-start | bytes 153604
  93.3 7.9 %collective-permute-start.2 = (f32[32,4,640]{2,1,0:T(4,128)S(1)}, f32[32,4,640]{2,1,0:T(4,128)S(1)}, u32[]{:S(2)}, u32[]{:S(2)}) collective-permute-start(f32[32,4,640]{2,1,0:T(4,128)S(1)} %all-to-all-done.5.right), channel_id=1, source_target_pairs={{0,16},{16,0},{1,17},{17,1},{2,18},{18,2},{3,19},{19,3},{4,20},{20... | collective-permute-start | bytes 983048 | tf_op jit(solution)/shard_map/ppermute | solution.py:374
